TPU v7x, 32 devices: a whole 2x2x4 slice. The times are simulated.
32 devices in a mesh: span: 2 (over y), height: 4 (over x, core), depth: 4 (over z).
Axes of the slice: x: 2, y: 2, z: 4, core: 2. Of those that a mesh axis runs over, the one named last changes fastest.
Arguments:
- load: float32 [8, 32, 64, 512], P(None, 'span', 'height', 'depth'), may hold values from -6 to 6
- phase: float32 [32, 64, 512], P('span', 'height', 'depth'), may hold values from 0.1 to 1
- void: int32 [4, 8, 64], P('span', 'height', 'depth'), may hold values from 0 to 1, as said below
- owner: int32 [4, 8, 64], P('span', 'height', 'depth'), may hold values from 0 to 1, as said below
- precond: bfloat16 [512, 512, 512], P(('span', 'height', 'depth')), may hold values from -1 to 2, as said below
Outputs:
- displacement: float32 [8, 32, 64, 512], P(None, 'span', 'height', 'depth')
- sensitivity: float32 [32, 64, 512], P('span', 'height', 'depth')
- phase_next: float32 [32, 64, 512], P('span', 'height', 'depth')
Inputs may be any that keep to these rules, and one draw needn't show every extreme that they name: `void`: each device's block of 16 x 16 x 128 cells holds at most 16 solid bricks; some device holds exactly 16. `owner`: among the solid bricks of one device at most 8 name any one value; on some device every value is named by exactly 8 solid bricks. Values of void bricks carry no meaning. `precond`: every block is symmetric with a positive diagonal that dominates each row.
All inputs are finite; a program needn't handle non-finite values.
Results may differ from a plain program's by a relative error of at most 0.0021.
Values may be sent and summed in bfloat16 or wider, within the bound.
No kernel may reach another device: no remote copies, remote signals or barrier semaphores. Data moves between devices by JAX's collectives and lax.ppermute only.
A program may use at most 128 MiB of HBM per device.

v0:
```python
import jax
import jax.numpy as jnp
from jax import lax
from jax.sharding import PartitionSpec as P

BE = 8
ITERS = 2
SWEEPS = 2


void_stiffness = 0.001
spring_rate = 0.05
time_step = 0.5
interface_weight = 0.5
epsilon_peak = 1e-06


def padded_2(block, sides, width):
    for axis, dim in sides:
        count = lax.axis_size(axis)
        forward = [(i, i + 1) for i in range(count - 1)]
        backward = [(target, source) for source, target in forward]
        low = lax.ppermute(
            lax.slice_in_dim(block, block.shape[dim] - width, None, axis=dim), axis, forward
        )
        high = lax.ppermute(lax.slice_in_dim(block, 0, width, axis=dim), axis, backward)
        block = jnp.concatenate([low, block, high], axis=dim)
    return block


def neighbours(padded):
    return [
        padded[..., 2:, 1:-1, 1:-1],
        padded[..., :-2, 1:-1, 1:-1],
        padded[..., 1:-1, 2:, 1:-1],
        padded[..., 1:-1, :-2, 1:-1],
        padded[..., 1:-1, 1:-1, 2:],
        padded[..., 1:-1, 1:-1, :-2],
    ]


def halo_stack(stacked):
    return padded_2(stacked, (("span", 1), ("height", 2), ("depth", 3)), 1)


def cell_sums(first, second):
    return jnp.sum(first * second, axis=(1, 2, 3))


def paired_sums(residual, search, image):
    return lax.psum(
        (cell_sums(residual, search), cell_sums(image, search)), ("span", "height", "depth")
    )


def local(load, phase, void, owner, precond):
    extents = phase.shape
    bricks_x, bricks_y, bricks_z = void.shape
    solid_bricks = (1 - void).astype(jnp.float32)
    expanded = jnp.broadcast_to(
        solid_bricks[:, None, :, None, :, None], (bricks_x, BE, bricks_y, BE, bricks_z, BE)
    )
    cell_mask = expanded.reshape(extents)
    stiffness = void_stiffness + (1.0 - void_stiffness) * phase**3
    coefficients = halo_stack(jnp.stack([cell_mask, cell_mask * stiffness]))
    near_pairs = neighbours(coefficients)
    weights = [cell_mask * 0.5 * (pair[0] * stiffness + pair[1]) for pair in near_pairs]

    def operate(field):
        padded = halo_stack(field)
        total = cell_mask * spring_rate * field
        for weight, near in zip(weights, neighbours(padded)):
            total = total + weight * (field - near)
        return (total, padded)

    span_count = lax.axis_size("span")
    slot_count = precond.shape[0]
    capacity = slot_count // span_count
    solid_flat = (1 - void).reshape(-1)
    owner_flat = owner.reshape(-1)
    columns = jnp.arange(span_count, dtype=jnp.int32)
    onehot = (owner_flat[:, None] == columns[None, :]).astype(jnp.int32) * solid_flat[:, None]
    before = jnp.cumsum(onehot, axis=0) - onehot
    rank = jnp.sum(before * onehot, axis=1)
    slot_of_brick = owner_flat * capacity + rank
    slot_ids = jnp.arange(slot_count, dtype=jnp.int32)
    matched = (slot_of_brick[None, :] == slot_ids[:, None]).astype(jnp.float32) * solid_flat[
        None, :
    ].astype(jnp.float32)
    selector = matched.reshape(slot_count, bricks_x, bricks_y, bricks_z)
    selector_low = selector.astype(jnp.bfloat16)
    loads = load.shape[0]

    def apply_blocks(incoming):
        image = jnp.einsum("sij,slj->sli", precond, incoming, preferred_element_type=jnp.float32)
        return lax.all_to_all(image, "span", split_axis=0, concat_axis=0, tiled=True)

    def precondition(residual):
        split = residual.astype(jnp.bfloat16).reshape(
            loads, bricks_x, BE, bricks_y, BE, bricks_z, BE
        )
        outgoing = jnp.einsum(
            "sxyz,lxiyjzk->slijk", selector_low, split, preferred_element_type=jnp.float32
        )
        outgoing = outgoing.astype(jnp.bfloat16).reshape(slot_count, loads, BE**3)
        returned = apply_blocks(
            lax.all_to_all(outgoing, "span", split_axis=0, concat_axis=0, tiled=True)
        )
        shaped = returned.reshape(slot_count, loads, BE, BE, BE)
        placed = jnp.einsum(
            "sxyz,slijk->lxiyjzk", selector, shaped, precision=lax.Precision.HIGHEST
        )
        return placed.reshape(loads, extents[0], extents[1], extents[2])

    right_side = cell_mask[None] * load
    solution = jnp.zeros_like(right_side)
    padded_solution = 0.0
    residual = right_side
    search = precondition(residual)
    image, padded_search = operate(search)
    norm_now, curvature_sum = paired_sums(residual, search, image)
    step_size = norm_now / curvature_sum
    direction = search
    padded_direction = padded_search
    along = image
    for iteration in range(ITERS):
        solution = solution + step_size[:, None, None, None] * direction
        padded_solution = padded_solution + step_size[:, None, None, None] * padded_direction
        residual = residual - step_size[:, None, None, None] * along
        if iteration + 1 < ITERS:
            search = precondition(residual)
            image, padded_search = operate(search)
            norm_next, curvature_sum = paired_sums(residual, search, image)
            factor = norm_next / norm_now
            step_size = norm_next / (curvature_sum - factor * norm_next / step_size)
            direction = search + factor[:, None, None, None] * direction
            padded_direction = padded_search + factor[:, None, None, None] * padded_direction
            along = image + factor[:, None, None, None] * along
            norm_now = norm_next
    solution_padded = halo_stack(solution)
    energy = jnp.zeros_like(phase)
    for pair, near in zip(near_pairs, neighbours(solution_padded)):
        energy = energy + pair[0] * jnp.sum((solution - near) ** 2, axis=0)
    sensitivity = -1.5 * (1.0 - void_stiffness) * phase**2 * cell_mask * energy
    peak_value = lax.pmax(jnp.max(-sensitivity), ("span", "height", "depth"))
    drive = (
        phase / time_step
        - 0.5 * phase * (1.0 - phase) * (1.0 - 2.0 * phase)
        - sensitivity / (peak_value + epsilon_peak)
    )
    inverse = 1.0 / (1.0 / time_step + 6.0 * interface_weight)
    current = phase
    for sweep_index in range(SWEEPS):
        padded = padded_2(
            current.astype(jnp.bfloat16), (("span", 0), ("height", 1), ("depth", 2)), 1
        ).astype(current.dtype)
        beside_all = neighbours(padded)
        current = (
            drive
            + interface_weight
            * (
                beside_all[0]
                + beside_all[1]
                + beside_all[2]
                + beside_all[3]
                + beside_all[4]
                + beside_all[5]
            )
        ) * inverse
    return (solution, sensitivity, current)


def solution(mesh):
    return jax.shard_map(
        local,
        mesh=mesh,
        in_specs=(
            P(None, "span", "height", "depth"),
            P("span", "height", "depth"),
            P("span", "height", "depth"),
            P("span", "height", "depth"),
            P(("span", "height", "depth"), None, None),
        ),
        out_specs=(
            P(None, "span", "height", "depth"),
            P("span", "height", "depth"),
            P("span", "height", "depth"),
        ),
        check_vma=False,
    )
```

profile of v0, /device:TPU:14, one launch (start us, length us, event | category | flops | bytes accessed | tf_op | source)
XLA Modules:
  0.0 461.6 jit_solution(4808410751461738423)
XLA Ops:
  5.8 2.4 collective-permute-start
  10.2 10.6 %reshape.116 = bf16[8,2,8,2,8,16,8]{6,5,4,3,2,1,0:T(8,128)(2,1)} reshape(bf16[8,16,16,128]{3,2,1,0:T(8,128)(2,1)S(1)} %multiply_convert_fusion) | data formatting | bytes 1048576 | tf_op jit(solution)/shard_map/reshape | solution.py:99
  25.2 6.2 %bitcast_convert_fusion.1 = bf16[16,8,8,8,8]{0,4,3,2,1:T(8,128)(2,1)S(1)} fusion(bf16[8,2,8,2,8,16,8]{6,5,4,3,2,1,0:T(8,128)(2,1)} %reshape.116, f32[2,2,16]{2,1,0:T(2,128)S(1)} %copy-done.42, s32[2,2,16]{2,1,0:T(2,128)S(1)} %multiply_add_fusion.1), kind=kOutput, calls=%fused_computation.3 | convolution fusion | flops 8456192 | bytes 655872 | tf_op jit(solution)/shard_map/sxyz,lxiyjzk->slijk/dot_general | solution.py:102
  32.5 6.0 %all-to-all-start = ((bf16[16,8,512]{2,1,0:T(8,128)(2,1)}), bf16[16,8,512]{2,1,0:T(8,128)(2,1)S(1)}, u32[]{:S(2)}, u32[]{:S(2)}) async-start(bf16[16,8,512]{2,1,0:T(8,128)(2,1)} %copy.23), calls=%async_computation | async-start | bytes 262144 | tf_op jit(solution)/shard_map/all_to_all | solution.py:107
  39.6 3.5 collective-permute-start.10
  43.1 3.2 collective-permute-start.8
  46.3 6.4 %fusion.123 = f32[16,8,512]{2,1,0:T(8,128)} fusion(bf16[16,8,512]{2,1,0:T(8,128)(2,1)S(1)} %all-to-all-done, bf16[16,512,512]{2,1,0:T(8,128)(2,1)} %param.9), kind=kOutput, calls=%fused_computation.250 | convolution fusion | flops 67108864 | bytes 8781824 | tf_op jit(solution)/shard_map/sij,slj->sli/dot_general | solution.py:95
  52.7 4.3 all-to-all-start.1
  61.9 9.6 %convolution_bitcast_fusion.1 = f32[8,2,8,2,8,16,8]{5,6,3,1,4,2,0:T(8,128)} fusion(f32[16,8,8,8,8,1,1]{0,4,6,5,3,2,1:T(8,128)S(1)} %bitcast.148, f32[2,2,16]{2,1,0:T(2,128)} %copy-done.41, s32[2,2,16]{2,1,0:T(2,128)} %copy-done.44), kind=kOutput, calls=%fused_computation.1 | convolution fusion | flops 50333696 | bytes 1311232 | tf_op jit(solution)/shard_map/sxyz,slijk->lxiyjzk/dot_general | solution.py:110
  71.4 12.3 %copy.25 = f32[8,2,8,2,8,16,8]{6,5,4,3,2,1,0:T(8,128)} copy(f32[8,2,8,2,8,16,8]{5,6,3,1,4,2,0:T(8,128)} %convolution_bitcast_fusion.1) | data formatting | bytes 2097152 | tf_op jit(solution)/shard_map/sxyz,slijk->lxiyjzk/transpose | solution.py:110
  83.8 11.8 %reshape.119 = f32[8,16,16,128]{3,2,1,0:T(8,128)S(1)} reshape(f32[8,2,8,2,8,16,8]{6,5,4,3,2,1,0:T(8,128)} %copy.25) | data formatting | bytes 2097152 | tf_op jit(solution)/shard_map/reshape | solution.py:113
  97.7 4.5 collective-permute-start.1
  117.7 2.7 collective-permute-start.11
  122.8 3.1 collective-permute-start.9
  132.2 5.9 %multiply_reduce_fusion.1 = (f32[8]{0:T(128)}, f32[8]{0:T(128)}, f32[8,16,16,128]{3,2,1,0:T(8,128)S(1)}) fusion(f32[8,16,16,128]{3,2,1,0:T(8,128)S(1)} %reshape.119, f32[8,16,16,128]{3,2,1,0:T(8,128)S(1)} %copy-done.1, f32[16,16,128]{2,1,0:T(8,128)S(1)} %mul.300, f32[8,18,1,128]{3,2,1,0:T(1,128)} %copy-done.33, f32[8,18,16,128]{3,2,1,0:T(8,128)} %copy-done.7, ...), kind=kLoop, calls=%fused_computation.104 | loop fusion | flops 8912880 | bytes 5673280 | tf_op jit(solution)/shard_map/reduce_sum | solution.py:47
  138.1 42.8 %all-reduce.1 = (f32[8]{0:T(128)}, f32[8]{0:T(128)}) all-reduce(f32[8]{0:T(128)} %get-tuple-element.10, f32[8]{0:T(128)} %get-tuple-element.9), channel_id=1, replica_groups=mesh['span'=2,'height'=4,'depth'=4] {'span','height','depth'}, use_global_device_ids=true, to_apply=%region_3.4 | all-reduce | flops 16 | bytes 128 | tf_op jit(solution)/shard_map/psum | solution.py:51
  183.2 11.9 %reshape.121 = bf16[8,2,8,2,8,16,8]{6,5,4,3,2,1,0:T(8,128)(2,1)} reshape(bf16[8,16,16,128]{3,2,1,0:T(8,128)(2,1)} %fusion.87) | data formatting | bytes 1048576 | tf_op jit(solution)/shard_map/reshape | solution.py:99
  195.1 6.2 %bitcast_convert_fusion = bf16[16,8,8,8,8]{0,4,3,2,1:T(8,128)(2,1)S(1)} fusion(bf16[8,2,8,2,8,16,8]{6,5,4,3,2,1,0:T(8,128)(2,1)} %reshape.121, f32[2,2,16]{2,1,0:T(2,128)} %copy-done.41, s32[2,2,16]{2,1,0:T(2,128)} %copy-done.44), kind=kOutput, calls=%fused_computation.2 | convolution fusion | flops 8456192 | bytes 655872 | tf_op jit(solution)/shard_map/sxyz,lxiyjzk->slijk/dot_general | solution.py:102
  201.7 5.5 %all_to_all.20 = bf16[16,8,512]{2,1,0:T(8,128)(2,1)S(1)} all-to-all(bf16[16,8,512]{2,1,0:T(8,128)(2,1)S(1)} %copy.31), channel_id=1, replica_groups=mesh['span'=2,'height'=4,'depth'=4] {'span'}, dimensions={0} | all-to-all | bytes 262144 | tf_op jit(solution)/shard_map/all_to_all | solution.py:107
  207.2 5.6 %fusion.124 = f32[16,8,512]{2,1,0:T(8,128)S(1)} fusion(bf16[16,8,512]{2,1,0:T(8,128)(2,1)S(1)} %all_to_all.20, bf16[16,512,512]{2,1,0:T(8,128)(2,1)} %param.9), kind=kOutput, calls=%fused_computation.251 | convolution fusion | flops 67108864 | bytes 8781824 | tf_op jit(solution)/shard_map/sij,slj->sli/dot_general | solution.py:95
  212.8 7.7 %all_to_all.21 = f32[16,8,512]{2,1,0:T(8,128)S(1)} all-to-all(f32[16,8,512]{2,1,0:T(8,128)S(1)} %fusion.124), channel_id=1, replica_groups=mesh['span'=2,'height'=4,'depth'=4] {'span'}, dimensions={0} | all-to-all | bytes 524288 | tf_op jit(solution)/shard_map/all_to_all | solution.py:96
  222.5 10.1 %convolution_bitcast_fusion = f32[8,2,8,2,8,16,8]{5,6,3,1,4,2,0:T(8,128)} fusion(f32[16,8,8,8,8,1,1]{0,4,6,5,3,2,1:T(8,128)} %bitcast.147, f32[2,2,16]{2,1,0:T(2,128)S(1)} %copy-done.43, s32[2,2,16]{2,1,0:T(2,128)S(1)} %copy-done.45), kind=kOutput, calls=%fused_computation | convolution fusion | flops 50333696 | bytes 1311232 | tf_op jit(solution)/shard_map/sxyz,slijk->lxiyjzk/dot_general | solution.py:110
  232.6 12.3 %copy.33 = f32[8,2,8,2,8,16,8]{6,5,4,3,2,1,0:T(8,128)} copy(f32[8,2,8,2,8,16,8]{5,6,3,1,4,2,0:T(8,128)} %convolution_bitcast_fusion) | data formatting | bytes 2097152 | tf_op jit(solution)/shard_map/sxyz,slijk->lxiyjzk/transpose | solution.py:110
  244.9 11.9 %reshape.124 = f32[8,16,16,128]{3,2,1,0:T(8,128)S(1)} reshape(f32[8,2,8,2,8,16,8]{6,5,4,3,2,1,0:T(8,128)} %copy.33) | data formatting | bytes 2097152 | tf_op jit(solution)/shard_map/reshape | solution.py:113
  258.8 4.5 collective-permute-start.25
  264.6 4.7 %collective-permute-start.12 = (f32[8,1,16,128]{3,2,1,0:T(8,128)S(1)}, f32[8,1,16,128]{3,2,1,0:T(8,128)S(1)}, u32[]{:S(2)}, u32[]{:S(2)}) collective-permute-start(f32[8,1,16,128]{3,2,1,0:T(8,128)S(1)} %get-tuple-element.34), channel_id=1, source_target_pairs={{16,0},{17,1},{18,2},{19,3},{20,4},{21,5},{22,6},{23,7},{24,8},{25... | collective-permute-start | bytes 196616 | tf_op jit(solution)/shard_map/ppermute | solution.py:26
  276.7 3.2 collective-permute-start.27
  285.2 3.1 copy.36
  288.2 3.3 collective-permute-start.17
  291.5 3.0 copy.34
  294.6 3.2 collective-permute-start.16
  298.6 3.1 copy.37
  301.7 3.1 copy.35
  304.9 5.0 %fusion.22 = f32[8]{0:T(128)S(1)} fusion(f32[8,16,16,128]{3,2,1,0:T(8,128)S(1)} %reshape.124, f32[8,18,18,1]{3,2,1,0:T(8,128)} %copy.37, f32[8,18,1,128]{3,2,1,0:T(1,128)S(1)} %collective-permute-done.14, f32[8,18,16,128]{3,2,1,0:T(8,128)} %copy-done.8, f32[8,18,1,128]{3,2,1,0:T(1,128)} %copy-done.35, f32[8,18,18,1]{3,2,1,0:T(8,128)} %copy.35, ...), kind=kLoop, calls=%fused_computation.48 | loop fusion | flops 8126456 | bytes 3445024 | tf_op jit(solution)/shard_map/reduce_sum | solution.py:47
  309.9 39.8 %all-reduce = (f32[8]{0:T(128)S(1)}, f32[8]{0:T(128)S(1)}) all-reduce(f32[8]{0:T(128)S(1)} %copy-done.59, f32[8]{0:T(128)S(1)} %fusion.22), channel_id=1, replica_groups=mesh['span'=2,'height'=4,'depth'=4] {'span','height','depth'}, use_global_device_ids=true, to_apply=%region_7.8 | all-reduce | flops 16 | bytes 128 | tf_op jit(solution)/shard_map/psum | solution.py:51
  350.8 2.8 collective-permute-start.18
  356.0 3.3 collective-permute-start.29
  359.2 2.6 collective-permute-start.28
  371.6 3.0 copy.38
  374.7 3.3 collective-permute-start.22
  379.5 2.6 collective-permute-start.23
  388.2 3.2 fusion.5
  393.4 41.7 %pmax.7 = f32[]{:T(128)} all-reduce(f32[]{:T(128)} %get-tuple-element.15), channel_id=1, replica_groups=mesh['span'=2,'height'=4,'depth'=4] {'span','height','depth'}, use_global_device_ids=true, to_apply=%region_17.18 | all-reduce | flops 1 | bytes 8 | tf_op jit(solution)/shard_map/pmax | solution.py:145
  439.1 4.2 collective-permute-done.30
  447.7 2.6 collective-permute-done.32
  450.4 3.2 collective-permute-start.35
  453.6 2.6 collective-permute-start.34
  457.0 3.2 collective-permute-done.34
  (245 shorter events, 97.9 us)
Async XLA Ops:
  5.8 15.1 %collective-permute-start = (f32[2,1,16,128]{3,2,1,0:T(8,128)S(1)}, f32[2,1,16,128]{3,2,1,0:T(8,128)S(1)}, u32[]{:S(2)}, u32[]{:S(2)}) collective-permute-start(f32[2,1,16,128]{3,2,1,0:T(8,128)S(1)} %get-tuple-element.49), channel_id=1, source_target_pairs={{16,0},{17,1},{18,2},{19,3},{20,4},{21,5},{22,6},{23,7},{24,8},{25... | collective-permute-start | bytes 49160 | tf_op jit(solution)/shard_map/ppermute | solution.py:26
  8.2 12.6 %collective-permute-start.2 = (f32[2,1,16,128]{3,2,1,0:T(8,128)S(1)}, f32[2,1,16,128]{3,2,1,0:T(8,128)S(1)}, u32[]{:S(2)}, u32[]{:S(2)}) collective-permute-start(f32[2,1,16,128]{3,2,1,0:T(8,128)S(1)} %get-tuple-element.48), channel_id=1, source_target_pairs={{0,16},{1,17},{2,18},{3,19},{4,20},{5,21},{6,22},{7,23},{8,24},{9,... | collective-permute-start | bytes 49160 | tf_op jit(solution)/shard_map/ppermute | solution.py:23
  20.8 36.2 %copy-start.21 = (f32[2,1,16,128]{3,2,1,0:T(8,128)}, f32[2,1,16,128]{3,2,1,0:T(8,128)S(1)}, u32[]{:S(2)}) copy-start(f32[2,1,16,128]{3,2,1,0:T(8,128)S(1)} %collective-permute-done.2) | copy-start | bytes 49156
  20.9 17.6 %collective-permute-start.4 = (f32[2,18,1,128]{3,2,1,0:T(1,128)S(1)}, f32[2,18,1,128]{3,2,1,0:T(1,128)S(1)}, u32[]{:S(2)}, u32[]{:S(2)}) collective-permute-start(f32[2,18,1,128]{3,2,1,0:T(1,128)S(1)} %get-tuple-element.47), channel_id=1, source_target_pairs={{4,0},{8,4},{12,8},{5,1},{9,5},{13,9},{6,2},{10,6},{14,10},{7,3},{... | collective-permute-start | bytes 55304 | tf_op jit(solution)/shard_map/ppermute | solution.py:26
  22.8 15.7 %collective-permute-start.6 = (f32[2,18,1,128]{3,2,1,0:T(1,128)S(1)}, f32[2,18,1,128]{3,2,1,0:T(1,128)S(1)}, u32[]{:S(2)}, u32[]{:S(2)}) collective-permute-start(f32[2,18,1,128]{3,2,1,0:T(1,128)S(1)} %get-tuple-element.46), channel_id=1, source_target_pairs={{0,4},{4,8},{8,12},{1,5},{5,9},{9,13},{2,6},{6,10},{10,14},{3,7},{... | collective-permute-start | bytes 55304 | tf_op jit(solution)/shard_map/ppermute | solution.py:23
  32.5 13.9 %all-to-all-start = ((bf16[16,8,512]{2,1,0:T(8,128)(2,1)}), bf16[16,8,512]{2,1,0:T(8,128)(2,1)S(1)}, u32[]{:S(2)}, u32[]{:S(2)}) async-start(bf16[16,8,512]{2,1,0:T(8,128)(2,1)} %copy.23), calls=%async_computation | async-start | bytes 262144 | tf_op jit(solution)/shard_map/all_to_all | solution.py:107
  38.5 18.6 %copy-start.30 = (f32[2,18,1,128]{3,2,1,0:T(1,128)}, f32[2,18,1,128]{3,2,1,0:T(1,128)S(1)}, u32[]{:S(2)}) copy-start(f32[2,18,1,128]{3,2,1,0:T(1,128)S(1)} %collective-permute-done.6) | copy-start | bytes 55300
  39.6 69.5 %collective-permute-start.10 = (f32[2,18,18,1]{3,2,1,0:T(8,128)}, f32[2,18,18,1]{3,2,1,0:T(8,128)}, u32[]{:S(2)}, u32[]{:S(2)}) collective-permute-start(f32[2,18,18,1]{3,2,1,0:T(8,128)} %get-tuple-element.45), channel_id=1, source_target_pairs={{0,1},{1,2},{2,3},{4,5},{5,6},{6,7},{8,9},{9,10},{10,11},{12,13},{... | collective-permute-start | bytes 7784 | tf_op jit(solution)/shard_map/ppermute | solution.py:23
  43.1 82.8 %collective-permute-start.8 = (f32[2,18,18,1]{3,2,1,0:T(8,128)}, f32[2,18,18,1]{3,2,1,0:T(8,128)}, u32[]{:S(2)}, u32[]{:S(2)}) collective-permute-start(f32[2,18,18,1]{3,2,1,0:T(8,128)} %get-tuple-element.44), channel_id=1, source_target_pairs={{1,0},{2,1},{3,2},{5,4},{6,5},{7,6},{9,8},{10,9},{11,10},{13,12},{... | collective-permute-start | bytes 7784 | tf_op jit(solution)/shard_map/ppermute | solution.py:26
  52.7 7.6 %all-to-all-start.1 = ((f32[16,8,512]{2,1,0:T(8,128)}), f32[16,8,512]{2,1,0:T(8,128)}, u32[]{:S(2)}, u32[]{:S(2)}) async-start(f32[16,8,512]{2,1,0:T(8,128)} %fusion.123), calls=%async_computation.1 | async-start | bytes 524288 | tf_op jit(solution)/shard_map/all_to_all | solution.py:96
  95.6 6.7 %collective-permute-start.3 = (f32[8,1,16,128]{3,2,1,0:T(8,128)S(1)}, f32[8,1,16,128]{3,2,1,0:T(8,128)S(1)}, u32[]{:S(2)}, u32[]{:S(2)}) collective-permute-start(f32[8,1,16,128]{3,2,1,0:T(8,128)S(1)} %get-tuple-element.39), channel_id=1, source_target_pairs={{0,16},{1,17},{2,18},{3,19},{4,20},{5,21},{6,22},{7,23},{8,24},{9,... | collective-permute-start | bytes 196616 | tf_op jit(solution)/shard_map/ppermute | solution.py:23
  97.7 6.4 %collective-permute-start.1 = (f32[8,1,16,128]{3,2,1,0:T(8,128)S(1)}, f32[8,1,16,128]{3,2,1,0:T(8,128)S(1)}, u32[]{:S(2)}, u32[]{:S(2)}) collective-permute-start(f32[8,1,16,128]{3,2,1,0:T(8,128)S(1)} %get-tuple-element.38), channel_id=1, source_target_pairs={{16,0},{17,1},{18,2},{19,3},{20,4},{21,5},{22,6},{23,7},{24,8},{25... | collective-permute-start | bytes 196616 | tf_op jit(solution)/shard_map/ppermute | solution.py:26
  104.8 6.2 %collective-permute-start.5 = (f32[8,18,1,128]{3,2,1,0:T(1,128)S(1)}, f32[8,18,1,128]{3,2,1,0:T(1,128)S(1)}, u32[]{:S(2)}, u32[]{:S(2)}) collective-permute-start(f32[8,18,1,128]{3,2,1,0:T(1,128)S(1)} %get-tuple-element.31), channel_id=1, source_target_pairs={{4,0},{8,4},{12,8},{5,1},{9,5},{13,9},{6,2},{10,6},{14,10},{7,3},{... | collective-permute-start | bytes 221192 | tf_op jit(solution)/shard_map/ppermute | solution.py:26
  106.9 5.7 %collective-permute-start.7 = (f32[8,18,1,128]{3,2,1,0:T(1,128)S(1)}, f32[8,18,1,128]{3,2,1,0:T(1,128)S(1)}, u32[]{:S(2)}, u32[]{:S(2)}) collective-permute-start(f32[8,18,1,128]{3,2,1,0:T(1,128)S(1)} %get-tuple-element.30), channel_id=1, source_target_pairs={{0,4},{4,8},{8,12},{1,5},{5,9},{9,13},{2,6},{6,10},{10,14},{3,7},{... | collective-permute-start | bytes 221192 | tf_op jit(solution)/shard_map/ppermute | solution.py:23
  117.7 10.2 %collective-permute-start.11 = (f32[8,18,18,1]{2,0,3,1:T(8,128)S(1)}, f32[8,18,18,1]{2,0,3,1:T(8,128)S(1)}, u32[]{:S(2)}, u32[]{:S(2)}) collective-permute-start(f32[8,18,18,1]{2,0,3,1:T(8,128)S(1)} %copy.28), channel_id=1, source_target_pairs={{0,1},{1,2},{2,3},{4,5},{5,6},{6,7},{8,9},{9,10},{10,11},{12,13},{... | collective-permute-start | bytes 31112 | tf_op jit(solution)/shard_map/ppermute | solution.py:23
  122.8 7.2 %collective-permute-start.9 = (f32[8,18,18,1]{2,0,3,1:T(8,128)S(1)}, f32[8,18,18,1]{2,0,3,1:T(8,128)S(1)}, u32[]{:S(2)}, u32[]{:S(2)}) collective-permute-start(f32[8,18,18,1]{2,0,3,1:T(8,128)S(1)} %copy.26), channel_id=1, source_target_pairs={{1,0},{2,1},{3,2},{5,4},{6,5},{7,6},{9,8},{10,9},{11,10},{13,12},{... | collective-permute-start | bytes 31112 | tf_op jit(solution)/shard_map/ppermute | solution.py:26
  138.1 57.0 %copy-start.3 = (f32[8,16,16,128]{3,2,1,0:T(8,128)}, f32[8,16,16,128]{3,2,1,0:T(8,128)S(1)}, u32[]{:S(2)}) copy-start(f32[8,16,16,128]{3,2,1,0:T(8,128)S(1)} %get-tuple-element.19) | copy-start | bytes 3145732
  244.9 25.1 %copy-start.2 = (f32[8,16,16,128]{3,2,1,0:T(8,128)S(1)}, f32[8,16,16,128]{3,2,1,0:T(8,128)}, u32[]{:S(2)}) copy-start(f32[8,16,16,128]{3,2,1,0:T(8,128)} %param.5) | copy-start | bytes 3145732
  256.8 12.6 %collective-permute-start.13 = (f32[8,1,16,128]{3,2,1,0:T(8,128)S(1)}, f32[8,1,16,128]{3,2,1,0:T(8,128)S(1)}, u32[]{:S(2)}, u32[]{:S(2)}) collective-permute-start(f32[8,1,16,128]{3,2,1,0:T(8,128)S(1)} %get-tuple-element.35), channel_id=1, source_target_pairs={{0,16},{1,17},{2,18},{3,19},{4,20},{5,21},{6,22},{7,23},{8,24},{9,... | collective-permute-start | bytes 196616 | tf_op jit(solution)/shard_map/ppermute | solution.py:23
  258.8 17.9 %collective-permute-start.25 = (bf16[1,16,128]{2,1,0:T(8,128)(2,1)S(1)}, bf16[1,16,128]{2,1,0:T(8,128)(2,1)S(1)}, u32[]{:S(2)}, u32[]{:S(2)}) collective-permute-start(bf16[1,16,128]{2,1,0:T(8,128)(2,1)S(1)} %get-tuple-element.63), channel_id=1, source_target_pairs={{16,0},{17,1},{18,2},{19,3},{20,4},{21,5},{22,6},{23,7},{24,8},{25... | collective-permute-start | bytes 12296 | tf_op jit(solution)/shard_map/ppermute | solution.py:26
  263.3 13.4 %collective-permute-start.24 = (bf16[1,16,128]{2,1,0:T(8,128)(2,1)S(1)}, bf16[1,16,128]{2,1,0:T(8,128)(2,1)S(1)}, u32[]{:S(2)}, u32[]{:S(2)}) collective-permute-start(bf16[1,16,128]{2,1,0:T(8,128)(2,1)S(1)} %get-tuple-element.62), channel_id=1, source_target_pairs={{0,16},{1,17},{2,18},{3,19},{4,20},{5,21},{6,22},{7,23},{8,24},{9,... | collective-permute-start | bytes 12296 | tf_op jit(solution)/shard_map/ppermute | solution.py:23
  264.6 7.6 %collective-permute-start.12 = (f32[8,1,16,128]{3,2,1,0:T(8,128)S(1)}, f32[8,1,16,128]{3,2,1,0:T(8,128)S(1)}, u32[]{:S(2)}, u32[]{:S(2)}) collective-permute-start(f32[8,1,16,128]{3,2,1,0:T(8,128)S(1)} %get-tuple-element.34), channel_id=1, source_target_pairs={{16,0},{17,1},{18,2},{19,3},{20,4},{21,5},{22,6},{23,7},{24,8},{25... | collective-permute-start | bytes 196616 | tf_op jit(solution)/shard_map/ppermute | solution.py:26
  272.3 9.5 %collective-permute-start.14 = (f32[8,18,1,128]{3,2,1,0:T(1,128)S(1)}, f32[8,18,1,128]{3,2,1,0:T(1,128)S(1)}, u32[]{:S(2)}, u32[]{:S(2)}) collective-permute-start(f32[8,18,1,128]{3,2,1,0:T(1,128)S(1)} %get-tuple-element.29), channel_id=1, source_target_pairs={{4,0},{8,4},{12,8},{5,1},{9,5},{13,9},{6,2},{10,6},{14,10},{7,3},{... | collective-permute-start | bytes 221192 | tf_op jit(solution)/shard_map/ppermute | solution.py:26
  274.2 7.6 %collective-permute-start.15 = (f32[8,18,1,128]{3,2,1,0:T(1,128)S(1)}, f32[8,18,1,128]{3,2,1,0:T(1,128)S(1)}, u32[]{:S(2)}, u32[]{:S(2)}) collective-permute-start(f32[8,18,1,128]{3,2,1,0:T(1,128)S(1)} %get-tuple-element.28), channel_id=1, source_target_pairs={{0,4},{4,8},{8,12},{1,5},{5,9},{9,13},{2,6},{6,10},{10,14},{3,7},{... | collective-permute-start | bytes 221192 | tf_op jit(solution)/shard_map/ppermute | solution.py:23
  276.7 21.0 %collective-permute-start.27 = (bf16[18,1,128]{2,1,0:T(2,128)(2,1)S(1)}, bf16[18,1,128]{2,1,0:T(2,128)(2,1)S(1)}, u32[]{:S(2)}, u32[]{:S(2)}) collective-permute-start(bf16[18,1,128]{2,1,0:T(2,128)(2,1)S(1)} %get-tuple-element.59), channel_id=1, source_target_pairs={{4,0},{8,4},{12,8},{5,1},{9,5},{13,9},{6,2},{10,6},{14,10},{7,3},{... | collective-permute-start | bytes 13832 | tf_op jit(solution)/shard_map/ppermute | solution.py:26
  279.9 17.9 %collective-permute-start.26 = (bf16[18,1,128]{2,1,0:T(2,128)(2,1)S(1)}, bf16[18,1,128]{2,1,0:T(2,128)(2,1)S(1)}, u32[]{:S(2)}, u32[]{:S(2)}) collective-permute-start(bf16[18,1,128]{2,1,0:T(2,128)(2,1)S(1)} %get-tuple-element.58), channel_id=1, source_target_pairs={{0,4},{4,8},{8,12},{1,5},{5,9},{9,13},{2,6},{6,10},{10,14},{3,7},{... | collective-permute-start | bytes 13832 | tf_op jit(solution)/shard_map/ppermute | solution.py:23
  288.2 10.3 %collective-permute-start.17 = (f32[8,18,18,1]{2,0,3,1:T(8,128)}, f32[8,18,18,1]{2,0,3,1:T(8,128)}, u32[]{:S(2)}, u32[]{:S(2)}) collective-permute-start(f32[8,18,18,1]{2,0,3,1:T(8,128)} %copy.36), channel_id=1, source_target_pairs={{0,1},{1,2},{2,3},{4,5},{5,6},{6,7},{8,9},{9,10},{10,11},{12,13},{... | collective-permute-start | bytes 31112 | tf_op jit(solution)/shard_map/ppermute | solution.py:23
  294.6 7.1 %collective-permute-start.16 = (f32[8,18,18,1]{2,0,3,1:T(8,128)}, f32[8,18,18,1]{2,0,3,1:T(8,128)}, u32[]{:S(2)}, u32[]{:S(2)}) collective-permute-start(f32[8,18,18,1]{2,0,3,1:T(8,128)} %copy.34), channel_id=1, source_target_pairs={{1,0},{2,1},{3,2},{5,4},{6,5},{7,6},{9,8},{10,9},{11,10},{13,12},{... | collective-permute-start | bytes 31112 | tf_op jit(solution)/shard_map/ppermute | solution.py:26
  304.8 44.9 %copy-start.60 = (f32[8]{0:T(128)S(1)}, f32[8]{0:T(128)}, u32[]{:S(2)}) copy-start(f32[8]{0:T(128)} %get-tuple-element.13) | copy-start | bytes 100
  304.8 44.9 %copy-start.61 = (f32[8]{0:T(128)S(1)}, f32[8]{0:T(128)}, u32[]{:S(2)}) copy-start(f32[8]{0:T(128)} %get-tuple-element.14) | copy-start | bytes 100
  350.7 37.4 %copy-start = (f32[8,16,16,128]{3,2,1,0:T(8,128)}, f32[8,16,16,128]{3,2,1,0:T(8,128)S(1)}, u32[]{:S(2)}) copy-start(f32[8,16,16,128]{3,2,1,0:T(8,128)S(1)} %multiply_add_fusion) | copy-start | bytes 3145732
  350.7 15.6 %copy-start.20 = (bf16[16,16,128]{2,1,0:T(8,128)(2,1)S(1)}, bf16[16,16,128]{2,1,0:T(8,128)(2,1)}, u32[]{:S(2)}) copy-start(bf16[16,16,128]{2,1,0:T(8,128)(2,1)} %get-tuple-element.50) | copy-start | bytes 196612
  350.8 11.1 %collective-permute-start.18 = (f32[8,1,16,128]{3,2,1,0:T(8,128)S(1)}, f32[8,1,16,128]{3,2,1,0:T(8,128)S(1)}, u32[]{:S(2)}, u32[]{:S(2)}) collective-permute-start(f32[8,1,16,128]{3,2,1,0:T(8,128)S(1)} %get-tuple-element.33), channel_id=1, source_target_pairs={{16,0},{17,1},{18,2},{19,3},{20,4},{21,5},{22,6},{23,7},{24,8},{25... | collective-permute-start | bytes 196616 | tf_op jit(solution)/shard_map/ppermute | solution.py:26
  353.6 8.2 %collective-permute-start.19 = (f32[8,1,16,128]{3,2,1,0:T(8,128)S(1)}, f32[8,1,16,128]{3,2,1,0:T(8,128)S(1)}, u32[]{:S(2)}, u32[]{:S(2)}) collective-permute-start(f32[8,1,16,128]{3,2,1,0:T(8,128)S(1)} %get-tuple-element.32), channel_id=1, source_target_pairs={{0,16},{1,17},{2,18},{3,19},{4,20},{5,21},{6,22},{7,23},{8,24},{9,... | collective-permute-start | bytes 196616 | tf_op jit(solution)/shard_map/ppermute | solution.py:23
  356.0 10.3 %collective-permute-start.29 = (bf16[18,18,1]{2,1,0:T(8,128)(2,1)S(1)}, bf16[18,18,1]{2,1,0:T(8,128)(2,1)S(1)}, u32[]{:S(2)}, u32[]{:S(2)}) collective-permute-start(bf16[18,18,1]{2,1,0:T(8,128)(2,1)S(1)} %get-tuple-element.55), channel_id=1, source_target_pairs={{1,0},{2,1},{3,2},{5,4},{6,5},{7,6},{9,8},{10,9},{11,10},{13,12},{... | collective-permute-start | bytes 1952 | tf_op jit(solution)/shard_map/ppermute | solution.py:26
  359.2 7.1 %collective-permute-start.28 = (bf16[18,18,1]{2,1,0:T(8,128)(2,1)S(1)}, bf16[18,18,1]{2,1,0:T(8,128)(2,1)S(1)}, u32[]{:S(2)}, u32[]{:S(2)}) collective-permute-start(bf16[18,18,1]{2,1,0:T(8,128)(2,1)S(1)} %get-tuple-element.54), channel_id=1, source_target_pairs={{0,1},{1,2},{2,3},{4,5},{5,6},{6,7},{8,9},{9,10},{10,11},{12,13},{... | collective-permute-start | bytes 1952 | tf_op jit(solution)/shard_map/ppermute | solution.py:23
  362.0 5.4 %collective-permute-start.20 = (f32[8,18,1,128]{3,2,1,0:T(1,128)S(1)}, f32[8,18,1,128]{3,2,1,0:T(1,128)S(1)}, u32[]{:S(2)}, u32[]{:S(2)}) collective-permute-start(f32[8,18,1,128]{3,2,1,0:T(1,128)S(1)} %get-tuple-element.27), channel_id=1, source_target_pairs={{4,0},{8,4},{12,8},{5,1},{9,5},{13,9},{6,2},{10,6},{14,10},{7,3},{... | collective-permute-start | bytes 221192 | tf_op jit(solution)/shard_map/ppermute | solution.py:26
  363.9 5.7 %collective-permute-start.21 = (f32[8,18,1,128]{3,2,1,0:T(1,128)S(1)}, f32[8,18,1,128]{3,2,1,0:T(1,128)S(1)}, u32[]{:S(2)}, u32[]{:S(2)}) collective-permute-start(f32[8,18,1,128]{3,2,1,0:T(1,128)S(1)} %get-tuple-element.26), channel_id=1, source_target_pairs={{0,4},{4,8},{8,12},{1,5},{5,9},{9,13},{2,6},{6,10},{10,14},{3,7},{... | collective-permute-start | bytes 221192 | tf_op jit(solution)/shard_map/ppermute | solution.py:23
  374.7 8.4 %collective-permute-start.22 = (f32[8,18,18,1]{2,0,3,1:T(8,128)}, f32[8,18,18,1]{2,0,3,1:T(8,128)}, u32[]{:S(2)}, u32[]{:S(2)}) collective-permute-start(f32[8,18,18,1]{2,0,3,1:T(8,128)} %copy.38), channel_id=1, source_target_pairs={{1,0},{2,1},{3,2},{5,4},{6,5},{7,6},{9,8},{10,9},{11,10},{13,12},{... | collective-permute-start | bytes 31112 | tf_op jit(solution)/shard_map/ppermute | solution.py:26
  379.5 6.4 %collective-permute-start.23 = (f32[8,18,18,1]{2,0,3,1:T(8,128)}, f32[8,18,18,1]{2,0,3,1:T(8,128)S(1)}, u32[]{:S(2)}, u32[]{:S(2)}) collective-permute-start(f32[8,18,18,1]{2,0,3,1:T(8,128)} %copy.40), channel_id=1, source_target_pairs={{0,1},{1,2},{2,3},{4,5},{5,6},{6,7},{8,9},{9,10},{10,11},{12,13},{... | collective-permute-start | bytes 31112 | tf_op jit(solution)/shard_map/ppermute | solution.py:23
  391.4 44.4 %copy-start.9 = (f32[18,18,130]{2,1,0:T(8,128)S(1)}, f32[18,18,130]{2,1,0:T(8,128)}, u32[]{:S(2)}) copy-start(f32[18,18,130]{2,1,0:T(8,128)} %maximum_convert_fusion) | copy-start | bytes 505444
  393.4 68.0 %copy-start.17 = (f32[16,16,128]{2,1,0:T(8,128)}, f32[16,16,128]{2,1,0:T(8,128)S(1)}, u32[]{:S(2)}) copy-start(f32[16,16,128]{2,1,0:T(8,128)S(1)} %get-tuple-element.16) | copy-start | bytes 393220
  436.1 3.1 collective-permute-start.31
  437.8 5.5 %collective-permute-start.30 = (bf16[1,16,128]{2,1,0:T(8,128)(2,1)S(1)}, bf16[1,16,128]{2,1,0:T(8,128)(2,1)S(1)}, u32[]{:S(2)}, u32[]{:S(2)}) collective-permute-start(bf16[1,16,128]{2,1,0:T(8,128)(2,1)S(1)} %get-tuple-element.60), channel_id=1, source_target_pairs={{0,16},{1,17},{2,18},{3,19},{4,20},{5,21},{6,22},{7,23},{8,24},{9,... | collective-permute-start | bytes 12296 | tf_op jit(solution)/shard_map/ppermute | solution.py:23
  443.3 4.3 collective-permute-start.33
  445.2 5.0 %collective-permute-start.32 = (bf16[18,1,128]{2,1,0:T(2,128)(2,1)S(1)}, bf16[18,1,128]{2,1,0:T(2,128)(2,1)S(1)}, u32[]{:S(2)}, u32[]{:S(2)}) collective-permute-start(bf16[18,1,128]{2,1,0:T(2,128)(2,1)S(1)} %get-tuple-element.56), channel_id=1, source_target_pairs={{0,4},{4,8},{8,12},{1,5},{5,9},{9,13},{2,6},{6,10},{10,14},{3,7},{... | collective-permute-start | bytes 13832 | tf_op jit(solution)/shard_map/ppermute | solution.py:23
  450.4 6.6 %collective-permute-start.35 = (bf16[18,18,1]{2,1,0:T(8,128)(2,1)S(1)}, bf16[18,18,1]{2,1,0:T(8,128)(2,1)S(1)}, u32[]{:S(2)}, u32[]{:S(2)}) collective-permute-start(bf16[18,18,1]{2,1,0:T(8,128)(2,1)S(1)} %get-tuple-element.53), channel_id=1, source_target_pairs={{1,0},{2,1},{3,2},{5,4},{6,5},{7,6},{9,8},{10,9},{11,10},{13,12},{... | collective-permute-start | bytes 1952 | tf_op jit(solution)/shard_map/ppermute | solution.py:26
  453.6 6.6 %collective-permute-start.34 = (bf16[18,18,1]{2,1,0:T(8,128)(2,1)S(1)}, bf16[18,18,1]{2,1,0:T(8,128)(2,1)S(1)}, u32[]{:S(2)}, u32[]{:S(2)}) collective-permute-start(bf16[18,18,1]{2,1,0:T(8,128)(2,1)S(1)} %get-tuple-element.52), channel_id=1, source_target_pairs={{0,1},{1,2},{2,3},{4,5},{5,6},{6,7},{8,9},{9,10},{10,11},{12,13},{... | collective-permute-start | bytes 1952 | tf_op jit(solution)/shard_map/ppermute | solution.py:23
  (52 other events, 400.6 us)
where the time goes:
time: 471 us; the launch traced here: 462 us
  blocking collectives  138 us (29%)
  local copies, waits for them, and re-layouts  121 us (26%)
  starting transfers between devices  102 us (22%)
  matrix products  44 us (9%)
  other arithmetic  34.2 us (7%)
  waiting for transfers between devices  19.7 us (4%)
    psum x2, blocking collectives, paired_sums(): lax.psum((cell_sums(residual, search), cell_sums(image, search)), ('span'...  82.7 us
    ppermute x18, starting transfers between devices, padded_2(): lax.ppermute(lax.slice_in_dim(block, 0, width, axis=dim), axis, backward)  53 us
    pmax x1, blocking collectives, local(): peak_value = lax.pmax(jnp.max(-sensitivity), ('span', 'height', 'depth'))  41.7 us
    ppermute x18, starting transfers between devices, padded_2(): lax.ppermute(lax.slice_in_dim(block, block.shape[dim] - width, None, axis...  38.7 us
    transpose x2, local copies, waits for them, and re-layouts, precondition(): jnp.einsum('sxyz,slijk->lxiyjzk', selector, shaped, precision=lax.Precisi...  24.7 us
    reshape x2, local copies, waits for them, and re-layouts, precondition(): return placed.reshape(loads, extents[0], extents[1], extents[2])  23.7 us
    reshape x2, local copies, waits for them, and re-layouts, precondition(): residual.astype(jnp.bfloat16)  22.5 us
    dot_general x2, matrix products, precondition(): jnp.einsum('sxyz,slijk->lxiyjzk', selector, shaped, precision=lax.Precisi...  19.6 us
  transfers between devices with their start and end apart: 38, of which 9 were waited for; matrix products, arithmetic and copies ran while one was open for 21% of the time, Pallas kernels for 0%

commit v1 on v0

v1 whole, which is shorter than its diff:
```python
import jax
import jax.numpy as jnp
from jax import lax
from jax.experimental import pallas as pl
from jax.experimental.pallas import tpu as pltpu
from jax.sharding import PartitionSpec as P

BE = 8
AXES = ("span", "height", "depth")

void_stiffness = 0.001
spring_rate = 0.05
time_step = 0.5
interface_weight = 0.5
epsilon_peak = 1e-06
inverse = 1.0 / (1.0 / time_step + 6.0 * interface_weight)

F32 = jnp.float32
BF16 = jnp.bfloat16
VM = pl.BlockSpec(memory_space=pltpu.VMEM)
SM = pl.BlockSpec(memory_space=pltpu.SMEM)


def call(kernel, ins, outs, scratch=(), aliases=None, flops=0, name=None):
    return pl.pallas_call(
        kernel,
        in_specs=[spec for _, spec in ins],
        out_specs=[spec for _, _, spec in outs],
        out_shape=[jax.ShapeDtypeStruct(shape, dtype) for shape, dtype, _ in outs],
        scratch_shapes=list(scratch),
        input_output_aliases=aliases or {},
        cost_estimate=pl.CostEstimate(flops=flops, bytes_accessed=1 << 20, transcendentals=0),
        name=name,
    )(*[array for array, _ in ins])


def local(load, phase, void, owner, precond):
    loads, X, Y, Z = load.shape
    bricks_x, bricks_y, bricks_z = void.shape
    bricks = bricks_x * bricks_y * bricks_z
    T = Y // BE
    tiles = X * T
    cells = BE**3
    lanes = Z
    assert lanes == 128 and BE == 8 and lanes % tiles == 0
    per_pack = lanes // tiles
    packs = -(-loads // per_pack)
    assert loads % per_pack == 0 and per_pack >= 2
    sizes = [lax.axis_size(axis) for axis in AXES]
    assert all(size % 2 == 0 for size in sizes)
    spans = sizes[0]
    devices = sizes[0] * sizes[1] * sizes[2]
    slots = precond.shape[0]
    cap = slots // spans
    bits = 32 // spans
    assert cap < (1 << min(bits, 8)) and bits >= 2
    remote = (spans - 1) * cap

    coords = jnp.stack([lax.axis_index(axis) for axis in AXES]).astype(jnp.int32)
    load_f = load.reshape(loads, X * Y, Z)
    phase_f = phase.reshape(X * Y, Z)
    void_f = void.reshape(bricks)
    owner_f = owner.reshape(bricks)

    def iotas():
        return (
            lax.broadcasted_iota(jnp.int32, (8, lanes), 0),
            lax.broadcasted_iota(jnp.int32, (8, lanes), 1),
        )

    def row(x, t):
        start = x * Y + t * 8
        return pl.ds(start if isinstance(start, int) else pl.multiple_of(start, 8), 8)

    def brick_at(n):
        m = jnp.maximum(n, 0)
        return m // (bricks_y * bricks_z), (m // bricks_z) % bricks_y, m % bricks_z

    def stagger(tile, shift):
        sub, _ = iotas()
        for bit in (1, 2, 4):
            turned = pltpu.roll(tile, bit * shift % lanes, 1)
            tile = jnp.where((sub & bit) != 0, turned, tile)
        return tile

    def gather_bricks(source, table, base, count, out):
        sub, lane = iotas()
        keep = ((lane >> 3) & 7) == sub
        pick = (
            lax.broadcasted_iota(jnp.int32, (loads, loads * 8), 1) >> 3
            == lax.broadcasted_iota(jnp.int32, (loads, loads * 8), 0)
        ).astype(F32).astype(BF16)

        def one(r, carry):
            n = table[base + r]
            bx, by, bz = brick_at(n)

            @pl.when(n >= 0)
            def _():
                rows = []
                for l in range(loads):
                    merged = jnp.zeros((8, lanes), F32)
                    for i in range(BE):
                        group = 8 * (i % 2) + i // 2
                        tile = source[l, row(bx * 8 + i, by), :]
                        merged = jnp.where(
                            (lane >> 3) == group,
                            pltpu.roll(tile, (8 * group + lanes - 8 * bz) % lanes, 1),
                            merged,
                        )
                    merged = stagger(merged, 8)
                    columns = []
                    for q in range(4):
                        turned = pltpu.roll(merged, lanes - 8 * q, 1) if q else merged
                        columns.append(jnp.where(keep, turned, 0.0))
                    rows.append(jnp.concatenate(columns, axis=1))
                stacked = jnp.concatenate(rows, axis=0).astype(BF16)
                out[r] = jnp.dot(pick, stacked, preferred_element_type=F32).astype(BF16)

            @pl.when(n < 0)
            def _():
                out[r] = jnp.zeros((loads, cells), BF16)

            return carry

        lax.fori_loop(0, count, one, 0)

    def scatter_bricks(field, table, base, count, images):
        sub, lane = iotas()
        keep = ((lane >> 3) & 7) == sub

        def one(r, carry):
            n = table[base + r]
            bx, by, bz = brick_at(n)
            inside = (lane >> 3) == bz

            @pl.when(n >= 0)
            def _():
                for l in range(loads):
                    merged = jnp.zeros((8, lanes), F32)
                    for q in range(4):
                        spread = jnp.where(
                            keep,
                            jnp.broadcast_to(
                                images[r, pl.ds(l, 1), pl.ds(q * lanes, lanes)], (8, lanes)
                            ),
                            0.0,
                        )
                        merged = merged + (pltpu.roll(spread, 8 * q, 1) if q else spread)
                    merged = stagger(merged, lanes - 8)
                    for i in range(BE):
                        group = 8 * (i % 2) + i // 2
                        turned = pltpu.roll(merged, (8 * bz + lanes - 8 * group) % lanes, 1)
                        at = row(bx * 8 + i, by)
                        field[l, at, :] = jnp.where(inside, turned, field[l, at, :])

            return carry

        lax.fori_loop(0, count, one, 0)

    def pack_depth(read, offsets, source_lane, acc):
        sub, lane = iotas()
        for x in range(X):
            for t in range(T):
                place = offsets + x * T + t
                acc = jnp.where(
                    lane == place,
                    pltpu.roll(read(x, t), (place + lanes - source_lane) % lanes, 1),
                    acc,
                )
        return acc

    def faces(read_tile, read_rows, coords_ref, count, index, outs, pack_index, offset):
        xa, xb, ya, yb, za, zb = outs
        odd = [coords_ref[d] % 2 for d in range(3)]
        for out, low in ((xa, odd[0]), (xb, 1 - odd[0])):
            x = (1 - low) * (X - 1)
            for t in range(T):
                out[index, pl.ds(t * 8, 8), :] = read_tile(x, t)
        for out, low in ((ya, odd[1]), (yb, 1 - odd[1])):
            y = (1 - low) * (Y - 1)
            out[index] = read_rows(y)
        for out, low in ((za, odd[2]), (zb, 1 - odd[2])):
            out[pack_index] = pack_depth(
                read_tile, offset, (1 - low) * (lanes - 1), out[pack_index]
            )

    def unswap(coords_ref, d, a, b, low, high):
        even = coords_ref[d] % 2 == 0
        has_low = coords_ref[d] > 0
        has_high = coords_ref[d] < sizes[d] - 1
        lead = a.shape[0]

        @pl.when(even)
        def _():
            high[...] = a[...]

        @pl.when(jnp.logical_not(even))
        def _():
            low[...] = a[...]

        if sizes[d] > 2:

            @pl.when(even)
            def _():
                low[...] = b[...]

            @pl.when(jnp.logical_not(even))
            def _():
                high[...] = b[...]

        @pl.when(jnp.logical_not(has_low))
        def _():
            low[...] = jnp.zeros(low.shape, F32)

        @pl.when(jnp.logical_not(has_high))
        def _():
            high[...] = jnp.zeros(high.shape, F32)

    def unswap_all(coords_ref, received, halos):
        for d in range(3):
            unswap(coords_ref, d, *received[2 * d : 2 * d + 2], *halos[2 * d : 2 * d + 2])

    def neighbours(read, x, t, first, last, halos, index, pack_index, offset):
        xl, xh, yl, yh, zl, zh = halos
        sub, lane = iotas()
        tile = read(x, t)
        at_t = pl.ds(t * 8, 8)
        x_low = xl[index, at_t, :] if first else read(x - 1, t)
        x_high = xh[index, at_t, :] if last else read(x + 1, t)

        def spread(ref):
            return jnp.broadcast_to(ref[index, pl.ds(x, 1), :], (8, lanes))

        before = spread(yl) if t == 0 else read(x, t - 1)
        after = spread(yh) if t == T - 1 else read(x, t + 1)
        y_low = pltpu.roll(jnp.where(sub == 7, before, tile), 1, 0)
        y_high = pltpu.roll(jnp.where(sub == 0, after, tile), 7, 0)
        place = offset + x * T + t
        z_low = jnp.where(
            lane == 0,
            pltpu.roll(zl[pack_index], (lanes - place) % lanes, 1),
            pltpu.roll(tile, 1, 1),
        )
        z_high = jnp.where(
            lane == lanes - 1,
            pltpu.roll(zh[pack_index], (2 * lanes - 1 - place) % lanes, 1),
            pltpu.roll(tile, lanes - 1, 1),
        )
        return tile, (x_low, x_high, y_low, y_high, z_low, z_high)

    def over_rows(body):
        body(0, True, False)

        def middle(x, carry):
            body(x, False, False)
            return carry

        lax.fori_loop(1, X - 1, middle, 0)
        body(X - 1, False, True)

    def halo_scratch(extra, extra_packs):
        shapes = ((loads + extra, Y, Z), (loads + extra, X, Z), (packs + extra_packs, 8, Z))
        return [pltpu.VMEM(shape, F32) for shape in shapes for _ in range(2)]

    def plain_halo_scratch(count):
        shapes = ((count, Y, Z), (count, X, Z), (1, 8, Z))
        return [pltpu.VMEM(shape, F32) for shape in shapes for _ in range(2)]

    def face_outs(count, pack_count):
        shapes = ((count, Y, Z), (count, X, Z), (pack_count, 8, Z))
        return [(shape, F32, VM) for shape in shapes for _ in range(2)]

    def exchange(payload):
        received = []
        for d, axis in enumerate(AXES):
            n = sizes[d]
            swap_a = [(i, i + 1 if i % 2 == 0 else i - 1) for i in range(n)]
            swap_b = [(i, (i - 1) % n if i % 2 == 0 else (i + 1) % n) for i in range(n)]
            received.append(lax.ppermute(payload[2 * d], axis, swap_a))
            received.append(
                lax.ppermute(payload[2 * d + 1], axis, swap_b) if n > 2 else received[-1]
            )
        return received

    def to_owners(rows, sign):
        parts = []
        for shift in range(1, spans):
            part = rows[(shift - 1) * cap : shift * cap]
            parts.append(
                lax.ppermute(
                    part, "span", [(i, (i + sign * shift) % spans) for i in range(spans)]
                )
            )
        return parts[0] if spans == 2 else jnp.concatenate(parts, axis=0)

    def everyone(partial):
        return lax.all_to_all(partial, AXES, split_axis=0, concat_axis=0, tiled=True)

    def first_kernel(coords_ref, void_ref, owner_ref, load_ref, table_ref, near_ref, far_ref):
        me = coords_ref[0]
        for i in range(slots + 1):
            table_ref[i] = -1
        used = jnp.int32(0)
        for n in range(bricks):
            solid = 1 - void_ref[n]
            relative = jnp.where(solid == 1, (owner_ref[n] + spans - me) % spans, 0)
            shift = relative * bits
            rank = lax.shift_right_logical(used, shift) & ((1 << bits) - 1)
            index = jnp.where(solid == 1, relative * cap + rank, slots)
            table_ref[index] = n
            used = used + lax.shift_left(solid, shift)
        gather_bricks(load_ref, table_ref, cap, remote, far_ref)
        gather_bricks(load_ref, table_ref, 0, cap, near_ref)

    table, near, far = call(
        first_kernel,
        [(coords, SM), (void_f, SM), (owner_f, SM), (load_f, VM)],
        [
            ((slots + 1,), jnp.int32, SM),
            ((cap, loads, cells), BF16, VM),
            ((remote, loads, cells), BF16, VM),
        ],
        name="first",
    )

    step = 2 if cap % 2 == 0 else 1

    def blocks(rows, far_side):
        count = rows.shape[0]

        def kernel(coords_ref, rows_ref, blocks_ref, out_ref):
            for i in range(step):
                out_ref[i] = jnp.dot(
                    rows_ref[i], blocks_ref[i], preferred_element_type=F32
                )

        per = cap // step

        def block_index(r, coords_ref):
            shift = r // per + 1 if far_side else 0
            source = (coords_ref[0] + spans - shift) % spans
            return (source * per + r % per, 0, 0)

        return pl.pallas_call(
            kernel,
            grid_spec=pltpu.PrefetchScalarGridSpec(
                num_scalar_prefetch=1,
                grid=(count // step,),
                in_specs=[
                    pl.BlockSpec((step, loads, cells), lambda r, c: (r, 0, 0)),
                    pl.BlockSpec((step, cells, cells), block_index),
                ],
                out_specs=pl.BlockSpec((step, loads, cells), lambda r, c: (r, 0, 0)),
            ),
            out_shape=jax.ShapeDtypeStruct((count, loads, cells), F32),
            cost_estimate=pl.CostEstimate(
                flops=4000000000, bytes_accessed=count * cells * cells * 2, transcendentals=0
            ),
            name="blocks_far" if far_side else "blocks_near",
        )(coords, rows, precond)

    def precondition(near_rows, far_rows):
        arrived = to_owners(far_rows, 1)
        near_image = blocks(near_rows, False)
        far_image = to_owners(blocks(arrived, True), -1)
        return near_image, far_image

    def near_kernel(with_stiffness):
        def kernel(*refs):
            if with_stiffness:
                table_ref, image_ref, void_ref, phase_ref, field_ref, ks_ref = refs
            else:
                table_ref, image_ref, field_ref = refs
            field_ref[...] = jnp.zeros(field_ref.shape, F32)
            scatter_bricks(field_ref, table_ref, 0, cap, image_ref)
            if with_stiffness:
                sub, lane = iotas()
                for bx in range(bricks_x):
                    for by in range(bricks_y):
                        mask = jnp.zeros((8, lanes), F32)
                        for bz in range(bricks_z):
                            solid = 1 - void_ref[(bx * bricks_y + by) * bricks_z + bz]
                            mask = jnp.where(
                                (lane >> 3) == bz, solid.astype(F32), mask
                            )
                        for i in range(BE):
                            at = row(bx * BE + i, by)
                            p = phase_ref[at, :]
                            stiffness = void_stiffness + (1.0 - void_stiffness) * (p * p * p)
                            ks_ref[at, :] = mask * stiffness

        return kernel

    field_shape = (loads, X * Y, Z)
    plain_shape = (X * Y, Z)

    def far_kernel(extra):
        def kernel(table_ref, coords_ref, image_ref, begun_ref, *refs):
            extras = refs[:extra]
            field_ref = refs[extra]
            outs = refs[extra + 1 :]
            field_ref[...] = begun_ref[...]
            scatter_bricks(field_ref, table_ref, cap, remote, image_ref)
            for out in outs[4:]:
                out[...] = jnp.zeros(out.shape, F32)
            for l in range(loads):
                faces(
                    lambda x, t: field_ref[l, row(x, t), :],
                    lambda y: field_ref[l, pl.ds(y, X, stride=Y), :],
                    coords_ref, loads, l, outs, l // per_pack, (l % per_pack) * tiles,
                )
            for e in range(extra):
                ref = extras[e]
                faces(
                    lambda x, t: ref[row(x, t), :],
                    lambda y: ref[pl.ds(y, X, stride=Y), :],
                    coords_ref, loads, loads + e, outs, packs, e * tiles,
                )

        return kernel

    def to_field(images, extras, with_stiffness):
        near_image, far_image = images
        ins = [(table, SM), (near_image, VM)]
        outs = [(field_shape, F32, VM)]
        if with_stiffness:
            ins += [(void_f, SM), (phase_f, VM)]
            outs += [(plain_shape, F32, VM)]
        made = call(
            near_kernel(with_stiffness), ins, outs, flops=2000000000,
            name="near" + str(len(extras)),
        )
        field = made[0]
        if with_stiffness:
            extras = [made[1]] + extras
        result = call(
            far_kernel(len(extras)),
            [(table, SM), (coords, SM), (far_image, VM), (field, VM)]
            + [(e, VM) for e in extras],
            [(field_shape, F32, VM)] + face_outs(loads + len(extras), packs + 1),
            name="far" + str(len(extras)),
        )
        return result[0], exchange(result[1:]), made[1:]

    z_field, z_halo, (ks,) = to_field(precondition(near, far), [phase_f], True)

    def operate_kernel(
        coords_ref, table_ref, z_ref, load_ref, ks_ref, phase_ref, *refs
    ):
        received = refs[:6]
        q_ref, weight_ref, start_ref, dots_ref, near_ref, far_ref = refs[6:12]
        halos = refs[12:]
        unswap_all(coords_ref, received, halos)
        dots_ref[...] = jnp.zeros(dots_ref.shape, F32)

        def body(x, first, last):
            for t in range(T):
                at = row(x, t)
                ks_tile, ks_near = neighbours(
                    lambda x, t: ks_ref[row(x, t), :],
                    x, t, first, last, halos, loads, packs, 0,
                )
                p, p_near = neighbours(
                    lambda x, t: phase_ref[row(x, t), :],
                    x, t, first, last, halos, loads + 1, packs, tiles,
                )
                around = p_near[0]
                for other in p_near[1:]:
                    around = around + other
                start_ref[at, :] = (
                    p / time_step
                    - 0.5 * p * (1.0 - p) * (1.0 - 2.0 * p)
                    + interface_weight * around
                ) * inverse
                total = jnp.where(ks_tile > 0.0, spring_rate, 0.0)
                weights = []
                for d in range(6):
                    both = jnp.logical_and(ks_tile > 0.0, ks_near[d] > 0.0)
                    weight = jnp.where(both, 0.5 * (ks_tile + ks_near[d]), 0.0)
                    weights.append(weight)
                    weight_ref[d + 1, at, :] = weight
                    total = total + weight
                weight_ref[0, at, :] = total
                for l in range(loads):
                    tile, near_tiles = neighbours(
                        lambda x, t: z_ref[l, row(x, t), :],
                        x, t, first, last, halos, l, l // per_pack, (l % per_pack) * tiles,
                    )
                    image = total * tile
                    for d in range(6):
                        image = image - weights[d] * near_tiles[d]
                    q_ref[l, at, :] = image
                    dots_ref[0, l] += load_ref[l, at, :] * tile
                    dots_ref[1, l] += image * tile

        over_rows(body)
        gather_bricks(q_ref, table_ref, cap, remote, far_ref)
        gather_bricks(q_ref, table_ref, 0, cap, near_ref)

    q_field, weights, start, dots, near, far = call(
        operate_kernel,
        [(coords, SM), (table, SM), (z_field, VM), (load_f, VM), (ks, VM), (phase_f, VM)]
        + [(a, VM) for a in z_halo],
        [
            (field_shape, F32, VM),
            ((7, X * Y, Z), F32, VM),
            (plain_shape, F32, VM),
            ((2, loads, 8, Z), F32, VM),
            ((cap, loads, cells), BF16, VM),
            ((remote, loads, cells), BF16, VM),
        ],
        scratch=halo_scratch(2, 1),
        name="operate",
    )

    w_field, w_halo, _ = to_field(precondition(near, far), [start], False)

    products = 5

    def dots_kernel(
        coords_ref, w_ref, q_ref, load_ref, weight_ref, dots_ref, *refs
    ):
        received = refs[:6]
        out_ref = refs[6]
        more_ref = refs[7]
        halos = refs[8:]
        unswap_all(coords_ref, received, halos)
        more_ref[...] = jnp.zeros(more_ref.shape, F32)

        def body(x, first, last):
            for t in range(T):
                at = row(x, t)
                weights = [weight_ref[d, at, :] for d in range(7)]
                for l in range(loads):
                    tile, near_tiles = neighbours(
                        lambda x, t: w_ref[l, row(x, t), :],
                        x, t, first, last, halos, l, l // per_pack, (l % per_pack) * tiles,
                    )
                    image = weights[0] * tile
                    for d in range(6):
                        image = image - weights[d + 1] * near_tiles[d]
                    more_ref[0, l] += load_ref[l, at, :] * tile
                    more_ref[1, l] += q_ref[l, at, :] * tile
                    more_ref[2, l] += image * tile

        over_rows(body)
        sub, lane = iotas()
        result = jnp.zeros((1, lanes), F32)
        lane1 = lane[:1]
        for k in range(products):
            for l in range(loads):
                part = dots_ref[k, l] if k < 2 else more_ref[k - 2, l]
                value = jnp.sum(jnp.sum(part, axis=0, keepdims=True), axis=1, keepdims=True)
                result = jnp.where(lane1 == k * loads + l, value, result)
        out_ref[...] = jnp.broadcast_to(result, (devices, lanes))

    (partial,) = call(
        dots_kernel,
        [(coords, SM), (w_field, VM), (q_field, VM), (load_f, VM), (weights, VM), (dots, VM)]
        + [(a, VM) for a in w_halo],
        [((devices, lanes), F32, VM)],
        scratch=[pltpu.VMEM((3, loads, 8, Z), F32)] + halo_scratch(1, 1),
        name="dots",
    )
    sums = everyone(partial)

    def solve_kernel(coords_ref, sums_ref, z_ref, w_ref, weight_ref, phase_ref, *refs):
        z_received = refs[:6]
        w_received = refs[6:12]
        x_ref, sens_ref, peak_ref = refs[12:15]
        outs = refs[15:21]
        halos = refs[21:27]
        mixed = refs[27:33]
        sub, lane = iotas()
        total = jnp.sum(sums_ref[...], axis=0, keepdims=True)

        def product(k):
            return pltpu.roll(total, (lanes - k * loads) % lanes, 1)

        total = jnp.broadcast_to(total, (8, lanes))
        bz, zq, bw, qw, ws = [product(k) for k in range(products)]
        alpha = bz / zq
        bz_next = bz - alpha * (bw + zq) + alpha * alpha * qw
        beta = bz_next / bz
        grow = 1.0 + beta
        curvature = grow * grow * zq - 2.0 * grow * alpha * qw + alpha * alpha * ws
        alpha_next = bz_next / curvature
        for_z = alpha + alpha_next * grow
        for_w = -alpha_next * alpha
        c_z = [jnp.broadcast_to(for_z[0:1, l : l + 1], (8, lanes)) for l in range(loads)]
        c_w = [jnp.broadcast_to(for_w[0:1, l : l + 1], (8, lanes)) for l in range(loads)]

        for a, b, out in zip(z_received[:4], w_received[:4], mixed[:4]):
            for l in range(loads):
                for i in range(a.shape[1] // 8):
                    at = pl.ds(i * 8, 8)
                    out[l, at, :] = c_z[l] * a[l, at, :] + c_w[l] * b[l, at, :]
        for a, b, out in zip(z_received[4:], w_received[4:], mixed[4:]):
            for k in range(packs):
                value_z = c_z[k * per_pack]
                value_w = c_w[k * per_pack]
                for i in range(1, per_pack):
                    value_z = jnp.where(lane >= i * tiles, c_z[k * per_pack + i], value_z)
                    value_w = jnp.where(lane >= i * tiles, c_w[k * per_pack + i], value_w)
                out[k] = value_z * a[k] + value_w * b[k]
        unswap_all(coords_ref, mixed, halos)

        def combine(x, carry):
            for t in range(T):
                at = row(x, t)
                for l in range(loads):
                    x_ref[l, at, :] = c_z[l] * z_ref[l, at, :] + c_w[l] * w_ref[l, at, :]
            return carry

        lax.fori_loop(0, X, combine, 0)
        peak_ref[pl.ds(0, 8), :] = jnp.zeros((8, lanes), F32)

        def body(x, first, last):
            for t in range(T):
                at = row(x, t)
                sums_of = [jnp.zeros((8, lanes), F32) for _ in range(6)]
                for l in range(loads):
                    tile, near_tiles = neighbours(
                        lambda x, t: x_ref[l, row(x, t), :],
                        x, t, first, last, halos, l, l // per_pack, (l % per_pack) * tiles,
                    )
                    for d in range(6):
                        gap = tile - near_tiles[d]
                        sums_of[d] = sums_of[d] + gap * gap
                energy = jnp.zeros((8, lanes), F32)
                for d in range(6):
                    energy = energy + jnp.where(
                        weight_ref[d + 1, at, :] > 0.0, sums_of[d], 0.0
                    )
                p = phase_ref[at, :]
                negative = 1.5 * (1.0 - void_stiffness) * (p * p) * energy
                sens_ref[at, :] = -negative
                peak_ref[pl.ds(0, 8), :] = jnp.maximum(peak_ref[pl.ds(0, 8), :], negative)

        over_rows(body)
        peak = jnp.max(
            jnp.max(peak_ref[pl.ds(0, 8), :], axis=0, keepdims=True), axis=1, keepdims=True
        )
        peak_ref[...] = jnp.broadcast_to(peak, (devices, lanes))
        for out in outs[4:]:
            out[...] = jnp.zeros(out.shape, F32)
        faces(
            lambda x, t: sens_ref[row(x, t), :],
            lambda y: sens_ref[pl.ds(y, X, stride=Y), :],
            coords_ref, 0, 0, outs, 0, 0,
        )

    made = call(
        solve_kernel,
        [(coords, SM), (sums, VM), (z_field, VM), (w_field, VM), (weights, VM), (phase_f, VM)]
        + [(a, VM) for a in z_halo]
        + [(a, VM) for a in w_halo],
        [(field_shape, F32, VM), (plain_shape, F32, VM), ((devices, lanes), F32, VM)]
        + face_outs(1, 1),
        scratch=halo_scratch(0, 0) + halo_scratch(0, 0),
        name="solve",
    )
    displacement, sensitivity, peak = made[:3]
    sens_halo = exchange(made[3:])
    peaks = everyone(peak)

    def sweep_kernel(coords_ref, peaks_ref, sens_ref, start_ref, phase_ref, *refs):
        sens_received = refs[:6]
        start_received = refs[6:12]
        out_ref = refs[12]
        once_ref = refs[13]
        halos = refs[14:20]
        mixed = refs[20:26]
        sub, lane = iotas()
        peak = jnp.max(
            jnp.max(peaks_ref[...], axis=0, keepdims=True), axis=1, keepdims=True
        )
        scale = jnp.broadcast_to(1.0 / (peak + epsilon_peak), (8, lanes))
        for s, b, out in zip(sens_received[:4], start_received[:4], mixed[:4]):
            for i in range(out.shape[1] // 8):
                at = pl.ds(i * 8, 8)
                out[0, at, :] = b[loads, at, :] - inverse * (s[0, at, :] * scale)
        for s, b, out in zip(sens_received[4:], start_received[4:], mixed[4:]):
            out[0] = b[packs] - inverse * (s[0] * scale)
        unswap_all(coords_ref, mixed, halos)
        for i in range(tiles):
            at = pl.ds(i * 8, 8)
            once_ref[at, :] = start_ref[at, :] - inverse * (sens_ref[at, :] * scale)

        def body(x, first, last):
            for t in range(T):
                at = row(x, t)
                _, near_tiles = neighbours(
                    lambda x, t: once_ref[row(x, t), :],
                    x, t, first, last, halos, 0, 0, 0,
                )
                around = near_tiles[0]
                for other in near_tiles[1:]:
                    around = around + other
                p = phase_ref[at, :]
                drive = (
                    p / time_step
                    - 0.5 * p * (1.0 - p) * (1.0 - 2.0 * p)
                    - sens_ref[at, :] * scale
                )
                out_ref[at, :] = (drive + interface_weight * around) * inverse

        over_rows(body)

    (phase_next,) = call(
        sweep_kernel,
        [(coords, SM), (peaks, VM), (sensitivity, VM), (start, VM), (phase_f, VM)]
        + [(a, VM) for a in sens_halo]
        + [(a, VM) for a in w_halo],
        [(plain_shape, F32, VM)],
        scratch=[pltpu.VMEM(plain_shape, F32)] + plain_halo_scratch(1) + plain_halo_scratch(1),
        name="sweeps",
    )
    return (
        displacement.reshape(load.shape),
        sensitivity.reshape(phase.shape),
        phase_next.reshape(phase.shape),
    )


def solution(mesh):
    return jax.shard_map(
        local,
        mesh=mesh,
        in_specs=(
            P(None, "span", "height", "depth"),
            P("span", "height", "depth"),
            P("span", "height", "depth"),
            P("span", "height", "depth"),
            P(("span", "height", "depth"), None, None),
        ),
        out_specs=(
            P(None, "span", "height", "depth"),
            P("span", "height", "depth"),
            P("span", "height", "depth"),
        ),
        check_vma=False,
    )
```

time: 471 us -> 141 us (0.30)
  the two profiles are of different devices: /device:TPU:14 before, /device:TPU:0 now
where the time goes in v1:
time: 141 us; the launch traced here: 139 us
  Pallas kernels  76.5 us (54%)
  starting transfers between devices  32.3 us (23%)
  blocking collectives  11.5 us (8%)
  waiting for transfers between devices  10.1 us (7%)
  local copies, waits for them, and re-layouts  7.05 us (5%)
    pallas_call x9, Pallas kernels, call(): pl.pallas_call(kernel, in_specs=[spec for _, spec in ins], out_specs=[spe...  56.6 us
    pallas_call x4, Pallas kernels, blocks(): pl.pallas_call(kernel, grid_spec=pltpu.PrefetchScalarGridSpec(num_scalar_...  19.9 us
    ppermute x6, starting transfers between devices, exchange(): lax.ppermute(payload[2 * d + 1], axis, swap_b)  18.2 us
    all_to_all x1, blocking collectives, everyone(): lax.all_to_all(partial, AXES, split_axis=0, concat_axis=0, tiled=True)  11.5 us
    ppermute x6, waiting for transfers between devices, exchange(): lax.ppermute(payload[2 * d + 1], axis, swap_b)  8.15 us
    ppermute x9, starting transfers between devices, exchange(): received.append(lax.ppermute(payload[2 * d], axis, swap_a))  7.39 us
    unnamed x40, local copies, waits for them, and re-layouts  4.47 us
    ppermute x4, starting transfers between devices, to_owners(): lax.ppermute(part, 'span', [(i, (i + sign * shift) % spans) for i in rang...  4.15 us
  transfers between devices with their start and end apart: 20, of which 4 were waited for; matrix products, arithmetic and copies ran while one was open for 0% of the time, Pallas kernels for 15%

profile of v1, /device:TPU:0, one launch (start us, length us, event | category | flops | bytes accessed | tf_op | source)
XLA Modules:
  0.0 138.8 jit_solution(10234024685715965839)
XLA Ops:
  0.6 1.2 reshape.31.void_ref.refs_2_
  1.9 1.3 reshape.32.owner_ref
  3.2 0.6 pad_add_fusion.coords_ref
  3.8 8.0 %first.1 = (s32[17]{0:T(128)}, bf16[8,8,512]{2,1,0:T(8,128)(2,1)}, bf16[8,8,512]{2,1,0:T(8,128)(2,1)}) custom-call(s32[3]{0:T(128)} %pad_add_fusion.coords_ref, s32[64]{0:T(128)} %reshape.31.void_ref.refs_2_, s32[64]{0:T(128)} %reshape.32.owner_ref, f32[8,256,128]{2,1,0:T(8,128)} %bitcast.16), custom_call_target="tpu_custom_call" | custom-call | bytes 1048576 | tf_op jit(solution)/shard_map/first/pallas_call | solution.py:25
  11.8 0.1 collective-permute-start
  11.9 5.0 %blocks_near.2.refs_1_ = f32[8,8,512]{2,1,0:T(8,128)} custom-call(s32[3]{0:T(128)} %pad_add_fusion.coords_ref, bf16[8,8,512]{2,1,0:T(8,128)(2,1)} %get-tuple-element.36.rows_ref, bf16[16,512,512]{2,1,0:T(8,128)(2,1)} %blocks_ref.7), custom_call_target="tpu_custom_call" | custom-call | flops 4000000000 | bytes 4194304 | tf_op jit(solution)/shard_map/blocks_near/pallas_call | solution.py:345
  16.9 0.6 copy-done.18
  17.5 5.0 %blocks_far.2 = f32[8,8,512]{2,1,0:T(8,128)} custom-call(s32[3]{0:T(128)} %pad_add_fusion.coords_ref, bf16[8,8,512]{2,1,0:T(8,128)(2,1)} %copy-done.18, bf16[16,512,512]{2,1,0:T(8,128)(2,1)} %blocks_ref.7), custom_call_target="tpu_custom_call" | custom-call | flops 4000000000 | bytes 4194304 | tf_op jit(solution)/shard_map/blocks_far/pallas_call | solution.py:345
  22.5 2.0 %collective-permute-start.1 = (f32[8,8,512]{2,1,0:T(8,128)}, f32[8,8,512]{2,1,0:T(8,128)S(1)}, u32[]{:S(2)}, u32[]{:S(2)}) collective-permute-start(f32[8,8,512]{2,1,0:T(8,128)} %blocks_far.2), channel_id=1, source_target_pairs={{0,16},{16,0},{1,17},{17,1},{2,18},{18,2},{3,19},{19,3},{4,20},{20... | collective-permute-start | bytes 393224 | tf_op jit(solution)/shard_map/ppermute | solution.py:291
  24.5 5.5 %near1.2 = (f32[8,256,128]{2,1,0:T(8,128)}, f32[256,128]{1,0:T(8,128)}) custom-call(s32[17]{0:T(128)} %get-tuple-element.34.refs_0_.table_ref, f32[8,8,512]{2,1,0:T(8,128)} %blocks_near.2.refs_1_, s32[64]{0:T(128)} %reshape.31.void_ref.refs_2_, f32[256,128]{1,0:T(8,128)} %bitcast.19), custom_call_target="tpu_custom_call" | custom-call | flops 2000000000 | bytes 1048576 | tf_op jit(solution)/shard_map/near1/pallas_call | solution.py:25
  30.0 0.7 copy-done.6
  30.7 5.8 %far2.1 = (f32[8,256,128]{2,1,0:T(8,128)}, f32[10,16,128]{2,1,0:T(8,128)}, f32[10,16,128]{2,1,0:T(8,128)}, f32[10,16,128]{2,1,0:T(8,128)}, f32[10,16,128]{2,1,0:...) custom-call(s32[17]{0:T(128)} %get-tuple-element.34.refs_0_.table_ref, s32[3]{0:T(128)} %pad_add_fusion.coords_ref, ...), custom_call_target="tpu_custom_call" | custom-call | bytes 1048576 | tf_op jit(solution)/shard_map/far2/pallas_call | solution.py:25
  36.5 1.2 collective-permute-start.2
  37.7 0.4 collective-permute-start.3
  38.1 5.7 %collective-permute-start.4 = (f32[10,16,128]{2,1,0:T(8,128)}, f32[10,16,128]{2,1,0:T(8,128)S(1)}, u32[]{:S(2)}, u32[]{:S(2)}) collective-permute-start(f32[10,16,128]{2,1,0:T(8,128)} %get-tuple-element.42), channel_id=1, source_target_pairs={{0,12},{4,8},{8,4},{12,0},{1,13},{5,9},{9,5},{13,1},{2,14},{6,10},... | collective-permute-start | bytes 245768 | tf_op jit(solution)/shard_map/ppermute | solution.py:282
  43.9 1.9 %collective-permute-start.5 = (f32[3,8,128]{2,1,0:T(8,128)}, f32[3,8,128]{2,1,0:T(8,128)S(1)}, u32[]{:S(2)}, u32[]{:S(2)}) collective-permute-start(f32[3,8,128]{2,1,0:T(8,128)} %get-tuple-element.43), channel_id=1, source_target_pairs={{0,1},{1,0},{2,3},{3,2},{4,5},{5,4},{6,7},{7,6},{8,9},{9,8},{10,11... | collective-permute-start | bytes 36872 | tf_op jit(solution)/shard_map/ppermute | solution.py:280
  45.8 2.5 %collective-permute-start.6 = (f32[3,8,128]{2,1,0:T(8,128)}, f32[3,8,128]{2,1,0:T(8,128)S(1)}, u32[]{:S(2)}, u32[]{:S(2)}) collective-permute-start(f32[3,8,128]{2,1,0:T(8,128)} %get-tuple-element.44), channel_id=1, source_target_pairs={{0,3},{1,2},{2,1},{3,0},{4,7},{5,6},{6,5},{7,4},{8,11},{9,10},{10,... | collective-permute-start | bytes 36872 | tf_op jit(solution)/shard_map/ppermute | solution.py:282
  48.3 3.2 %collective-permute-done.6.refs_5_ = f32[3,8,128]{2,1,0:T(8,128)S(1)} collective-permute-done((f32[3,8,128]{2,1,0:T(8,128)}, f32[3,8,128]{2,1,0:T(8,128)S(1)}, u32[]{:S(2)}, u32[]{:S(2)}) %collective-permute-start.6) | collective-permute-done | bytes 12320 | tf_op jit(solution)/shard_map/ppermute | solution.py:282
  51.5 0.5 copy-done.12
  52.1 0.0 copy-done.1
  52.1 0.0 copy-done.5
  52.2 11.5 %operate.1 = (f32[8,256,128]{2,1,0:T(8,128)}, f32[7,256,128]{2,1,0:T(8,128)}, f32[256,128]{1,0:T(8,128)}, f32[2,8,8,128]{3,2,1,0:T(8,128)}, bf16[8,8,512]{2,1,0:T(8,128)(2,1)}, /*index=5*/bf16[8,8,512]{2,1,0:T(8,128)(2,1)}) custom-call(s32[3]{0:T(128)} %pad_add_fusion.coords_ref, s32[17]{0:T(128)} %get-tuple-element.34.refs_0_.table_ref, ...), custom_call_target="tpu_custom_call" | custom-call | bytes 1048576 | tf_op jit(solution)/shard_map/operate/pallas_call | solution.py:25
  63.6 0.0 collective-permute-start.7
  63.7 5.0 %blocks_near.3.refs_1_ = f32[8,8,512]{2,1,0:T(8,128)} custom-call(s32[3]{0:T(128)} %pad_add_fusion.coords_ref, bf16[8,8,512]{2,1,0:T(8,128)(2,1)} %get-tuple-element.46.rows_ref, bf16[16,512,512]{2,1,0:T(8,128)(2,1)} %blocks_ref.7), custom_call_target="tpu_custom_call" | custom-call | flops 4000000000 | bytes 4194304 | tf_op jit(solution)/shard_map/blocks_near/pallas_call | solution.py:345
  68.7 0.6 copy-done.19
  69.3 5.0 %blocks_far.3 = f32[8,8,512]{2,1,0:T(8,128)} custom-call(s32[3]{0:T(128)} %pad_add_fusion.coords_ref, bf16[8,8,512]{2,1,0:T(8,128)(2,1)} %copy-done.19, bf16[16,512,512]{2,1,0:T(8,128)(2,1)} %blocks_ref.7), custom_call_target="tpu_custom_call" | custom-call | flops 4000000000 | bytes 4194304 | tf_op jit(solution)/shard_map/blocks_far/pallas_call | solution.py:345
  74.3 2.0 %collective-permute-start.8 = (f32[8,8,512]{2,1,0:T(8,128)}, f32[8,8,512]{2,1,0:T(8,128)S(1)}, u32[]{:S(2)}, u32[]{:S(2)}) collective-permute-start(f32[8,8,512]{2,1,0:T(8,128)} %blocks_far.3), channel_id=1, source_target_pairs={{0,16},{16,0},{1,17},{17,1},{2,18},{18,2},{3,19},{19,3},{4,20},{20... | collective-permute-start | bytes 393224 | tf_op jit(solution)/shard_map/ppermute | solution.py:291
  76.3 5.4 %near1.3.begun_ref = f32[8,256,128]{2,1,0:T(8,128)} custom-call(s32[17]{0:T(128)} %get-tuple-element.34.refs_0_.table_ref, f32[8,8,512]{2,1,0:T(8,128)} %blocks_near.3.refs_1_), custom_call_target="tpu_custom_call" | custom-call | flops 2000000000 | bytes 1048576 | tf_op jit(solution)/shard_map/near1/pallas_call | solution.py:25
  81.7 0.7 copy-done.7
  82.3 5.5 %far1.1 = (f32[8,256,128]{2,1,0:T(8,128)}, f32[9,16,128]{2,1,0:T(8,128)}, f32[9,16,128]{2,1,0:T(8,128)}, f32[9,16,128]{2,1,0:T(8,128)}, f32[9,16,128]{2,1,0:T(8,...) custom-call(s32[17]{0:T(128)} %get-tuple-element.34.refs_0_.table_ref, s32[3]{0:T(128)} %pad_add_fusion.coords_ref, ...), custom_call_target="tpu_custom_call" | custom-call | bytes 1048576 | tf_op jit(solution)/shard_map/far1/pallas_call | solution.py:25
  87.9 0.6 collective-permute-start.9
  88.5 3.9 %collective-permute-start.11 = (f32[9,16,128]{2,1,0:T(8,128)}, f32[9,16,128]{2,1,0:T(8,128)S(1)}, u32[]{:S(2)}, u32[]{:S(2)}) collective-permute-start(f32[9,16,128]{2,1,0:T(8,128)} %get-tuple-element.54), channel_id=1, source_target_pairs={{0,12},{4,8},{8,4},{12,0},{1,13},{5,9},{9,5},{13,1},{2,14},{6,10},... | collective-permute-start | bytes 221192 | tf_op jit(solution)/shard_map/ppermute | solution.py:282
  92.4 2.0 %collective-permute-start.13 = (f32[3,8,128]{2,1,0:T(8,128)}, f32[3,8,128]{2,1,0:T(8,128)S(1)}, u32[]{:S(2)}, u32[]{:S(2)}) collective-permute-start(f32[3,8,128]{2,1,0:T(8,128)} %get-tuple-element.56), channel_id=1, source_target_pairs={{0,3},{1,2},{2,1},{3,0},{4,7},{5,6},{6,5},{7,4},{8,11},{9,10},{10,... | collective-permute-start | bytes 36872 | tf_op jit(solution)/shard_map/ppermute | solution.py:282
  94.4 1.9 %collective-permute-done.12.refs_4_.refs_10_ = f32[3,8,128]{2,1,0:T(8,128)S(1)} collective-permute-done((f32[3,8,128]{2,1,0:T(8,128)}, f32[3,8,128]{2,1,0:T(8,128)S(1)}, u32[]{:S(2)}, u32[]{:S(2)}) %collective-permute-start.12) | collective-permute-done | bytes 12320 | tf_op jit(solution)/shard_map/ppermute | solution.py:280
  96.3 1.8 %collective-permute-done.13.refs_5_.refs_11_ = f32[3,8,128]{2,1,0:T(8,128)S(1)} collective-permute-done((f32[3,8,128]{2,1,0:T(8,128)}, f32[3,8,128]{2,1,0:T(8,128)S(1)}, u32[]{:S(2)}, u32[]{:S(2)}) %collective-permute-start.13) | collective-permute-done | bytes 12320 | tf_op jit(solution)/shard_map/ppermute | solution.py:282
  98.1 0.5 copy-done.9
  98.7 0.0 copy-done.2
  98.8 5.4 %dots.1 = f32[32,128]{1,0:T(8,128)} custom-call(s32[3]{0:T(128)} %pad_add_fusion.coords_ref, f32[8,256,128]{2,1,0:T(8,128)} %get-tuple-element.48.w_ref, f32[8,256,128]{2,1,0:T(8,128)} %get-tuple-element.49.q_ref, f32[8,256,128]{2,1,0:T(8,128)} %bitcast.18, f32[7,256,128]{2,1,0:T(8,128)} %get-tuple-element.50.weight_ref, ...), custom_call_target="tpu_custom_call" | custom-call | bytes 1048576 | tf_op jit(solution)/shard_map/dots/pallas_call | solution.py:25
  104.2 11.5 %all_to_all.22 = f32[32,1,128]{2,1,0:T(1,128)} all-to-all(f32[32,1,128]{2,1,0:T(1,128)} %bitcast.28), channel_id=1, replica_groups=mesh['span'=2,'height'=4,'depth'=4] {'span','height','depth'}, dimensions={0} | all-to-all | bytes 32768 | tf_op jit(solution)/shard_map/all_to_all | solution.py:298
  115.7 6.1 %solve.1 = (f32[8,256,128]{2,1,0:T(8,128)}, f32[256,128]{1,0:T(8,128)}, f32[32,128]{1,0:T(8,128)}, f32[1,16,128]{2,1,0:T(8,128)}, f32[1,16,128]{2,1,0:T(8,128)},...) custom-call(s32[3]{0:T(128)} %pad_add_fusion.coords_ref, ...), custom_call_target="tpu_custom_call" | custom-call | bytes 1048576 | tf_op jit(solution)/shard_map/solve/pallas_call | solution.py:25
  121.8 2.6 %all-to-all-start.1 = ((f32[32,1,128]{2,1,0:T(1,128)}), f32[32,1,128]{2,1,0:T(1,128)S(1)}, u32[]{:S(2)}, u32[]{:S(2)}) async-start(f32[32,1,128]{2,1,0:T(1,128)} %bitcast.29), calls=%async_computation.1 | async-start | bytes 32768 | tf_op jit(solution)/shard_map/all_to_all | solution.py:298
  124.3 1.7 %collective-permute-start.14 = (f32[1,16,128]{2,1,0:T(8,128)}, f32[1,16,128]{2,1,0:T(8,128)S(1)}, u32[]{:S(2)}, u32[]{:S(2)}) collective-permute-start(f32[1,16,128]{2,1,0:T(8,128)} %get-tuple-element.60), channel_id=1, source_target_pairs={{0,16},{16,0},{1,17},{17,1},{2,18},{18,2},{3,19},{19,3},{4,20},{20... | collective-permute-start | bytes 24584 | tf_op jit(solution)/shard_map/ppermute | solution.py:280
  126.1 1.6 %collective-permute-start.16 = (f32[1,16,128]{2,1,0:T(8,128)}, f32[1,16,128]{2,1,0:T(8,128)S(1)}, u32[]{:S(2)}, u32[]{:S(2)}) collective-permute-start(f32[1,16,128]{2,1,0:T(8,128)} %get-tuple-element.62), channel_id=1, source_target_pairs={{0,12},{4,8},{8,4},{12,0},{1,13},{5,9},{9,5},{13,1},{2,14},{6,10},... | collective-permute-start | bytes 24584 | tf_op jit(solution)/shard_map/ppermute | solution.py:282
  127.7 1.5 %collective-permute-start.17 = (f32[1,8,128]{2,1,0:T(8,128)}, f32[1,8,128]{2,1,0:T(8,128)S(1)}, u32[]{:S(2)}, u32[]{:S(2)}) collective-permute-start(f32[1,8,128]{2,1,0:T(8,128)} %get-tuple-element.63), channel_id=1, source_target_pairs={{0,1},{1,0},{2,3},{3,2},{4,5},{5,4},{6,7},{7,6},{8,9},{9,8},{10,11... | collective-permute-start | bytes 12296 | tf_op jit(solution)/shard_map/ppermute | solution.py:280
  129.2 2.4 %collective-permute-start.18 = (f32[1,8,128]{2,1,0:T(8,128)}, f32[1,8,128]{2,1,0:T(8,128)S(1)}, u32[]{:S(2)}, u32[]{:S(2)}) collective-permute-start(f32[1,8,128]{2,1,0:T(8,128)} %get-tuple-element.64), channel_id=1, source_target_pairs={{0,3},{1,2},{2,1},{3,0},{4,7},{5,6},{6,5},{7,4},{8,11},{9,10},{10,... | collective-permute-start | bytes 12296 | tf_op jit(solution)/shard_map/ppermute | solution.py:282
  131.6 3.2 %collective-permute-done.18.refs_5_ = f32[1,8,128]{2,1,0:T(8,128)S(1)} collective-permute-done((f32[1,8,128]{2,1,0:T(8,128)}, f32[1,8,128]{2,1,0:T(8,128)S(1)}, u32[]{:S(2)}, u32[]{:S(2)}) %collective-permute-start.18) | collective-permute-done | bytes 4128 | tf_op jit(solution)/shard_map/ppermute | solution.py:282
  134.9 0.5 copy-done.17
  135.5 3.3 %sweeps.1 = f32[256,128]{1,0:T(8,128)} custom-call(s32[3]{0:T(128)} %pad_add_fusion.coords_ref, f32[32,128]{1,0:T(8,128)} %bitcast.26, f32[256,128]{1,0:T(8,128)} %get-tuple-element.58.sens_ref, f32[256,128]{1,0:T(8,128)} %get-tuple-element.47.refs_0_.start_ref, f32[256,128]{1,0:T(8,128)} %bitcast.23, f32[1,16,128]{2,1,0:T(8,128)} %copy-done.13, ...), custom_call_target="tpu_custom_call" | custom-call | bytes 1048576 | tf_op jit(solution)/shard_map/sweeps/pallas_call | solution.py:25
  (49 shorter events, 0.3 us)
Async XLA Ops:
  11.8 5.1 %collective-permute-start = (bf16[8,8,512]{2,1,0:T(8,128)(2,1)}, bf16[8,8,512]{2,1,0:T(8,128)(2,1)S(1)}, u32[]{:S(2)}, u32[]{:S(2)}) collective-permute-start(bf16[8,8,512]{2,1,0:T(8,128)(2,1)} %get-tuple-element.35), channel_id=1, source_target_pairs={{0,16},{16,0},{1,17},{17,1},{2,18},{18,2},{3,19},{19,3},{4,20},{20... | collective-permute-start | bytes 196616 | tf_op jit(solution)/shard_map/ppermute | solution.py:291
  16.9 0.6 copy-start.18
  22.5 7.5 %collective-permute-start.1 = (f32[8,8,512]{2,1,0:T(8,128)}, f32[8,8,512]{2,1,0:T(8,128)S(1)}, u32[]{:S(2)}, u32[]{:S(2)}) collective-permute-start(f32[8,8,512]{2,1,0:T(8,128)} %blocks_far.2), channel_id=1, source_target_pairs={{0,16},{16,0},{1,17},{17,1},{2,18},{18,2},{3,19},{19,3},{4,20},{20... | collective-permute-start | bytes 393224 | tf_op jit(solution)/shard_map/ppermute | solution.py:291
  30.0 0.7 copy-start.6
  36.5 15.0 %collective-permute-start.2 = (f32[10,16,128]{2,1,0:T(8,128)}, f32[10,16,128]{2,1,0:T(8,128)S(1)}, u32[]{:S(2)}, u32[]{:S(2)}) collective-permute-start(f32[10,16,128]{2,1,0:T(8,128)} %get-tuple-element.40), channel_id=1, source_target_pairs={{0,16},{16,0},{1,17},{17,1},{2,18},{18,2},{3,19},{19,3},{4,20},{20... | collective-permute-start | bytes 245768 | tf_op jit(solution)/shard_map/ppermute | solution.py:280
  37.7 13.8 %collective-permute-start.3 = (f32[10,16,128]{2,1,0:T(8,128)}, f32[10,16,128]{2,1,0:T(8,128)S(1)}, u32[]{:S(2)}, u32[]{:S(2)}) collective-permute-start(f32[10,16,128]{2,1,0:T(8,128)} %get-tuple-element.41), channel_id=1, source_target_pairs={{0,4},{4,0},{8,12},{12,8},{1,5},{5,1},{9,13},{13,9},{2,6},{6,2},{1... | collective-permute-start | bytes 245768 | tf_op jit(solution)/shard_map/ppermute | solution.py:280
  38.1 13.4 %collective-permute-start.4 = (f32[10,16,128]{2,1,0:T(8,128)}, f32[10,16,128]{2,1,0:T(8,128)S(1)}, u32[]{:S(2)}, u32[]{:S(2)}) collective-permute-start(f32[10,16,128]{2,1,0:T(8,128)} %get-tuple-element.42), channel_id=1, source_target_pairs={{0,12},{4,8},{8,4},{12,0},{1,13},{5,9},{9,5},{13,1},{2,14},{6,10},... | collective-permute-start | bytes 245768 | tf_op jit(solution)/shard_map/ppermute | solution.py:282
  43.9 4.5 %collective-permute-start.5 = (f32[3,8,128]{2,1,0:T(8,128)}, f32[3,8,128]{2,1,0:T(8,128)S(1)}, u32[]{:S(2)}, u32[]{:S(2)}) collective-permute-start(f32[3,8,128]{2,1,0:T(8,128)} %get-tuple-element.43), channel_id=1, source_target_pairs={{0,1},{1,0},{2,3},{3,2},{4,5},{5,4},{6,7},{7,6},{8,9},{9,8},{10,11... | collective-permute-start | bytes 36872 | tf_op jit(solution)/shard_map/ppermute | solution.py:280
  45.8 5.7 %collective-permute-start.6 = (f32[3,8,128]{2,1,0:T(8,128)}, f32[3,8,128]{2,1,0:T(8,128)S(1)}, u32[]{:S(2)}, u32[]{:S(2)}) collective-permute-start(f32[3,8,128]{2,1,0:T(8,128)} %get-tuple-element.44), channel_id=1, source_target_pairs={{0,3},{1,2},{2,1},{3,0},{4,7},{5,6},{6,5},{7,4},{8,11},{9,10},{10,... | collective-permute-start | bytes 36872 | tf_op jit(solution)/shard_map/ppermute | solution.py:282
  48.3 3.2 %copy-start.11 = (f32[3,8,128]{2,1,0:T(8,128)}, f32[3,8,128]{2,1,0:T(8,128)S(1)}, u32[]{:S(2)}) copy-start(f32[3,8,128]{2,1,0:T(8,128)S(1)} %collective-permute-done.5.refs_4_) | copy-start | bytes 36868
  51.5 0.6 copy-start.12
  51.5 0.6 copy-start.1
  51.5 0.7 copy-start.4
  51.5 0.7 copy-start.5
  63.6 5.0 %collective-permute-start.7 = (bf16[8,8,512]{2,1,0:T(8,128)(2,1)}, bf16[8,8,512]{2,1,0:T(8,128)(2,1)S(1)}, u32[]{:S(2)}, u32[]{:S(2)}) collective-permute-start(bf16[8,8,512]{2,1,0:T(8,128)(2,1)} %get-tuple-element.45), channel_id=1, source_target_pairs={{0,16},{16,0},{1,17},{17,1},{2,18},{18,2},{3,19},{19,3},{4,20},{20... | collective-permute-start | bytes 196616 | tf_op jit(solution)/shard_map/ppermute | solution.py:291
  68.7 0.6 copy-start.19
  74.3 7.4 %collective-permute-start.8 = (f32[8,8,512]{2,1,0:T(8,128)}, f32[8,8,512]{2,1,0:T(8,128)S(1)}, u32[]{:S(2)}, u32[]{:S(2)}) collective-permute-start(f32[8,8,512]{2,1,0:T(8,128)} %blocks_far.3), channel_id=1, source_target_pairs={{0,16},{16,0},{1,17},{17,1},{2,18},{18,2},{3,19},{19,3},{4,20},{20... | collective-permute-start | bytes 393224 | tf_op jit(solution)/shard_map/ppermute | solution.py:291
  81.7 0.7 copy-start.7
  87.9 10.2 %collective-permute-start.9 = (f32[9,16,128]{2,1,0:T(8,128)}, f32[9,16,128]{2,1,0:T(8,128)S(1)}, u32[]{:S(2)}, u32[]{:S(2)}) collective-permute-start(f32[9,16,128]{2,1,0:T(8,128)} %get-tuple-element.52), channel_id=1, source_target_pairs={{0,16},{16,0},{1,17},{17,1},{2,18},{18,2},{3,19},{19,3},{4,20},{20... | collective-permute-start | bytes 221192 | tf_op jit(solution)/shard_map/ppermute | solution.py:280
  88.5 9.6 %collective-permute-start.10 = (f32[9,16,128]{2,1,0:T(8,128)}, f32[9,16,128]{2,1,0:T(8,128)S(1)}, u32[]{:S(2)}, u32[]{:S(2)}) collective-permute-start(f32[9,16,128]{2,1,0:T(8,128)} %get-tuple-element.53), channel_id=1, source_target_pairs={{0,4},{4,0},{8,12},{12,8},{1,5},{5,1},{9,13},{13,9},{2,6},{6,2},{1... | collective-permute-start | bytes 221192 | tf_op jit(solution)/shard_map/ppermute | solution.py:280
  88.5 9.6 %collective-permute-start.11 = (f32[9,16,128]{2,1,0:T(8,128)}, f32[9,16,128]{2,1,0:T(8,128)S(1)}, u32[]{:S(2)}, u32[]{:S(2)}) collective-permute-start(f32[9,16,128]{2,1,0:T(8,128)} %get-tuple-element.54), channel_id=1, source_target_pairs={{0,12},{4,8},{8,4},{12,0},{1,13},{5,9},{9,5},{13,1},{2,14},{6,10},... | collective-permute-start | bytes 221192 | tf_op jit(solution)/shard_map/ppermute | solution.py:282
  92.4 3.9 %collective-permute-start.12 = (f32[3,8,128]{2,1,0:T(8,128)}, f32[3,8,128]{2,1,0:T(8,128)S(1)}, u32[]{:S(2)}, u32[]{:S(2)}) collective-permute-start(f32[3,8,128]{2,1,0:T(8,128)} %get-tuple-element.55), channel_id=1, source_target_pairs={{0,1},{1,0},{2,3},{3,2},{4,5},{5,4},{6,7},{7,6},{8,9},{9,8},{10,11... | collective-permute-start | bytes 36872 | tf_op jit(solution)/shard_map/ppermute | solution.py:280
  92.4 5.7 %collective-permute-start.13 = (f32[3,8,128]{2,1,0:T(8,128)}, f32[3,8,128]{2,1,0:T(8,128)S(1)}, u32[]{:S(2)}, u32[]{:S(2)}) collective-permute-start(f32[3,8,128]{2,1,0:T(8,128)} %get-tuple-element.56), channel_id=1, source_target_pairs={{0,3},{1,2},{2,1},{3,0},{4,7},{5,6},{6,5},{7,4},{8,11},{9,10},{10,... | collective-permute-start | bytes 36872 | tf_op jit(solution)/shard_map/ppermute | solution.py:282
  96.3 1.8 %copy-start.8 = (f32[3,8,128]{2,1,0:T(8,128)}, f32[3,8,128]{2,1,0:T(8,128)S(1)}, u32[]{:S(2)}) copy-start(f32[3,8,128]{2,1,0:T(8,128)S(1)} %collective-permute-done.12.refs_4_.refs_10_) | copy-start | bytes 36868
  98.1 0.6 copy-start.9
  98.1 0.6 copy-start
  98.1 0.7 copy-start.2
  98.1 0.7 copy-start.3
  121.8 13.1 %all-to-all-start.1 = ((f32[32,1,128]{2,1,0:T(1,128)}), f32[32,1,128]{2,1,0:T(1,128)S(1)}, u32[]{:S(2)}, u32[]{:S(2)}) async-start(f32[32,1,128]{2,1,0:T(1,128)} %bitcast.29), calls=%async_computation.1 | async-start | bytes 32768 | tf_op jit(solution)/shard_map/all_to_all | solution.py:298
  124.3 10.5 %collective-permute-start.14 = (f32[1,16,128]{2,1,0:T(8,128)}, f32[1,16,128]{2,1,0:T(8,128)S(1)}, u32[]{:S(2)}, u32[]{:S(2)}) collective-permute-start(f32[1,16,128]{2,1,0:T(8,128)} %get-tuple-element.60), channel_id=1, source_target_pairs={{0,16},{16,0},{1,17},{17,1},{2,18},{18,2},{3,19},{19,3},{4,20},{20... | collective-permute-start | bytes 24584 | tf_op jit(solution)/shard_map/ppermute | solution.py:280
  126.1 8.8 %collective-permute-start.15 = (f32[1,16,128]{2,1,0:T(8,128)}, f32[1,16,128]{2,1,0:T(8,128)S(1)}, u32[]{:S(2)}, u32[]{:S(2)}) collective-permute-start(f32[1,16,128]{2,1,0:T(8,128)} %get-tuple-element.61), channel_id=1, source_target_pairs={{0,4},{4,0},{8,12},{12,8},{1,5},{5,1},{9,13},{13,9},{2,6},{6,2},{1... | collective-permute-start | bytes 24584 | tf_op jit(solution)/shard_map/ppermute | solution.py:280
  126.1 8.8 %collective-permute-start.16 = (f32[1,16,128]{2,1,0:T(8,128)}, f32[1,16,128]{2,1,0:T(8,128)S(1)}, u32[]{:S(2)}, u32[]{:S(2)}) collective-permute-start(f32[1,16,128]{2,1,0:T(8,128)} %get-tuple-element.62), channel_id=1, source_target_pairs={{0,12},{4,8},{8,4},{12,0},{1,13},{5,9},{9,5},{13,1},{2,14},{6,10},... | collective-permute-start | bytes 24584 | tf_op jit(solution)/shard_map/ppermute | solution.py:282
  127.7 4.0 %collective-permute-start.17 = (f32[1,8,128]{2,1,0:T(8,128)}, f32[1,8,128]{2,1,0:T(8,128)S(1)}, u32[]{:S(2)}, u32[]{:S(2)}) collective-permute-start(f32[1,8,128]{2,1,0:T(8,128)} %get-tuple-element.63), channel_id=1, source_target_pairs={{0,1},{1,0},{2,3},{3,2},{4,5},{5,4},{6,7},{7,6},{8,9},{9,8},{10,11... | collective-permute-start | bytes 12296 | tf_op jit(solution)/shard_map/ppermute | solution.py:280
  129.2 5.6 %collective-permute-start.18 = (f32[1,8,128]{2,1,0:T(8,128)}, f32[1,8,128]{2,1,0:T(8,128)S(1)}, u32[]{:S(2)}, u32[]{:S(2)}) collective-permute-start(f32[1,8,128]{2,1,0:T(8,128)} %get-tuple-element.64), channel_id=1, source_target_pairs={{0,3},{1,2},{2,1},{3,0},{4,7},{5,6},{6,5},{7,4},{8,11},{9,10},{10,... | collective-permute-start | bytes 12296 | tf_op jit(solution)/shard_map/ppermute | solution.py:282
  131.6 3.3 %copy-start.16 = (f32[1,8,128]{2,1,0:T(8,128)}, f32[1,8,128]{2,1,0:T(8,128)S(1)}, u32[]{:S(2)}) copy-start(f32[1,8,128]{2,1,0:T(8,128)S(1)} %collective-permute-done.17.refs_4_) | copy-start | bytes 12292
  134.8 0.6 copy-start.17
  134.8 0.6 copy-start.13
  134.8 0.6 copy-start.14
  134.8 0.6 copy-start.15
  134.9 0.6 copy-start.10

commit v2 on v0

v2 whole, which is shorter than its diff:
```python
import jax
import jax.numpy as jnp
from jax import lax
from jax.experimental import pallas as pl
from jax.experimental.pallas import tpu as pltpu
from jax.sharding import PartitionSpec as P

BE = 8
AXES = ("span", "height", "depth")

void_stiffness = 0.001
spring_rate = 0.05
time_step = 0.5
interface_weight = 0.5
epsilon_peak = 1e-06
inverse = 1.0 / (1.0 / time_step + 6.0 * interface_weight)

F32 = jnp.float32
BF16 = jnp.bfloat16
VM = pl.BlockSpec(memory_space=pltpu.VMEM)
SM = pl.BlockSpec(memory_space=pltpu.SMEM)


HB = pl.BlockSpec(memory_space=pltpu.HBM)


def call(kernel, ins, outs, scratch=(), flops=0, aliases=None, name=None):
    arrays = [
        pltpu.with_memory_space_constraint(array, pltpu.SMEM if spec is SM else pltpu.VMEM)
        for array, spec in ins
    ]
    return pl.pallas_call(
        kernel,
        in_specs=[spec for _, spec in ins],
        out_specs=[spec for _, _, spec in outs],
        out_shape=[
            jax.ShapeDtypeStruct(shape, dtype)
            if spec is HB
            else (pltpu.SMEM if spec is SM else pltpu.VMEM)(shape, dtype)
            for shape, dtype, spec in outs
        ],
        scratch_shapes=list(scratch),
        input_output_aliases=aliases or {},
        cost_estimate=pl.CostEstimate(flops=flops, bytes_accessed=1 << 20, transcendentals=0),
        compiler_params=pltpu.CompilerParams(vmem_limit_bytes=12 << 20),
        name=name,
    )(*arrays)


def slots_fit(bricks, cells):
    return all(n * BE == size for n, size in zip(bricks, cells))


def local(load, phase, void, owner, precond):
    loads, X, Y, Z = load.shape
    bricks_x, bricks_y, bricks_z = void.shape
    bricks = bricks_x * bricks_y * bricks_z
    T = Y // BE
    tiles = X * T
    cells = BE**3
    lanes = Z
    wide = -(-(loads + 2) // 8) * 8
    assert lanes == 128 and BE == 8 and loads == 8 and slots_fit(void.shape, phase.shape)
    sizes = [lax.axis_size(axis) for axis in AXES]
    assert all(size % 2 == 0 for size in sizes)
    spans = sizes[0]
    devices = sizes[0] * sizes[1] * sizes[2]
    slots = precond.shape[0]
    cap = slots // spans
    bits = 32 // spans
    assert cap < (1 << min(bits, 8)) and bits >= 2
    remote = (spans - 1) * cap

    has_b = [size > 2 for size in sizes]
    faces = [(d, b) for d in range(3) for b in range(2) if b == 0 or has_b[d]]
    load_f = load.reshape(loads, X * Y, Z)
    phase_f = phase.reshape(X * Y, Z)

    def iotas():
        return (
            lax.broadcasted_iota(jnp.int32, (8, lanes), 0),
            lax.broadcasted_iota(jnp.int32, (8, lanes), 1),
        )

    def row(x, t):
        start = x * Y + t * 8
        return pl.ds(start if isinstance(start, int) else pl.multiple_of(start, 8), 8)

    def brick_at(n):
        m = jnp.maximum(n, 0)
        return m // (bricks_y * bricks_z), (m // bricks_z) % bricks_y, m % bricks_z

    def spread_of(rows, columns, row_part, column_part):
        r = lax.broadcasted_iota(jnp.int32, (rows, columns), 0)
        c = lax.broadcasted_iota(jnp.int32, (rows, columns), 1)
        same = jnp.logical_and(row_part(r) == column_part(c), (r & 7) == (c & 7))
        return jnp.where(same, 1.0, 0.0).astype(BF16)

    def halves(value):
        high = value.astype(BF16).astype(F32)
        return high, value - high

    def gather_bricks(source, table, base, count, out):
        sub, lane = iotas()
        keep = ((lane >> 3) & 7) == sub
        fold = spread_of(2 * lanes, lanes, lambda r: r >> 7, lambda c: c >> 6)
        pick = jnp.where(
            lax.broadcasted_iota(jnp.int32, (loads, loads * 8), 1) >> 3
            == lax.broadcasted_iota(jnp.int32, (loads, loads * 8), 0),
            1.0,
            0.0,
        ).astype(BF16)

        def one(r, carry):
            n = table[base + r]
            bx, by, bz = brick_at(n)
            inside = (lane >> 3) == bz

            @pl.when(n >= 0)
            def _():
                rows = []
                for q in range(4):
                    for l in range(loads):
                        pair = [
                            jnp.where(inside, source[l, row(bx * 8 + 2 * q + h, by), :], 0.0)
                            for h in range(2)
                        ]
                        rows.append(jnp.concatenate(pair, axis=1))
                stacked = jnp.concatenate(rows, axis=0).astype(BF16)
                folded = jnp.dot(stacked, fold, preferred_element_type=F32)
                columns = []
                for q in range(4):
                    columns.append(
                        jnp.concatenate(
                            [
                                jnp.where(
                                    keep,
                                    folded[(q * loads + l) * 8 : (q * loads + l + 1) * 8],
                                    0.0,
                                )
                                for l in range(loads)
                            ],
                            axis=0,
                        )
                    )
                cells_of = jnp.concatenate(columns, axis=1).astype(BF16)
                out[r] = jnp.dot(pick, cells_of, preferred_element_type=F32).astype(BF16)

            @pl.when(n < 0)
            def _():
                out[r] = jnp.zeros((loads, cells), BF16)

            return carry

        lax.fori_loop(0, count, one, 0)

    def scatter_bricks(field, table, base, count, images, split):
        sub, lane = iotas()
        keep = ((lane >> 3) & 7) == sub
        unfold = spread_of(
            2 * lanes, 2 * lanes, lambda r: (r >> 6) & 1, lambda c: c >> 7
        )

        def one(r, carry):
            n = table[base + r]
            bx, by, bz = brick_at(n)
            inside = (lane >> 3) == bz

            @pl.when(n >= 0)
            def _():
                high, low = halves(images[r])
                split[0] = high
                split[1] = low
                rows = []
                for q in range(4):
                    for l in range(loads):
                        pair = [
                            jnp.where(
                                keep,
                                jnp.broadcast_to(
                                    split[part, pl.ds(l, 1), pl.ds(q * lanes, lanes)],
                                    (8, lanes),
                                ),
                                0.0,
                            )
                            for part in range(2)
                        ]
                        rows.append(jnp.concatenate(pair, axis=1))
                stacked = jnp.concatenate(rows, axis=0).astype(BF16)
                spread = jnp.dot(stacked, unfold, preferred_element_type=F32)
                for q in range(4):
                    for l in range(loads):
                        for h in range(2):
                            at = row(bx * 8 + 2 * q + h, by)
                            tile = spread[
                                (q * loads + l) * 8 : (q * loads + l + 1) * 8,
                                h * lanes : (h + 1) * lanes,
                            ]
                            field[l, at, :] = jnp.where(inside, tile, field[l, at, :])

            return carry

        lax.fori_loop(0, count, one, 0)

    def face_position(coords_ref, d, b, extent):
        high = (coords_ref[d] + b) % 2 == 0
        return jnp.where(high, extent - 1, 0)

    def face_open(coords_ref, d, b):
        if b == 0:
            return jnp.bool_(True)
        return jnp.logical_and(coords_ref[d] > 0, coords_ref[d] < sizes[d] - 1)

    def put_faces(read_tile, read_rows, coords_ref, index, outs):
        for (d, b), out in zip(faces, outs):
            if d == 0:
                x = face_position(coords_ref, d, b, X)
                for t in range(T):
                    out[index, pl.ds(t * 8, 8), :] = read_tile(x, t)
            elif d == 1:
                out[index] = read_rows(face_position(coords_ref, d, b, Y))

    def depth_faces(fields, coords_ref, count):
        rows_i = lax.broadcasted_iota(jnp.int32, (2 * count, lanes), 0)
        lanes_i = lax.broadcasted_iota(jnp.int32, (2 * count, lanes), 1)
        z = [face_position(coords_ref, 2, b, lanes) for b in range(2)]
        total = jnp.zeros((2 * count, X * Y), F32)
        for f, field in enumerate(fields):
            hit = [
                jnp.logical_and(rows_i == b * count + f, lanes_i == z[b]) for b in range(2)
            ]
            pick = jnp.where(jnp.logical_or(*hit), 1.0, 0.0).astype(BF16)
            for part in halves(field()):
                total = total + lax.dot_general(
                    pick,
                    part.astype(BF16),
                    (((1,), (1,)), ((), ())),
                    preferred_element_type=F32,
                )
        return total

    def turned_depth(values):
        return jnp.transpose(jnp.concatenate(halves(values), axis=0)).astype(BF16)

    def spread_depth(turned, coords_ref, rows_of):
        total = turned.shape[1] // 2
        rows_i = lax.broadcasted_iota(jnp.int32, (2 * total, lanes), 0) % total
        lanes_i = lax.broadcasted_iota(jnp.int32, (2 * total, lanes), 1)
        hit = [
            jnp.logical_and(
                rows_i == rows_of[b], lanes_i == face_position(coords_ref, 2, b, lanes)
            )
            for b in range(2)
        ]
        place = jnp.where(jnp.logical_or(*hit), 1.0, 0.0).astype(BF16)
        return jnp.dot(turned, place, preferred_element_type=F32)

    def plain_neighbours(read, x, t):
        sub, lane = iotas()
        tile = read(x, t)
        x_low = read(jnp.maximum(x - 1, 0), t)
        x_high = read(jnp.minimum(x + 1, X - 1), t)
        before = jnp.where(sub == 7, read(x, t - 1), tile) if t > 0 else tile
        after = jnp.where(sub == 0, read(x, t + 1), tile) if t < T - 1 else tile
        return tile, (
            x_low,
            x_high,
            pltpu.roll(before, 1, 0),
            pltpu.roll(after, 7, 0),
            pltpu.roll(tile, 1, 1),
            pltpu.roll(tile, lanes - 1, 1),
        )

    def valid(x, t):
        sub, lane = iotas()
        yes = sub >= 0
        return (
            jnp.logical_and(yes, x > 0),
            jnp.logical_and(yes, x < X - 1),
            sub > 0 if t == 0 else yes,
            sub < 7 if t == T - 1 else yes,
            lane > 0,
            lane < lanes - 1,
        )

    def over_rows(body):
        def one(x, carry):
            body(x)
            return carry

        lax.fori_loop(0, X, one, 0)

    def face_shape(d, count):
        return ((count, Y, Z), (count, X, Z), (-(-count // 8) * 8, X * Y))[d]

    def face_outs(count):
        return [(face_shape(d, count), F32, VM) for d, _ in faces]

    def exchange(payload):
        received = []
        for (d, b), part in zip(faces, payload):
            n = sizes[d]
            swap = [(i, (i + 1 if (i + b) % 2 == 0 else i - 1) % n) for i in range(n)]
            with jax.named_scope("swap" + str(d) + str(b)):
                received.append(lax.ppermute(part, AXES[d], swap))
        return received

    def to_owners(rows, sign):
        parts = []
        for shift in range(1, spans):
            part = rows[(shift - 1) * cap : shift * cap]
            parts.append(
                lax.ppermute(
                    part, "span", [(i, (i + sign * shift) % spans) for i in range(spans)]
                )
            )
        return parts[0] if spans == 2 else jnp.concatenate(parts, axis=0)

    def everyone(partial):
        return lax.all_to_all(partial, AXES, split_axis=0, concat_axis=0, tiled=True)

    field_shape = (loads, X * Y, Z)
    plain_shape = (X * Y, Z)
    face_count = len(faces)

    def first_kernel(
        void_hbm, owner_hbm, load_hbm, phase_hbm, blocks_hbm,
        table_ref, far_ref, load_ref, phase_ref, blocks_ref, coords_ref, void_ref,
        owner_ref, arrived,
    ):
        copies = [
            pltpu.make_async_copy(source, target, arrived.at[i])
            for i, (source, target) in enumerate(
                (
                    (void_hbm, void_ref),
                    (owner_hbm, owner_ref),
                    (load_hbm, load_ref),
                    (phase_hbm, phase_ref),
                    (blocks_hbm, blocks_ref),
                )
            )
        ]
        for copy in copies:
            copy.start()
        for d, axis in enumerate(AXES):
            coords_ref[d] = lax.axis_index(axis)
        me = lax.axis_index("span")
        for i in range(slots + 1):
            table_ref[i] = -1
        copies[0].wait()
        copies[1].wait()
        used = jnp.int32(0)
        for n in range(bricks):
            at = (n // (bricks_y * bricks_z), n // bricks_z % bricks_y, n % bricks_z)
            solid = 1 - void_ref[at]
            relative = jnp.where(solid == 1, (owner_ref[at] + spans - me) % spans, 0)
            shift = relative * bits
            rank = lax.shift_right_logical(used, shift) & ((1 << bits) - 1)
            index = jnp.where(solid == 1, relative * cap + rank, slots)
            table_ref[index] = n
            used = used + lax.shift_left(solid, shift)
        copies[2].wait()
        gather_bricks(load_ref, table_ref, cap, remote, far_ref)
        copies[3].wait()
        copies[4].wait()

    table, far, load_f, phase_f, precond, coords, void = pl.pallas_call(
        first_kernel,
        in_specs=[HB] * 5,
        out_specs=[SM, VM, VM, VM, VM, SM, SM],
        out_shape=[
            pltpu.SMEM((slots + 1,), jnp.int32),
            pltpu.VMEM((remote, loads, cells), BF16),
            pltpu.VMEM(field_shape, F32),
            pltpu.VMEM(plain_shape, F32),
            pltpu.VMEM(precond.shape, BF16),
            pltpu.SMEM((3,), jnp.int32),
            pltpu.SMEM(void.shape, jnp.int32),
        ],
        scratch_shapes=[
            pltpu.SMEM(owner.shape, jnp.int32),
            pltpu.SemaphoreType.DMA((5,)),
        ],
        compiler_params=pltpu.CompilerParams(vmem_limit_bytes=12 << 20),
        name="first",
    )(*[
        pltpu.with_memory_space_constraint(a, pltpu.HBM)
        for a in (void, owner, load_f, phase_f, precond)
    ])

    def near_kernel(
        table_ref, coords_ref, source_ref, blocks_ref, field_ref, rows_ref, image_ref, split
    ):
        field_ref[...] = jnp.zeros(field_ref.shape, F32)
        gather_bricks(source_ref, table_ref, 0, cap, rows_ref)
        for r in range(cap):
            image_ref[r] = jnp.dot(
                rows_ref[r], blocks_ref[coords_ref[0] * cap + r], preferred_element_type=F32
            )
        scatter_bricks(field_ref, table_ref, 0, cap, image_ref, split)

    def near_part(source):
        return call(
            near_kernel,
            [(table, SM), (coords, SM), (source, VM), (precond, VM)],
            [(field_shape, F32, VM)],
            scratch=[
                pltpu.VMEM((cap, loads, cells), BF16),
                pltpu.VMEM((cap, loads, cells), F32),
                pltpu.VMEM((2, loads, cells), F32),
            ],
            flops=8000000000,
            name="near",
        )[0]

    def blocks_kernel(coords_ref, rows_ref, blocks_ref, out_ref):
        for r in range(remote):
            slot = (coords_ref[0] + spans - (r // cap + 1)) % spans * cap + r % cap
            out_ref[r] = jnp.dot(rows_ref[r], blocks_ref[slot], preferred_element_type=F32)

    def far_part(rows):
        (image,) = call(
            blocks_kernel,
            [(coords, SM), (to_owners(rows, 1), VM), (precond, VM)],
            [((remote, loads, cells), F32, VM)],
            name="blocks",
        )
        return to_owners(image, -1)

    def faces_kernel(extra):
        def kernel(table_ref, coords_ref, image_ref, begun_ref, *refs):
            extras = refs[:extra]
            field_ref = refs[extra]
            outs = refs[extra + 1 : extra + 1 + face_count]
            split = refs[extra + 1 + face_count]
            scatter_bricks(field_ref, table_ref, cap, remote, image_ref, split)
            for l in range(loads):
                put_faces(
                    lambda x, t: field_ref[l, row(x, t), :],
                    lambda y: field_ref[l, pl.ds(y, X, stride=Y), :],
                    coords_ref, l, outs,
                )
            for e in range(extra):
                ref = extras[e]
                put_faces(
                    lambda x, t: ref[row(x, t), :],
                    lambda y: ref[pl.ds(y, X, stride=Y), :],
                    coords_ref, loads + e, outs,
                )
            count = outs[-1].shape[0]
            depth = depth_faces(
                [lambda l=l: field_ref[l] for l in range(loads)]
                + [lambda e=e: extras[e][...] for e in range(extra)],
                coords_ref, count,
            )
            for (d, b), out in zip(faces, outs):
                if d == 2:
                    out[...] = depth[b * count : (b + 1) * count]

        return kernel

    def to_field(begun, image, extras):
        result = call(
            faces_kernel(len(extras)),
            [(table, SM), (coords, SM), (image, VM), (begun, VM)]
            + [(e, VM) for e in extras],
            [(field_shape, F32, VM)] + face_outs(loads + len(extras)),
            scratch=[pltpu.VMEM((2, loads, cells), F32)],
            aliases={3: 0},
            name="faces" + str(len(extras)),
        )
        return result[0], result[1:], exchange(result[1:])

    def stiffness_kernel(void_ref, phase_ref, ks_ref):
        sub, lane = iotas()
        for bx in range(bricks_x):
            for by in range(bricks_y):
                mask = jnp.zeros((8, lanes), F32)
                for bz in range(bricks_z):
                    solid = 1 - void_ref[bx, by, bz]
                    mask = jnp.where((lane >> 3) == bz, solid.astype(F32), mask)
                for i in range(BE):
                    at = row(bx * BE + i, by)
                    p = phase_ref[at, :]
                    stiffness = void_stiffness + (1.0 - void_stiffness) * (p * p * p)
                    ks_ref[at, :] = mask * stiffness

    far_image = far_part(far)
    begun = near_part(load_f)
    (ks,) = call(
        stiffness_kernel, [(void, SM), (phase_f, VM)], [(plain_shape, F32, VM)],
        flops=2000000000, name="stiffness",
    )
    z_field, z_sent, z_halo = to_field(begun, far_image, [ks, phase_f])

    def joined(mine, other):
        both = jnp.logical_and(mine > 0.0, other > 0.0)
        return jnp.where(both, 0.5 * (mine + other), 0.0)

    def inner_kernel(z_ref, load_ref, ks_ref, phase_ref, q_ref, weight_ref, start_ref, dots_ref):
        dots_ref[...] = jnp.zeros(dots_ref.shape, F32)

        def body(x):
            for t in range(T):
                at = row(x, t)
                inside = valid(x, t)
                ks_tile, ks_near = plain_neighbours(lambda x, t: ks_ref[row(x, t), :], x, t)
                p, p_near = plain_neighbours(lambda x, t: phase_ref[row(x, t), :], x, t)
                around = jnp.zeros((8, lanes), F32)
                for d in range(6):
                    around = around + jnp.where(inside[d], p_near[d], 0.0)
                start_ref[at, :] = (
                    p / time_step
                    - 0.5 * p * (1.0 - p) * (1.0 - 2.0 * p)
                    + interface_weight * around
                ) * inverse
                total = jnp.where(ks_tile > 0.0, spring_rate, 0.0)
                weights = []
                for d in range(6):
                    weight = jnp.where(inside[d], joined(ks_tile, ks_near[d]), 0.0)
                    weights.append(weight)
                    weight_ref[d, at, :] = weight
                    total = total + weight
                for l in range(loads):
                    tile, near_tiles = plain_neighbours(
                        lambda x, t: z_ref[l, row(x, t), :], x, t
                    )
                    image = total * tile
                    for d in range(6):
                        image = image - weights[d] * near_tiles[d]
                    q_ref[l, at, :] = image
                    dots_ref[0, l] += load_ref[l, at, :] * tile
                    dots_ref[1, l] += image * tile

        over_rows(body)

    q_inner, weights, start_inner, dots = call(
        inner_kernel,
        [(z_field, VM), (load_f, VM), (ks, VM), (phase_f, VM)],
        [
            (field_shape, F32, VM),
            ((6, X * Y, Z), F32, VM),
            (plain_shape, F32, VM),
            ((2, loads, 8, Z), F32, VM),
        ],
        flops=8000000000,
        name="inner",
    )

    def face_weight(coords_ref, d, b, sent, received, at):
        other = jnp.where(face_open(coords_ref, d, b), received[at], 0.0)
        return joined(sent[at], other)

    def row_pieces(d):
        return [pl.ds(i * 8, 8) for i in range((Y if d == 0 else X) // 8)]

    def edges_kernel(coords_ref, table_ref, q_in, start_in, dots_in, *refs):
        sent = refs[:face_count]
        received = refs[face_count : 2 * face_count]
        q_ref, start_ref, dots_ref, far_ref = refs[2 * face_count : 2 * face_count + 4]
        moved = refs[2 * face_count + 4 :]
        scale = interface_weight * inverse
        for (d, b), mine, other, shift in zip(faces, sent, received, moved):
            is_open = face_open(coords_ref, d, b)
            if d < 2:
                for at in row_pieces(d):
                    weight = face_weight(coords_ref, d, b, mine, other, (loads, at))
                    for l in range(loads):
                        tile = mine[l, at, :]
                        change = weight * (tile - other[l, at, :])
                        shift[l, at, :] = change
                        dots_ref[1, l] += tile * change
                    shift[loads, at, :] = jnp.where(
                        is_open, scale * other[loads + 1, at, :], 0.0
                    )
                for l in range(loads + 1):
                    target = q_ref.at[l] if l < loads else start_ref
                    if d == 0:
                        x = face_position(coords_ref, d, b, X)
                        for t in range(T):
                            target[row(x, t), :] += shift[l, pl.ds(t * 8, 8), :]
                    else:
                        y = face_position(coords_ref, d, b, Y)
                        at = pl.ds(y, X, stride=Y)
                        target[at, :] = target[at, :] + shift[l]
            else:
                weight = face_weight(coords_ref, d, b, mine, other, (pl.ds(loads, 1), slice(None)))
                tile = mine[pl.ds(0, loads), :]
                change = weight * (tile - other[pl.ds(0, loads), :])
                shift[pl.ds(0, loads), :] = change
                shift[pl.ds(loads, 8), :] = jnp.zeros((8, X * Y), F32)
                shift[pl.ds(loads, 1), :] = jnp.where(
                    is_open, scale * other[pl.ds(loads + 1, 1), :], 0.0
                )
                product = tile * change
                eight = sum(
                    product[:, i * lanes : (i + 1) * lanes] for i in range(X * Y // lanes)
                )
                sub, lane = iotas()
                for l in range(loads):
                    dots_ref[1, l] += jnp.where(sub == l, eight, 0.0)
        depth = [shift for (d, _), shift in zip(faces, moved) if d == 2]
        turned = turned_depth(jnp.concatenate([ref[...] for ref in depth], axis=0))
        for l in range(loads + 1):
            target = q_ref.at[l] if l < loads else start_ref
            target[...] = target[...] + spread_depth(
                turned, coords_ref, (l, depth[0].shape[0] + l)
            )
        gather_bricks(q_ref, table_ref, cap, remote, far_ref)

    q_field, start, dots, far = call(
        edges_kernel,
        [(coords, SM), (table, SM), (q_inner, VM), (start_inner, VM), (dots, VM)]
        + [(a, VM) for a in z_sent]
        + [(a, VM) for a in z_halo],
        [
            (field_shape, F32, VM),
            (plain_shape, F32, VM),
            ((2, loads, 8, Z), F32, VM),
            ((remote, loads, cells), BF16, VM),
        ],
        scratch=[pltpu.VMEM(face_shape(d, loads + 1), F32) for d, _ in faces],
        aliases={2: 0, 3: 1, 4: 2},
        name="edges",
    )

    far_image = far_part(far)
    w_field, w_sent, w_halo = to_field(near_part(q_field), far_image, [start])

    products = 5

    def more_kernel(w_ref, q_ref, load_ref, weight_ref, ks_ref, more_ref):
        more_ref[...] = jnp.zeros(more_ref.shape, F32)

        def body(x):
            for t in range(T):
                at = row(x, t)
                weights = [weight_ref[d, at, :] for d in (1, 3, 5)]
                spring = jnp.where(ks_ref[at, :] > 0.0, spring_rate, 0.0)
                for l in range(loads):
                    tile, near_tiles = plain_neighbours(
                        lambda x, t: w_ref[l, row(x, t), :], x, t
                    )
                    energy = spring * tile * tile
                    for weight, d in zip(weights, (1, 3, 5)):
                        gap = tile - near_tiles[d]
                        energy = energy + weight * gap * gap
                    more_ref[0, l] += load_ref[l, at, :] * tile
                    more_ref[1, l] += q_ref[l, at, :] * tile
                    more_ref[2, l] += energy

        over_rows(body)

    (more,) = call(
        more_kernel,
        [(w_field, VM), (q_field, VM), (load_f, VM), (weights, VM), (ks, VM)],
        [((3, loads, 8, Z), F32, VM)],
        flops=8000000000,
        name="more",
    )

    def energy_kernel(z_ref, w_ref, ks_ref, energy_ref):
        def body(x):
            for t in range(T):
                at = row(x, t)
                inside = valid(x, t)
                ks_tile, ks_near = plain_neighbours(lambda x, t: ks_ref[row(x, t), :], x, t)
                solid = [
                    jnp.where(
                        jnp.logical_and(inside[d], joined(ks_tile, ks_near[d]) > 0.0), 1.0, 0.0
                    )
                    for d in range(6)
                ]
                for l in range(loads):
                    z, z_near = plain_neighbours(lambda x, t: z_ref[l, row(x, t), :], x, t)
                    w, w_near = plain_neighbours(lambda x, t: w_ref[l, row(x, t), :], x, t)
                    zz = zw = ww = jnp.zeros((8, lanes), F32)
                    for d in range(6):
                        gap_z = solid[d] * (z - z_near[d])
                        gap_w = solid[d] * (w - w_near[d])
                        zz = zz + gap_z * gap_z
                        zw = zw + gap_z * gap_w
                        ww = ww + gap_w * gap_w
                    energy_ref[0, l, at, :] = zz
                    energy_ref[1, l, at, :] = zw
                    energy_ref[2, l, at, :] = ww

        over_rows(body)

    (energies,) = call(
        energy_kernel,
        [(z_field, VM), (w_field, VM), (ks, VM)],
        [((3,) + field_shape, F32, VM)],
        flops=16000000000,
        name="energy",
    )

    def total_kernel(coords_ref, dots_ref, more_in, _, *refs):
        z_mine = refs[:face_count]
        z_other = refs[face_count : 2 * face_count]
        w_mine = refs[2 * face_count : 3 * face_count]
        w_other = refs[3 * face_count : 4 * face_count]
        out_ref, more_ref = refs[4 * face_count : 4 * face_count + 2]
        gaps = refs[4 * face_count + 2 : 5 * face_count + 2]
        starts = refs[5 * face_count + 2 :]
        sub, lane = iotas()
        for (d, b), z_a, z_b, w_a, w_b, gap, begin in zip(
            faces, z_mine, z_other, w_mine, w_other, gaps, starts
        ):
            if d < 2:
                begin[...] = w_b[loads]
                for at in row_pieces(d):
                    weight = face_weight(coords_ref, d, b, z_a, z_b, (loads, at))
                    solid = weight > 0.0
                    for l in range(loads):
                        tile = w_a[l, at, :]
                        between = tile - w_b[l, at, :]
                        more_ref[2, l] += weight * tile * between
                        gap[1, l, at, :] = jnp.where(solid, between, 0.0)
                        gap[0, l, at, :] = jnp.where(
                            solid, z_a[l, at, :] - z_b[l, at, :], 0.0
                        )
            else:
                begin[...] = w_b[pl.ds(loads, 8), :]
                weight = face_weight(coords_ref, d, b, z_a, z_b, (pl.ds(loads, 1), slice(None)))
                solid = weight > 0.0
                tile = w_a[pl.ds(0, loads), :]
                between = tile - w_b[pl.ds(0, loads), :]
                product = weight * tile * between
                gap[1] = jnp.where(solid, between, 0.0)
                gap[0] = jnp.where(
                    solid, z_a[pl.ds(0, loads), :] - z_b[pl.ds(0, loads), :], 0.0
                )
                eight = sum(
                    product[:, i * lanes : (i + 1) * lanes] for i in range(X * Y // lanes)
                )
                for l in range(loads):
                    more_ref[2, l] += jnp.where(sub == l, eight, 0.0)
        result = jnp.zeros((1, lanes), F32)
        lane1 = lane[:1]
        for k in range(products):
            for l in range(loads):
                part = dots_ref[k, l] if k < 2 else more_ref[k - 2, l]
                value = jnp.sum(jnp.sum(part, axis=0, keepdims=True), axis=1, keepdims=True)
                result = jnp.where(lane1 == k * loads + l, value, result)
        out_ref[...] = jnp.broadcast_to(result, (devices, lanes))

    partial, _, *kept = call(
        total_kernel,
        [(coords, SM), (dots, VM), (more, VM), (energies, VM)]
        + [(a, VM) for part in (z_sent, z_halo, w_sent, w_halo) for a in part],
        [((devices, lanes), F32, VM), ((3, loads, 8, Z), F32, VM)]
        + [((2,) + face_shape(d, loads), F32, VM) for d, _ in faces]
        + [((8, X * Y) if d == 2 else face_shape(d, 1)[1:], F32, VM) for d, _ in faces],
        aliases={2: 1},
        name="total",
    )
    gaps, start_halo = kept[:face_count], kept[face_count:]
    sums = everyone(partial)

    def device_beyond(coords_ref, d, b):
        place = [coords_ref[i] for i in range(3)]
        step = jnp.where((place[d] + b) % 2 == 0, 1, -1)
        place[d] = jnp.where(face_open(coords_ref, d, b), place[d] + step, place[d])
        return (place[0] * sizes[1] + place[1]) * sizes[2] + place[2]

    face_rows = max(X, Y)
    message = face_rows + 1

    def solve_kernel(
        coords_ref, sums_ref, energy_ref, phase_ref, z_ref, w_ref, *refs
    ):
        gap_refs = refs[:face_count]
        (sens_ref, out_ref, x_hbm, sens_hbm, x_ref, plain_ref, held_ref, written) = refs[
            face_count:
        ]
        sub, lane = iotas()
        total = jnp.broadcast_to(
            jnp.sum(sums_ref[...], axis=0, keepdims=True), (8, lanes)
        )
        bz, zq, bw, qw, ws = [
            pltpu.roll(total, (lanes - k * loads) % lanes, 1) for k in range(products)
        ]
        alpha = bz / zq
        bz_next = bz - alpha * (bw + zq) + alpha * alpha * qw
        beta = bz_next / bz
        grow = 1.0 + beta
        curvature = grow * grow * zq - 2.0 * grow * alpha * qw + alpha * alpha * ws
        alpha_next = bz_next / curvature
        for_z = alpha + alpha_next * grow
        for_w = -alpha_next * alpha
        c_z = [jnp.broadcast_to(for_z[0:1, l : l + 1], (8, lanes)) for l in range(loads)]
        c_w = [jnp.broadcast_to(for_w[0:1, l : l + 1], (8, lanes)) for l in range(loads)]
        c_zz = [c * c for c in c_z]
        c_zw = [2.0 * a * c for a, c in zip(c_z, c_w)]
        c_ww = [c * c for c in c_w]
        writes = []
        for l in range(loads):

            def mix(i, carry, l=l):
                at = pl.ds(pl.multiple_of(i * 8, 8), 8)
                x_ref[l, at, :] = c_z[l] * z_ref[l, at, :] + c_w[l] * w_ref[l, at, :]
                return carry

            lax.fori_loop(0, tiles, mix, 0, unroll=8)
            writes.append(
                pltpu.make_async_copy(x_ref.at[l], x_hbm.at[l], written.at[l])
            )
            writes[-1].start()

        def body(x):
            for t in range(T):
                at = row(x, t)
                energy = jnp.zeros((8, lanes), F32)
                for l in range(loads):
                    energy = energy + c_zz[l] * energy_ref[0, l, at, :]
                    energy = energy + c_zw[l] * energy_ref[1, l, at, :]
                    energy = energy + c_ww[l] * energy_ref[2, l, at, :]
                plain_ref[at, :] = energy

        over_rows(body)
        held_ref[...] = jnp.zeros(held_ref.shape, F32)
        for (d, b), between in zip(faces, gap_refs):
            if d < 2:
                pieces = []
                for at in row_pieces(d):
                    energy = jnp.zeros((8, lanes), F32)
                    for l in range(loads):
                        gap = c_z[l] * between[0, l, at, :] + c_w[l] * between[1, l, at, :]
                        energy = energy + gap * gap
                    pieces.append(energy)
                if d == 0:
                    x = face_position(coords_ref, d, b, X)
                    for t in range(T):
                        plain_ref[row(x, t), :] += pieces[t]
                else:
                    at = pl.ds(face_position(coords_ref, d, b, Y), X, stride=Y)
                    plain_ref[at, :] = plain_ref[at, :] + jnp.concatenate(pieces, axis=0)
            else:
                by_z = jnp.concatenate([c[0:1, :1] for c in c_z], axis=0)
                by_w = jnp.concatenate([c[0:1, :1] for c in c_w], axis=0)
                gap = by_z * between[0] + by_w * between[1]
                held_ref[pl.ds(b, 1), :] = jnp.sum(gap * gap, axis=0, keepdims=True)
        spread = spread_depth(turned_depth(held_ref[...]), coords_ref, (0, 1))
        energy = plain_ref[...] + spread
        p = phase_ref[...]
        negative = 1.5 * (1.0 - void_stiffness) * (p * p) * energy
        sens_ref[...] = -negative
        writes.append(pltpu.make_async_copy(sens_ref, sens_hbm, written.at[loads]))
        writes[-1].start()
        peak = jnp.max(jnp.max(negative, axis=0, keepdims=True), axis=1, keepdims=True)
        peak = jnp.broadcast_to(peak, (1, lanes))
        high, rest = halves(peak)
        middle, low = halves(rest)
        lane1 = lane[:1]
        tail = jnp.where(lane1 == 0, high, jnp.where(lane1 == 1, middle, low)).astype(BF16)
        for i in range(devices):
            out_ref[i, pl.ds(face_rows, 1), :] = tail
        depth = depth_faces([lambda: sens_ref[...]], coords_ref, 8)
        for d, b in faces:
            @pl.when(face_open(coords_ref, d, b))
            def _(d=d, b=b):
                to = device_beyond(coords_ref, d, b)
                if d == 0:
                    x = face_position(coords_ref, d, b, X)
                    value = sens_ref[pl.ds(pl.multiple_of(x * Y, 8), Y), :]
                elif d == 1:
                    value = sens_ref[
                        pl.ds(face_position(coords_ref, d, b, Y), X, stride=Y), :
                    ]
                else:
                    value = jnp.concatenate(
                        [
                            depth[b * 8 : b * 8 + 1, i * lanes : (i + 1) * lanes]
                            for i in range(X * Y // lanes)
                        ],
                        axis=0,
                    )
                out_ref[to, pl.ds(0, value.shape[0]), :] = value.astype(BF16)
        for write in writes:
            write.wait()

    sens_field, outgoing, displacement, sensitivity = call(
        solve_kernel,
        [
            (coords, SM), (sums, VM), (energies, VM), (phase_f, VM), (z_field, VM),
            (w_field, VM),
        ]
        + [(a, VM) for a in gaps],
        [
            (plain_shape, F32, VM),
            ((devices, message, lanes), BF16, VM),
            (field_shape, F32, HB),
            (plain_shape, F32, HB),
        ],
        scratch=[
            pltpu.VMEM(field_shape, F32),
            pltpu.VMEM(plain_shape, F32),
            pltpu.VMEM((8, X * Y), F32),
            pltpu.SemaphoreType.DMA((loads + 1,)),
        ],
        name="solve",
    )
    incoming = everyone(outgoing)

    def sweep_kernel(coords_ref, in_ref, sens_ref, start_ref, phase_ref, *refs):
        starts = refs[:face_count]
        out_hbm, out_ref, once_ref, held_ref, written = refs[face_count:]
        sub, lane = iotas()
        tails = in_ref[:, pl.ds(face_rows, 1), :].astype(F32)
        tails = tails.reshape(devices, lanes)
        peaks = tails + pltpu.roll(tails, lanes - 1, 1) + pltpu.roll(tails, lanes - 2, 1)
        peak = jnp.max(peaks, axis=0, keepdims=True)[:, :1]
        scale1 = jnp.broadcast_to(1.0 / (peak + epsilon_peak), (1, lanes))
        scale = jnp.broadcast_to(scale1, (8, lanes))
        for i in range(tiles):
            at = pl.ds(i * 8, 8)
            once_ref[at, :] = start_ref[at, :] - inverse * (sens_ref[at, :] * scale)

        def body(x):
            for t in range(T):
                at = row(x, t)
                inside = valid(x, t)
                _, near_tiles = plain_neighbours(lambda x, t: once_ref[row(x, t), :], x, t)
                around = jnp.zeros((8, lanes), F32)
                for d in range(6):
                    around = around + jnp.where(inside[d], near_tiles[d], 0.0)
                p = phase_ref[at, :]
                drive = (
                    p / time_step
                    - 0.5 * p * (1.0 - p) * (1.0 - 2.0 * p)
                    - sens_ref[at, :] * scale
                )
                out_ref[at, :] = (drive + interface_weight * around) * inverse

        over_rows(body)
        held_ref[...] = jnp.zeros(held_ref.shape, F32)
        factor = interface_weight * inverse
        for (d, b), start_b in zip(faces, starts):
            is_open = face_open(coords_ref, d, b)
            source = device_beyond(coords_ref, d, b)
            sent = in_ref[source].astype(F32)
            if d < 2:
                value = start_b[...] - (inverse * scale1) * sent[: (Y if d == 0 else X)]
                value = jnp.where(is_open, factor * value, 0.0)
                if d == 0:
                    x = face_position(coords_ref, d, b, X)
                    at = pl.ds(pl.multiple_of(x * Y, 8), Y)
                else:
                    at = pl.ds(face_position(coords_ref, d, b, Y), X, stride=Y)
                out_ref[at, :] = out_ref[at, :] + value
            else:
                for i in range(X * Y // lanes):
                    at = pl.ds(i * lanes, lanes)
                    value = start_b[pl.ds(0, 1), at] - (inverse * scale1) * sent[i : i + 1]
                    held_ref[pl.ds(b, 1), at] = jnp.where(is_open, factor * value, 0.0)
        out_ref[...] = out_ref[...] + spread_depth(
            turned_depth(held_ref[...]), coords_ref, (0, 1)
        )
        write = pltpu.make_async_copy(out_ref, out_hbm, written)
        write.start()
        write.wait()

    (phase_next,) = call(
        sweep_kernel,
        [(coords, SM), (incoming, VM), (sens_field, VM), (start, VM), (phase_f, VM)]
        + [(a, VM) for a in start_halo],
        [(plain_shape, F32, HB)],
        scratch=[
            pltpu.VMEM(plain_shape, F32),
            pltpu.VMEM(plain_shape, F32),
            pltpu.VMEM((8, X * Y), F32),
            pltpu.SemaphoreType.DMA,
        ],
        name="sweeps",
    )
    return (
        displacement.reshape(load.shape),
        sensitivity.reshape(phase.shape),
        phase_next.reshape(phase.shape),
    )


def solution(mesh):
    return jax.shard_map(
        local,
        mesh=mesh,
        in_specs=(
            P(None, "span", "height", "depth"),
            P("span", "height", "depth"),
            P("span", "height", "depth"),
            P("span", "height", "depth"),
            P(("span", "height", "depth"), None, None),
        ),
        out_specs=(
            P(None, "span", "height", "depth"),
            P("span", "height", "depth"),
            P("span", "height", "depth"),
        ),
        check_vma=False,
    )
```

time: 471 us -> 79.8 us (0.17)
  the two profiles are of different devices: /device:TPU:14 before, /device:TPU:0 now
where the time goes in v2:
time: 79.8 us; the launch traced here: 79.5 us
  Pallas kernels  23.2 us (29%)
  blocking collectives  22.3 us (28%)
  starting transfers between devices  19.2 us (24%)
  waiting for transfers between devices  14 us (18%)
    all_to_all x2, blocking collectives, everyone(): lax.all_to_all(partial, AXES, split_axis=0, concat_axis=0, tiled=True)  22.3 us
    pallas_call x14, Pallas kernels, call(): pl.pallas_call(kernel, in_specs=[spec for _, spec in ins], out_specs=[spe...  19.4 us
    ppermute x10, starting transfers between devices, exchange(): received.append(lax.ppermute(part, AXES[d], swap))  13.1 us
    ppermute x4, waiting for transfers between devices, to_owners(): lax.ppermute(part, 'span', [(i, (i + sign * shift) % spans) for i in rang...  13.1 us
    ppermute x4, starting transfers between devices, to_owners(): lax.ppermute(part, 'span', [(i, (i + sign * shift) % spans) for i in rang...  6.02 us
    pallas_call x1, Pallas kernels, local(): pl.pallas_call(first_kernel, in_specs=[HB] * 5, out_specs=[SM, VM, VM, VM...  3.81 us
  transfers between devices with their start and end apart: 14, of which 5 were waited for; matrix products, arithmetic and copies ran while one was open for 0% of the time, Pallas kernels for 10%

profile of v2, /device:TPU:0, one launch (start us, length us, event | category | flops | bytes accessed | tf_op | source)
XLA Modules:
  0.0 79.5 jit_solution(11143735484253436776)
XLA Ops:
  0.6 3.8 %first.1 = (s32[17]{0:T(128)S(4)}, bf16[8,8,512]{2,1,0:T(8,128)(2,1)S(1)}, f32[8,256,128]{2,1,0:T(8,128)S(1)}, f32[256,128]{1,0:T(8,128)S(1)}, bf16[16,512,512]{...) custom-call(s32[2,2,16]{2,1,0:T(2,128)} %void_hbm.1, s32[2,2,16]{2,1,0:T(2,128)} %owner_hbm.1, ...), custom_call_target="tpu_custom_call" | custom-call | tf_op jit(solution)/shard_map/first/pallas_call | solution.py:367
  4.4 3.1 %collective-permute-start = (bf16[8,8,512]{2,1,0:T(8,128)(2,1)S(1)}, bf16[8,8,512]{2,1,0:T(8,128)(2,1)S(1)}, u32[]{:S(2)}, u32[]{:S(2)}) collective-permute-start(bf16[8,8,512]{2,1,0:T(8,128)(2,1)S(1)} %get-tuple-element.47), channel_id=1, source_target_pairs={{0,16},{16,0},{1,17},{17,1},{2,18},{18,2},{3,19},{19,3},{4,20},{20... | collective-permute-start | bytes 196616 | tf_op jit(solution)/shard_map/ppermute | solution.py:313
  7.5 1.0 %near.2.begun_ref = f32[8,256,128]{2,1,0:T(8,128)S(1)} custom-call(s32[17]{0:T(128)S(4)} %get-tuple-element.46.table_ref, s32[3]{0:T(128)S(4)} %get-tuple-element.45.coords_ref, f32[8,256,128]{2,1,0:T(8,128)S(1)} %get-tuple-element.49.source_ref.load_ref, bf16[16,512,512]{2,1,0:T(8,128)(2,1)S(1)} %get-tuple-element.48.blocks_ref), custom_call_target="tpu_custom_call" | custom-call | flops 8000000000 | bytes 1048576 | tf_op jit(solution)/shard_map/near/pallas_call | solution.py:32
  8.6 1.2 %collective-permute-done.rows_ref = bf16[8,8,512]{2,1,0:T(8,128)(2,1)S(1)} collective-permute-done((bf16[8,8,512]{2,1,0:T(8,128)(2,1)S(1)}, bf16[8,8,512]{2,1,0:T(8,128)(2,1)S(1)}, u32[]{:S(2)}, u32[]{:S(2)}) %collective-permute-start) | collective-permute-done | bytes 65568 | tf_op jit(solution)/shard_map/ppermute | solution.py:313
  9.8 0.6 blocks.2
  10.4 2.6 %collective-permute-start.1 = (f32[8,8,512]{2,1,0:T(8,128)S(1)}, f32[8,8,512]{2,1,0:T(8,128)S(1)}, u32[]{:S(2)}, u32[]{:S(2)}) collective-permute-start(f32[8,8,512]{2,1,0:T(8,128)S(1)} %blocks.2), channel_id=1, source_target_pairs={{0,16},{16,0},{1,17},{17,1},{2,18},{18,2},{3,19},{19,3},{4,20},{20... | collective-permute-start | bytes 393224 | tf_op jit(solution)/shard_map/ppermute | solution.py:313
  13.0 0.1 stiffness.1.refs_0_.ks_ref
  13.1 3.0 %collective-permute-done.1.image_ref = f32[8,8,512]{2,1,0:T(8,128)S(1)} collective-permute-done((f32[8,8,512]{2,1,0:T(8,128)S(1)}, f32[8,8,512]{2,1,0:T(8,128)S(1)}, u32[]{:S(2)}, u32[]{:S(2)}) %collective-permute-start.1) | collective-permute-done | bytes 131104 | tf_op jit(solution)/shard_map/ppermute | solution.py:313
  16.0 1.7 %faces2.1 = (f32[8,256,128]{2,1,0:T(8,128)S(1)}, f32[10,16,128]{2,1,0:T(8,128)S(1)}, f32[10,16,128]{2,1,0:T(8,128)S(1)}, f32[10,16,128]{2,1,0:T(8,128)S(1)}, f32...) custom-call(s32[17]{0:T(128)S(4)} %get-tuple-element.46.table_ref, ...), custom_call_target="tpu_custom_call", output_to_operand_aliasing={{0}: (3, {})} | custom-call | bytes 1048576 | tf_op jit(solution)/shard_map/faces2/pallas_call | solution.py:32
  17.8 2.1 %collective-permute-start.5 = (f32[16,256]{1,0:T(8,128)S(1)}, f32[16,256]{1,0:T(8,128)S(1)}, u32[]{:S(2)}, u32[]{:S(2)}) collective-permute-start(f32[16,256]{1,0:T(8,128)S(1)} %get-tuple-element.59.refs_3_), channel_id=1, source_target_pairs={{0,1},{1,0},{2,3},{3,2},{4,5},{5,4},{6,7},{7,6},{8,9},{9,8},{10,11... | collective-permute-start | bytes 49160 | tf_op jit(solution)/shard_map/swap20/ppermute | solution.py:305
  19.9 4.4 %collective-permute-start.6 = (f32[16,256]{1,0:T(8,128)S(1)}, f32[16,256]{1,0:T(8,128)S(1)}, u32[]{:S(2)}, u32[]{:S(2)}) collective-permute-start(f32[16,256]{1,0:T(8,128)S(1)} %get-tuple-element.60.refs_4_), channel_id=1, source_target_pairs={{0,3},{1,2},{2,1},{3,0},{4,7},{5,6},{6,5},{7,4},{8,11},{9,10},{10,... | collective-permute-start | bytes 49160 | tf_op jit(solution)/shard_map/swap21/ppermute | solution.py:305
  24.3 0.0 collective-permute-start.2
  24.3 0.0 collective-permute-start.3
  24.3 1.6 %collective-permute-start.4 = (f32[10,16,128]{2,1,0:T(8,128)S(1)}, f32[10,16,128]{2,1,0:T(8,128)S(1)}, u32[]{:S(2)}, u32[]{:S(2)}) collective-permute-start(f32[10,16,128]{2,1,0:T(8,128)S(1)} %get-tuple-element.58.refs_2_), channel_id=1, source_target_pairs={{0,12},{4,8},{8,4},{12,0},{1,13},{5,9},{9,5},{13,1},{2,14},{6,10},... | collective-permute-start | bytes 245768 | tf_op jit(solution)/shard_map/swap11/ppermute | solution.py:305
  25.9 1.8 %inner.1 = (f32[8,256,128]{2,1,0:T(8,128)S(1)}, f32[6,256,128]{2,1,0:T(8,128)S(1)}, f32[256,128]{1,0:T(8,128)S(1)}, f32[2,8,8,128]{3,2,1,0:T(8,128)S(1)}) custom-call(f32[8,256,128]{2,1,0:T(8,128)S(1)} %get-tuple-element.52.z_ref, f32[8,256,128]{2,1,0:T(8,128)S(1)} %get-tuple-element.49.source_ref.load_ref, f32[256,128]{1,0:T(8,128)S(1)} %stiffness.1.refs_0_.ks_ref, ...), custom_call_target="tpu_custom_call" | custom-call | flops 8000000000 | bytes 1048576 | tf_op jit(solution)/shard_map/inner/pallas_call | solution.py:32
  27.7 0.0 collective-permute-done.5.refs_8_
  27.8 0.0 collective-permute-done.6.refs_9_
  27.8 1.0 %collective-permute-done.2.refs_5_ = f32[10,16,128]{2,1,0:T(8,128)S(1)} collective-permute-done((f32[10,16,128]{2,1,0:T(8,128)S(1)}, f32[10,16,128]{2,1,0:T(8,128)S(1)}, u32[]{:S(2)}, u32[]{:S(2)}) %collective-permute-start.2) | collective-permute-done | bytes 81952 | tf_op jit(solution)/shard_map/swap00/ppermute | solution.py:305
  28.7 0.0 collective-permute-done.3.refs_6_
  28.7 0.0 collective-permute-done.4.refs_7_
  28.8 2.1 %edges.1 = (f32[8,256,128]{2,1,0:T(8,128)S(1)}, f32[256,128]{1,0:T(8,128)S(1)}, f32[2,8,8,128]{3,2,1,0:T(8,128)S(1)}, bf16[8,8,512]{2,1,0:T(8,128)(2,1)S(1)}) custom-call(s32[3]{0:T(128)S(4)} %get-tuple-element.45.coords_ref, s32[17]{0:T(128)S(4)} %get-tuple-element.46.table_ref, ...), custom_call_target="tpu_custom_call", output_to_operand_aliasing={{0}: (2, {}), {1}: (3, {}), {2}: (4, {})} | custom-call | bytes 1048576 | tf_op jit(solution)/shard_map/edges/pallas_call | solution.py:32
  30.8 0.4 collective-permute-start.7
  31.2 4.4 %collective-permute-done.7.rows_ref = bf16[8,8,512]{2,1,0:T(8,128)(2,1)S(1)} collective-permute-done((bf16[8,8,512]{2,1,0:T(8,128)(2,1)S(1)}, bf16[8,8,512]{2,1,0:T(8,128)(2,1)S(1)}, u32[]{:S(2)}, u32[]{:S(2)}) %collective-permute-start.7) | collective-permute-done | bytes 65568 | tf_op jit(solution)/shard_map/ppermute | solution.py:313
  35.6 0.6 blocks.3
  36.3 0.0 collective-permute-start.8
  36.3 1.1 %near.3.begun_ref = f32[8,256,128]{2,1,0:T(8,128)S(1)} custom-call(s32[17]{0:T(128)S(4)} %get-tuple-element.46.table_ref, s32[3]{0:T(128)S(4)} %get-tuple-element.45.coords_ref, f32[8,256,128]{2,1,0:T(8,128)S(1)} %get-tuple-element.63.source_ref.q_ref, bf16[16,512,512]{2,1,0:T(8,128)(2,1)S(1)} %get-tuple-element.48.blocks_ref), custom_call_target="tpu_custom_call" | custom-call | flops 8000000000 | bytes 1048576 | tf_op jit(solution)/shard_map/near/pallas_call | solution.py:32
  37.4 4.5 %collective-permute-done.8.image_ref = f32[8,8,512]{2,1,0:T(8,128)S(1)} collective-permute-done((f32[8,8,512]{2,1,0:T(8,128)S(1)}, f32[8,8,512]{2,1,0:T(8,128)S(1)}, u32[]{:S(2)}, u32[]{:S(2)}) %collective-permute-start.8) | collective-permute-done | bytes 131104 | tf_op jit(solution)/shard_map/ppermute | solution.py:313
  41.8 1.7 %faces1.1 = (f32[8,256,128]{2,1,0:T(8,128)S(1)}, f32[9,16,128]{2,1,0:T(8,128)S(1)}, f32[9,16,128]{2,1,0:T(8,128)S(1)}, f32[9,16,128]{2,1,0:T(8,128)S(1)}, f32[16,256]{1,0:T(8,128)S(1)}, /*index=5*/f32[16,256]{1,0:T(8,128)S(1)}) custom-call(s32[17]{0:T(128)S(4)} %get-tuple-element.46.table_ref, ...), custom_call_target="tpu_custom_call", output_to_operand_aliasing={{0}: (3, {})} | custom-call | bytes 1048576 | tf_op jit(solution)/shard_map/faces1/pallas_call | solution.py:32
  43.5 0.7 collective-permute-start.12
  44.2 2.0 %collective-permute-start.13 = (f32[16,256]{1,0:T(8,128)S(1)}, f32[16,256]{1,0:T(8,128)S(1)}, u32[]{:S(2)}, u32[]{:S(2)}) collective-permute-start(f32[16,256]{1,0:T(8,128)S(1)} %get-tuple-element.71.refs_14_), channel_id=1, source_target_pairs={{0,3},{1,2},{2,1},{3,0},{4,7},{5,6},{6,5},{7,4},{8,11},{9,10},{10,... | collective-permute-start | bytes 49160 | tf_op jit(solution)/shard_map/swap21/ppermute | solution.py:305
  46.2 0.1 collective-permute-start.9
  46.3 0.0 collective-permute-start.10
  46.3 2.2 %collective-permute-start.11 = (f32[9,16,128]{2,1,0:T(8,128)S(1)}, f32[9,16,128]{2,1,0:T(8,128)S(1)}, u32[]{:S(2)}, u32[]{:S(2)}) collective-permute-start(f32[9,16,128]{2,1,0:T(8,128)S(1)} %get-tuple-element.69.refs_12_), channel_id=1, source_target_pairs={{0,12},{4,8},{8,4},{12,0},{1,13},{5,9},{9,5},{13,1},{2,14},{6,10},... | collective-permute-start | bytes 221192 | tf_op jit(solution)/shard_map/swap11/ppermute | solution.py:305
  48.5 2.5 %energy.1._.energy_ref = f32[3,8,256,128]{3,2,1,0:T(8,128)S(1)} custom-call(f32[8,256,128]{2,1,0:T(8,128)S(1)} %get-tuple-element.52.z_ref, f32[8,256,128]{2,1,0:T(8,128)S(1)} %get-tuple-element.65.w_ref, f32[256,128]{1,0:T(8,128)S(1)} %stiffness.1.refs_0_.ks_ref), custom_call_target="tpu_custom_call" | custom-call | flops 16000000000 | bytes 1048576 | tf_op jit(solution)/shard_map/energy/pallas_call | solution.py:32
  51.0 1.5 %more.1.more_in = f32[3,8,8,128]{3,2,1,0:T(8,128)S(1)} custom-call(f32[8,256,128]{2,1,0:T(8,128)S(1)} %get-tuple-element.65.w_ref, f32[8,256,128]{2,1,0:T(8,128)S(1)} %get-tuple-element.63.source_ref.q_ref, f32[8,256,128]{2,1,0:T(8,128)S(1)} %get-tuple-element.49.source_ref.load_ref, f32[6,256,128]{2,1,0:T(8,128)S(1)} %get-tuple-element.66.weight_ref, ...), custom_call_target="tpu_custom_call" | custom-call | flops 8000000000 | bytes 1048576 | tf_op jit(solution)/shard_map/more/pallas_call | solution.py:32
  52.5 0.0 collective-permute-done.12.refs_18_
  52.6 0.0 collective-permute-done.13.refs_19_
  52.6 0.0 collective-permute-done.9.refs_15_
  52.6 0.0 collective-permute-done.10.refs_16_
  52.6 0.0 collective-permute-done.11.refs_17_
  52.6 0.2 total.1
  52.8 11.3 %all_to_all.16 = f32[32,1,128]{2,1,0:T(1,128)S(1)} all-to-all(f32[32,1,128]{2,1,0:T(1,128)S(1)} %bitcast.10), channel_id=1, replica_groups=mesh['span'=2,'height'=4,'depth'=4] {'span','height','depth'}, dimensions={0} | all-to-all | bytes 32768 | tf_op jit(solution)/shard_map/all_to_all | solution.py:320
  64.1 2.0 %solve.1 = (f32[256,128]{1,0:T(8,128)S(1)}, bf16[32,17,128]{2,1,0:T(8,128)(2,1)S(1)}, f32[8,256,128]{2,1,0:T(8,128)}, f32[256,128]{1,0:T(8,128)}) custom-call(s32[3]{0:T(128)S(4)} %get-tuple-element.45.coords_ref, f32[32,128]{1,0:T(8,128)S(1)} %bitcast.9, f32[3,8,256,128]{3,2,1,0:T(8,128)S(1)} %energy.1._.energy_ref, ...), custom_call_target="tpu_custom_call" | custom-call | bytes 1048576 | tf_op jit(solution)/shard_map/solve/pallas_call | solution.py:32
  66.2 11.0 %all_to_all.17.in_ref = bf16[32,17,128]{2,1,0:T(8,128)(2,1)S(1)} all-to-all(bf16[32,17,128]{2,1,0:T(8,128)(2,1)S(1)} %get-tuple-element.80), channel_id=1, replica_groups=mesh['span'=2,'height'=4,'depth'=4] {'span','height','depth'}, dimensions={0} | all-to-all | bytes 278528 | tf_op jit(solution)/shard_map/all_to_all | solution.py:320
  77.2 2.4 %sweeps.1 = f32[256,128]{1,0:T(8,128)} custom-call(s32[3]{0:T(128)S(4)} %get-tuple-element.45.coords_ref, bf16[32,17,128]{2,1,0:T(8,128)(2,1)S(1)} %all_to_all.17.in_ref, f32[256,128]{1,0:T(8,128)S(1)} %get-tuple-element.81.sens_ref, f32[256,128]{1,0:T(8,128)S(1)} %get-tuple-element.64.refs_0_.start_ref, f32[256,128]{1,0:T(8,128)S(1)} %get-tuple-element.51.phase_ref.refs_1_, ...), custom_call_target="tpu_custom_call" | custom-call | bytes 1048576 | tf_op jit(solution)/shard_map/sweeps/pallas_call | solution.py:32
Async XLA Ops:
  4.4 5.3 %collective-permute-start = (bf16[8,8,512]{2,1,0:T(8,128)(2,1)S(1)}, bf16[8,8,512]{2,1,0:T(8,128)(2,1)S(1)}, u32[]{:S(2)}, u32[]{:S(2)}) collective-permute-start(bf16[8,8,512]{2,1,0:T(8,128)(2,1)S(1)} %get-tuple-element.47), channel_id=1, source_target_pairs={{0,16},{16,0},{1,17},{17,1},{2,18},{18,2},{3,19},{19,3},{4,20},{20... | collective-permute-start | bytes 196616 | tf_op jit(solution)/shard_map/ppermute | solution.py:313
  10.4 5.6 %collective-permute-start.1 = (f32[8,8,512]{2,1,0:T(8,128)S(1)}, f32[8,8,512]{2,1,0:T(8,128)S(1)}, u32[]{:S(2)}, u32[]{:S(2)}) collective-permute-start(f32[8,8,512]{2,1,0:T(8,128)S(1)} %blocks.2), channel_id=1, source_target_pairs={{0,16},{16,0},{1,17},{17,1},{2,18},{18,2},{3,19},{19,3},{4,20},{20... | collective-permute-start | bytes 393224 | tf_op jit(solution)/shard_map/ppermute | solution.py:313
  17.8 10.0 %collective-permute-start.5 = (f32[16,256]{1,0:T(8,128)S(1)}, f32[16,256]{1,0:T(8,128)S(1)}, u32[]{:S(2)}, u32[]{:S(2)}) collective-permute-start(f32[16,256]{1,0:T(8,128)S(1)} %get-tuple-element.59.refs_3_), channel_id=1, source_target_pairs={{0,1},{1,0},{2,3},{3,2},{4,5},{5,4},{6,7},{7,6},{8,9},{9,8},{10,11... | collective-permute-start | bytes 49160 | tf_op jit(solution)/shard_map/swap20/ppermute | solution.py:305
  19.9 7.9 %collective-permute-start.6 = (f32[16,256]{1,0:T(8,128)S(1)}, f32[16,256]{1,0:T(8,128)S(1)}, u32[]{:S(2)}, u32[]{:S(2)}) collective-permute-start(f32[16,256]{1,0:T(8,128)S(1)} %get-tuple-element.60.refs_4_), channel_id=1, source_target_pairs={{0,3},{1,2},{2,1},{3,0},{4,7},{5,6},{6,5},{7,4},{8,11},{9,10},{10,... | collective-permute-start | bytes 49160 | tf_op jit(solution)/shard_map/swap21/ppermute | solution.py:305
  24.3 4.4 %collective-permute-start.2 = (f32[10,16,128]{2,1,0:T(8,128)S(1)}, f32[10,16,128]{2,1,0:T(8,128)S(1)}, u32[]{:S(2)}, u32[]{:S(2)}) collective-permute-start(f32[10,16,128]{2,1,0:T(8,128)S(1)} %get-tuple-element.56.refs_0_), channel_id=1, source_target_pairs={{0,16},{16,0},{1,17},{17,1},{2,18},{18,2},{3,19},{19,3},{4,20},{20... | collective-permute-start | bytes 245768 | tf_op jit(solution)/shard_map/swap00/ppermute | solution.py:305
  24.3 4.4 %collective-permute-start.3 = (f32[10,16,128]{2,1,0:T(8,128)S(1)}, f32[10,16,128]{2,1,0:T(8,128)S(1)}, u32[]{:S(2)}, u32[]{:S(2)}) collective-permute-start(f32[10,16,128]{2,1,0:T(8,128)S(1)} %get-tuple-element.57.refs_1_), channel_id=1, source_target_pairs={{0,4},{4,0},{8,12},{12,8},{1,5},{5,1},{9,13},{13,9},{2,6},{6,2},{1... | collective-permute-start | bytes 245768 | tf_op jit(solution)/shard_map/swap10/ppermute | solution.py:305
  24.3 4.4 %collective-permute-start.4 = (f32[10,16,128]{2,1,0:T(8,128)S(1)}, f32[10,16,128]{2,1,0:T(8,128)S(1)}, u32[]{:S(2)}, u32[]{:S(2)}) collective-permute-start(f32[10,16,128]{2,1,0:T(8,128)S(1)} %get-tuple-element.58.refs_2_), channel_id=1, source_target_pairs={{0,12},{4,8},{8,4},{12,0},{1,13},{5,9},{9,5},{13,1},{2,14},{6,10},... | collective-permute-start | bytes 245768 | tf_op jit(solution)/shard_map/swap11/ppermute | solution.py:305
  30.8 4.8 %collective-permute-start.7 = (bf16[8,8,512]{2,1,0:T(8,128)(2,1)S(1)}, bf16[8,8,512]{2,1,0:T(8,128)(2,1)S(1)}, u32[]{:S(2)}, u32[]{:S(2)}) collective-permute-start(bf16[8,8,512]{2,1,0:T(8,128)(2,1)S(1)} %get-tuple-element.62), channel_id=1, source_target_pairs={{0,16},{16,0},{1,17},{17,1},{2,18},{18,2},{3,19},{19,3},{4,20},{20... | collective-permute-start | bytes 196616 | tf_op jit(solution)/shard_map/ppermute | solution.py:313
  36.3 5.5 %collective-permute-start.8 = (f32[8,8,512]{2,1,0:T(8,128)S(1)}, f32[8,8,512]{2,1,0:T(8,128)S(1)}, u32[]{:S(2)}, u32[]{:S(2)}) collective-permute-start(f32[8,8,512]{2,1,0:T(8,128)S(1)} %blocks.3), channel_id=1, source_target_pairs={{0,16},{16,0},{1,17},{17,1},{2,18},{18,2},{3,19},{19,3},{4,20},{20... | collective-permute-start | bytes 393224 | tf_op jit(solution)/shard_map/ppermute | solution.py:313
  43.5 9.1 %collective-permute-start.12 = (f32[16,256]{1,0:T(8,128)S(1)}, f32[16,256]{1,0:T(8,128)S(1)}, u32[]{:S(2)}, u32[]{:S(2)}) collective-permute-start(f32[16,256]{1,0:T(8,128)S(1)} %get-tuple-element.70.refs_13_), channel_id=1, source_target_pairs={{0,1},{1,0},{2,3},{3,2},{4,5},{5,4},{6,7},{7,6},{8,9},{9,8},{10,11... | collective-permute-start | bytes 49160 | tf_op jit(solution)/shard_map/swap20/ppermute | solution.py:305
  44.2 8.4 %collective-permute-start.13 = (f32[16,256]{1,0:T(8,128)S(1)}, f32[16,256]{1,0:T(8,128)S(1)}, u32[]{:S(2)}, u32[]{:S(2)}) collective-permute-start(f32[16,256]{1,0:T(8,128)S(1)} %get-tuple-element.71.refs_14_), channel_id=1, source_target_pairs={{0,3},{1,2},{2,1},{3,0},{4,7},{5,6},{6,5},{7,4},{8,11},{9,10},{10,... | collective-permute-start | bytes 49160 | tf_op jit(solution)/shard_map/swap21/ppermute | solution.py:305
  46.2 6.4 %collective-permute-start.9 = (f32[9,16,128]{2,1,0:T(8,128)S(1)}, f32[9,16,128]{2,1,0:T(8,128)S(1)}, u32[]{:S(2)}, u32[]{:S(2)}) collective-permute-start(f32[9,16,128]{2,1,0:T(8,128)S(1)} %get-tuple-element.67.refs_10_), channel_id=1, source_target_pairs={{0,16},{16,0},{1,17},{17,1},{2,18},{18,2},{3,19},{19,3},{4,20},{20... | collective-permute-start | bytes 221192 | tf_op jit(solution)/shard_map/swap00/ppermute | solution.py:305
  46.3 6.3 %collective-permute-start.10 = (f32[9,16,128]{2,1,0:T(8,128)S(1)}, f32[9,16,128]{2,1,0:T(8,128)S(1)}, u32[]{:S(2)}, u32[]{:S(2)}) collective-permute-start(f32[9,16,128]{2,1,0:T(8,128)S(1)} %get-tuple-element.68.refs_11_), channel_id=1, source_target_pairs={{0,4},{4,0},{8,12},{12,8},{1,5},{5,1},{9,13},{13,9},{2,6},{6,2},{1... | collective-permute-start | bytes 221192 | tf_op jit(solution)/shard_map/swap10/ppermute | solution.py:305
  46.3 6.3 %collective-permute-start.11 = (f32[9,16,128]{2,1,0:T(8,128)S(1)}, f32[9,16,128]{2,1,0:T(8,128)S(1)}, u32[]{:S(2)}, u32[]{:S(2)}) collective-permute-start(f32[9,16,128]{2,1,0:T(8,128)S(1)} %get-tuple-element.69.refs_12_), channel_id=1, source_target_pairs={{0,12},{4,8},{8,4},{12,0},{1,13},{5,9},{9,5},{13,1},{2,14},{6,10},... | collective-permute-start | bytes 221192 | tf_op jit(solution)/shard_map/swap11/ppermute | solution.py:305

commit v3 on v2

--- a/solution.py
+++ b/solution.py
@@ -5,6 +5,7 @@
 from jax.experimental.pallas import tpu as pltpu
 from jax.sharding import PartitionSpec as P
 
+
 BE = 8
 AXES = ("span", "height", "depth")
 
@@ -24,9 +25,11 @@
 HB = pl.BlockSpec(memory_space=pltpu.HBM)
 
 
-def call(kernel, ins, outs, scratch=(), flops=0, aliases=None, name=None):
+def call(kernel, ins, outs, scratch=(), flops=0, aliases=None):
     arrays = [
-        pltpu.with_memory_space_constraint(array, pltpu.SMEM if spec is SM else pltpu.VMEM)
+        pltpu.with_memory_space_constraint(
+            array, pltpu.HBM if spec is HB else pltpu.SMEM if spec is SM else pltpu.VMEM
+        )
         for array, spec in ins
     ]
     return pl.pallas_call(
@@ -43,7 +46,6 @@
         input_output_aliases=aliases or {},
         cost_estimate=pl.CostEstimate(flops=flops, bytes_accessed=1 << 20, transcendentals=0),
         compiler_params=pltpu.CompilerParams(vmem_limit_bytes=12 << 20),
-        name=name,
     )(*arrays)
 
 
@@ -59,7 +61,6 @@
     tiles = X * T
     cells = BE**3
     lanes = Z
-    wide = -(-(loads + 2) // 8) * 8
     assert lanes == 128 and BE == 8 and loads == 8 and slots_fit(void.shape, phase.shape)
     sizes = [lax.axis_size(axis) for axis in AXES]
     assert all(size % 2 == 0 for size in sizes)
@@ -100,6 +101,17 @@
         high = value.astype(BF16).astype(F32)
         return high, value - high
 
+    def in_groups(count, one, group=4):
+        while count % group:
+            group //= 2
+
+        def several(i, carry):
+            for j in range(group):
+                one(i * group + j)
+            return carry
+
+        lax.fori_loop(0, count // group, several, 0)
+
     def gather_bricks(source, table, base, count, out):
         sub, lane = iotas()
         keep = ((lane >> 3) & 7) == sub
@@ -111,48 +123,39 @@
             0.0,
         ).astype(BF16)
 
-        def one(r, carry):
+        def one(r):
             n = table[base + r]
             bx, by, bz = brick_at(n)
-            inside = (lane >> 3) == bz
-
-            @pl.when(n >= 0)
-            def _():
-                rows = []
-                for q in range(4):
-                    for l in range(loads):
-                        pair = [
-                            jnp.where(inside, source[l, row(bx * 8 + 2 * q + h, by), :], 0.0)
-                            for h in range(2)
-                        ]
-                        rows.append(jnp.concatenate(pair, axis=1))
-                stacked = jnp.concatenate(rows, axis=0).astype(BF16)
-                folded = jnp.dot(stacked, fold, preferred_element_type=F32)
-                columns = []
-                for q in range(4):
-                    columns.append(
-                        jnp.concatenate(
-                            [
-                                jnp.where(
-                                    keep,
-                                    folded[(q * loads + l) * 8 : (q * loads + l + 1) * 8],
-                                    0.0,
-                                )
-                                for l in range(loads)
-                            ],
-                            axis=0,
-                        )
+            inside = (lane >> 3) == jnp.where(n >= 0, bz, -1)
+            rows = []
+            for q in range(4):
+                for l in range(loads):
+                    pair = [
+                        jnp.where(inside, source[l, row(bx * 8 + 2 * q + h, by), :], 0.0)
+                        for h in range(2)
+                    ]
+                    rows.append(jnp.concatenate(pair, axis=1))
+            stacked = jnp.concatenate(rows, axis=0).astype(BF16)
+            folded = jnp.dot(stacked, fold, preferred_element_type=F32)
+            columns = []
+            for q in range(4):
+                columns.append(
+                    jnp.concatenate(
+                        [
+                            jnp.where(
+                                keep,
+                                folded[(q * loads + l) * 8 : (q * loads + l + 1) * 8],
+                                0.0,
+                            )
+                            for l in range(loads)
+                        ],
+                        axis=0,
                     )
-                cells_of = jnp.concatenate(columns, axis=1).astype(BF16)
-                out[r] = jnp.dot(pick, cells_of, preferred_element_type=F32).astype(BF16)
-
-            @pl.when(n < 0)
-            def _():
-                out[r] = jnp.zeros((loads, cells), BF16)
-
-            return carry
-
-        lax.fori_loop(0, count, one, 0)
+                )
+            cells_of = jnp.concatenate(columns, axis=1).astype(BF16)
+            out[r] = jnp.dot(pick, cells_of, preferred_element_type=F32).astype(BF16)
+
+        in_groups(count, one)
 
     def scatter_bricks(field, table, base, count, images, split):
         sub, lane = iotas()
@@ -161,46 +164,41 @@
             2 * lanes, 2 * lanes, lambda r: (r >> 6) & 1, lambda c: c >> 7
         )
 
-        def one(r, carry):
+        def one(r):
             n = table[base + r]
             bx, by, bz = brick_at(n)
-            inside = (lane >> 3) == bz
-
-            @pl.when(n >= 0)
-            def _():
-                high, low = halves(images[r])
-                split[0] = high
-                split[1] = low
-                rows = []
-                for q in range(4):
-                    for l in range(loads):
-                        pair = [
-                            jnp.where(
-                                keep,
-                                jnp.broadcast_to(
-                                    split[part, pl.ds(l, 1), pl.ds(q * lanes, lanes)],
-                                    (8, lanes),
-                                ),
-                                0.0,
-                            )
-                            for part in range(2)
+            inside = (lane >> 3) == jnp.where(n >= 0, bz, -1)
+            high, low = halves(images[r])
+            split[r, 0] = high
+            split[r, 1] = low
+            rows = []
+            for q in range(4):
+                for l in range(loads):
+                    pair = [
+                        jnp.where(
+                            keep,
+                            jnp.broadcast_to(
+                                split[r, part, pl.ds(l, 1), pl.ds(q * lanes, lanes)],
+                                (8, lanes),
+                            ),
+                            0.0,
+                        )
+                        for part in range(2)
+                    ]
+                    rows.append(jnp.concatenate(pair, axis=1))
+            stacked = jnp.concatenate(rows, axis=0).astype(BF16)
+            spread = jnp.dot(stacked, unfold, preferred_element_type=F32)
+            for q in range(4):
+                for l in range(loads):
+                    for h in range(2):
+                        at = row(bx * 8 + 2 * q + h, by)
+                        tile = spread[
+                            (q * loads + l) * 8 : (q * loads + l + 1) * 8,
+                            h * lanes : (h + 1) * lanes,
                         ]
-                        rows.append(jnp.concatenate(pair, axis=1))
-                stacked = jnp.concatenate(rows, axis=0).astype(BF16)
-                spread = jnp.dot(stacked, unfold, preferred_element_type=F32)
-                for q in range(4):
-                    for l in range(loads):
-                        for h in range(2):
-                            at = row(bx * 8 + 2 * q + h, by)
-                            tile = spread[
-                                (q * loads + l) * 8 : (q * loads + l + 1) * 8,
-                                h * lanes : (h + 1) * lanes,
-                            ]
-                            field[l, at, :] = jnp.where(inside, tile, field[l, at, :])
-
-            return carry
-
-        lax.fori_loop(0, count, one, 0)
+                        field[l, at, :] = jnp.where(inside, tile, field[l, at, :])
+
+        in_groups(count, one)
 
     def face_position(coords_ref, d, b, extent):
         high = (coords_ref[d] + b) % 2 == 0
@@ -256,7 +254,7 @@
         return jnp.dot(turned, place, preferred_element_type=F32)
 
     def plain_neighbours(read, x, t):
-        sub, lane = iotas()
+        sub, _ = iotas()
         tile = read(x, t)
         x_low = read(jnp.maximum(x - 1, 0), t)
         x_high = read(jnp.minimum(x + 1, X - 1), t)
@@ -283,12 +281,13 @@
             lane < lanes - 1,
         )
 
-    def over_rows(body):
-        def one(x, carry):
-            body(x)
+    def over_rows(body, group=2):
+        def several(i, carry):
+            for j in range(group):
+                body(i * group + j)
             return carry
 
-        lax.fori_loop(0, X, one, 0)
+        lax.fori_loop(0, X // group, several, 0)
 
     def face_shape(d, count):
         return ((count, Y, Z), (count, X, Z), (-(-count // 8) * 8, X * Y))[d]
@@ -297,12 +296,11 @@
         return [(face_shape(d, count), F32, VM) for d, _ in faces]
 
     def exchange(payload):
-        received = []
+        received = [None] * len(faces)
         for (d, b), part in zip(faces, payload):
             n = sizes[d]
             swap = [(i, (i + 1 if (i + b) % 2 == 0 else i - 1) % n) for i in range(n)]
-            with jax.named_scope("swap" + str(d) + str(b)):
-                received.append(lax.ppermute(part, AXES[d], swap))
+            received[faces.index((d, b))] = lax.ppermute(part, AXES[d], swap)
         return received
 
     def to_owners(rows, sign):
@@ -328,6 +326,7 @@
         table_ref, far_ref, load_ref, phase_ref, blocks_ref, coords_ref, void_ref,
         owner_ref, arrived,
     ):
+        me = lax.axis_index("span")
         copies = [
             pltpu.make_async_copy(source, target, arrived.at[i])
             for i, (source, target) in enumerate(
@@ -336,7 +335,7 @@
                     (owner_hbm, owner_ref),
                     (load_hbm, load_ref),
                     (phase_hbm, phase_ref),
-                    (blocks_hbm, blocks_ref),
+                    (blocks_hbm.at[pl.ds(me * cap, cap)], blocks_ref),
                 )
             )
         ]
@@ -344,7 +343,6 @@
             copy.start()
         for d, axis in enumerate(AXES):
             coords_ref[d] = lax.axis_index(axis)
-        me = lax.axis_index("span")
         for i in range(slots + 1):
             table_ref[i] = -1
         copies[0].wait()
@@ -364,7 +362,7 @@
         copies[3].wait()
         copies[4].wait()
 
-    table, far, load_f, phase_f, precond, coords, void = pl.pallas_call(
+    table, far, load_f, phase_f, near_blocks, coords, void = pl.pallas_call(
         first_kernel,
         in_specs=[HB] * 5,
         out_specs=[SM, VM, VM, VM, VM, SM, SM],
@@ -373,7 +371,7 @@
             pltpu.VMEM((remote, loads, cells), BF16),
             pltpu.VMEM(field_shape, F32),
             pltpu.VMEM(plain_shape, F32),
-            pltpu.VMEM(precond.shape, BF16),
+            pltpu.VMEM((cap, cells, cells), BF16),
             pltpu.SMEM((3,), jnp.int32),
             pltpu.SMEM(void.shape, jnp.int32),
         ],
@@ -388,42 +386,58 @@
         for a in (void, owner, load_f, phase_f, precond)
     ])
 
-    def near_kernel(
-        table_ref, coords_ref, source_ref, blocks_ref, field_ref, rows_ref, image_ref, split
-    ):
-        field_ref[...] = jnp.zeros(field_ref.shape, F32)
-        gather_bricks(source_ref, table_ref, 0, cap, rows_ref)
-        for r in range(cap):
-            image_ref[r] = jnp.dot(
-                rows_ref[r], blocks_ref[coords_ref[0] * cap + r], preferred_element_type=F32
-            )
-        scatter_bricks(field_ref, table_ref, 0, cap, image_ref, split)
-
-    def near_part(source):
-        return call(
-            near_kernel,
-            [(table, SM), (coords, SM), (source, VM), (precond, VM)],
-            [(field_shape, F32, VM)],
-            scratch=[
-                pltpu.VMEM((cap, loads, cells), BF16),
-                pltpu.VMEM((cap, loads, cells), F32),
-                pltpu.VMEM((2, loads, cells), F32),
-            ],
-            flops=8000000000,
-            name="near",
-        )[0]
-
-    def blocks_kernel(coords_ref, rows_ref, blocks_ref, out_ref):
+    def near_kernel(bring):
+        def kernel(table_ref, coords_ref, source_ref, blocks_ref, *refs):
+            copies = []
+            if bring:
+                hbm, field_ref, far_ref, rows_ref, image_ref, split, arrived = refs
+                for shift in range(1, spans):
+                    source = (coords_ref[0] + spans - shift) % spans
+                    copies.append(
+                        pltpu.make_async_copy(
+                            hbm.at[pl.ds(source * cap, cap)],
+                            far_ref.at[pl.ds((shift - 1) * cap, cap)],
+                            arrived.at[shift - 1],
+                        )
+                    )
+                    copies[-1].start()
+            else:
+                field_ref, rows_ref, image_ref, split = refs
+            field_ref[...] = jnp.zeros(field_ref.shape, F32)
+            gather_bricks(source_ref, table_ref, 0, cap, rows_ref)
+            for r in range(cap):
+                image_ref[r] = jnp.dot(
+                    rows_ref[r], blocks_ref[r], preferred_element_type=F32
+                )
+            scatter_bricks(field_ref, table_ref, 0, cap, image_ref, split)
+            for copy in copies:
+                copy.wait()
+
+        return kernel
+
+    def near_part(source, bring):
+        ins = [(table, SM), (coords, SM), (source, VM), (near_blocks, VM)]
+        outs = [(field_shape, F32, VM)]
+        scratch = [
+            pltpu.VMEM((cap, loads, cells), BF16),
+            pltpu.VMEM((cap, loads, cells), F32),
+            pltpu.VMEM((cap, 2, loads, cells), F32),
+        ]
+        if bring:
+            ins.append((precond, HB))
+            outs.append(((remote, cells, cells), BF16, VM))
+            scratch.append(pltpu.SemaphoreType.DMA((spans - 1,)))
+        return call(near_kernel(bring), ins, outs, scratch=scratch, flops=8000000000)
+
+    def blocks_kernel(rows_ref, blocks_ref, out_ref):
         for r in range(remote):
-            slot = (coords_ref[0] + spans - (r // cap + 1)) % spans * cap + r % cap
-            out_ref[r] = jnp.dot(rows_ref[r], blocks_ref[slot], preferred_element_type=F32)
+            out_ref[r] = jnp.dot(rows_ref[r], blocks_ref[r], preferred_element_type=F32)
 
     def far_part(rows):
         (image,) = call(
             blocks_kernel,
-            [(coords, SM), (to_owners(rows, 1), VM), (precond, VM)],
+            [(to_owners(rows, 1), VM), (far_blocks, VM)],
             [((remote, loads, cells), F32, VM)],
-            name="blocks",
         )
         return to_owners(image, -1)
 
@@ -465,14 +479,13 @@
             [(table, SM), (coords, SM), (image, VM), (begun, VM)]
             + [(e, VM) for e in extras],
             [(field_shape, F32, VM)] + face_outs(loads + len(extras)),
-            scratch=[pltpu.VMEM((2, loads, cells), F32)],
+            scratch=[pltpu.VMEM((remote, 2, loads, cells), F32)],
             aliases={3: 0},
-            name="faces" + str(len(extras)),
         )
         return result[0], result[1:], exchange(result[1:])
 
     def stiffness_kernel(void_ref, phase_ref, ks_ref):
-        sub, lane = iotas()
+        _, lane = iotas()
         for bx in range(bricks_x):
             for by in range(bricks_y):
                 mask = jnp.zeros((8, lanes), F32)
@@ -485,11 +498,11 @@
                     stiffness = void_stiffness + (1.0 - void_stiffness) * (p * p * p)
                     ks_ref[at, :] = mask * stiffness
 
+    begun, far_blocks = near_part(load_f, True)
     far_image = far_part(far)
-    begun = near_part(load_f)
     (ks,) = call(
         stiffness_kernel, [(void, SM), (phase_f, VM)], [(plain_shape, F32, VM)],
-        flops=2000000000, name="stiffness",
+        flops=2000000000,
     )
     z_field, z_sent, z_halo = to_field(begun, far_image, [ks, phase_f])
 
@@ -544,7 +557,6 @@
             ((2, loads, 8, Z), F32, VM),
         ],
         flops=8000000000,
-        name="inner",
     )
 
     def face_weight(coords_ref, d, b, sent, received, at):
@@ -596,7 +608,7 @@
                 eight = sum(
                     product[:, i * lanes : (i + 1) * lanes] for i in range(X * Y // lanes)
                 )
-                sub, lane = iotas()
+                sub, _ = iotas()
                 for l in range(loads):
                     dots_ref[1, l] += jnp.where(sub == l, eight, 0.0)
         depth = [shift for (d, _), shift in zip(faces, moved) if d == 2]
@@ -621,11 +633,10 @@
         ],
         scratch=[pltpu.VMEM(face_shape(d, loads + 1), F32) for d, _ in faces],
         aliases={2: 0, 3: 1, 4: 2},
-        name="edges",
     )
 
     far_image = far_part(far)
-    w_field, w_sent, w_halo = to_field(near_part(q_field), far_image, [start])
+    w_field, w_sent, w_halo = to_field(near_part(q_field, False)[0], far_image, [start])
 
     products = 5
 
@@ -656,46 +667,9 @@
         [(w_field, VM), (q_field, VM), (load_f, VM), (weights, VM), (ks, VM)],
         [((3, loads, 8, Z), F32, VM)],
         flops=8000000000,
-        name="more",
     )
 
-    def energy_kernel(z_ref, w_ref, ks_ref, energy_ref):
-        def body(x):
-            for t in range(T):
-                at = row(x, t)
-                inside = valid(x, t)
-                ks_tile, ks_near = plain_neighbours(lambda x, t: ks_ref[row(x, t), :], x, t)
-                solid = [
-                    jnp.where(
-                        jnp.logical_and(inside[d], joined(ks_tile, ks_near[d]) > 0.0), 1.0, 0.0
-                    )
-                    for d in range(6)
-                ]
-                for l in range(loads):
-                    z, z_near = plain_neighbours(lambda x, t: z_ref[l, row(x, t), :], x, t)
-                    w, w_near = plain_neighbours(lambda x, t: w_ref[l, row(x, t), :], x, t)
-                    zz = zw = ww = jnp.zeros((8, lanes), F32)
-                    for d in range(6):
-                        gap_z = solid[d] * (z - z_near[d])
-                        gap_w = solid[d] * (w - w_near[d])
-                        zz = zz + gap_z * gap_z
-                        zw = zw + gap_z * gap_w
-                        ww = ww + gap_w * gap_w
-                    energy_ref[0, l, at, :] = zz
-                    energy_ref[1, l, at, :] = zw
-                    energy_ref[2, l, at, :] = ww
-
-        over_rows(body)
-
-    (energies,) = call(
-        energy_kernel,
-        [(z_field, VM), (w_field, VM), (ks, VM)],
-        [((3,) + field_shape, F32, VM)],
-        flops=16000000000,
-        name="energy",
-    )
-
-    def total_kernel(coords_ref, dots_ref, more_in, _, *refs):
+    def total_kernel(coords_ref, dots_ref, more_in, *refs):
         z_mine = refs[:face_count]
         z_other = refs[face_count : 2 * face_count]
         w_mine = refs[2 * face_count : 3 * face_count]
@@ -747,13 +721,12 @@
 
     partial, _, *kept = call(
         total_kernel,
-        [(coords, SM), (dots, VM), (more, VM), (energies, VM)]
+        [(coords, SM), (dots, VM), (more, VM)]
         + [(a, VM) for part in (z_sent, z_halo, w_sent, w_halo) for a in part],
         [((devices, lanes), F32, VM), ((3, loads, 8, Z), F32, VM)]
         + [((2,) + face_shape(d, loads), F32, VM) for d, _ in faces]
         + [((8, X * Y) if d == 2 else face_shape(d, 1)[1:], F32, VM) for d, _ in faces],
         aliases={2: 1},
-        name="total",
     )
     gaps, start_halo = kept[:face_count], kept[face_count:]
     sums = everyone(partial)
@@ -768,13 +741,11 @@
     message = face_rows + 1
 
     def solve_kernel(
-        coords_ref, sums_ref, energy_ref, phase_ref, z_ref, w_ref, *refs
+        coords_ref, sums_ref, ks_ref, phase_ref, z_ref, w_ref, *refs
     ):
         gap_refs = refs[:face_count]
-        (sens_ref, out_ref, x_hbm, sens_hbm, x_ref, plain_ref, held_ref, written) = refs[
-            face_count:
-        ]
-        sub, lane = iotas()
+        sens_ref, out_ref, x_hbm, x_ref, plain_ref, held_ref, written = refs[face_count:]
+        _, lane = iotas()
         total = jnp.broadcast_to(
             jnp.sum(sums_ref[...], axis=0, keepdims=True), (8, lanes)
         )
@@ -791,18 +762,11 @@
         for_w = -alpha_next * alpha
         c_z = [jnp.broadcast_to(for_z[0:1, l : l + 1], (8, lanes)) for l in range(loads)]
         c_w = [jnp.broadcast_to(for_w[0:1, l : l + 1], (8, lanes)) for l in range(loads)]
-        c_zz = [c * c for c in c_z]
-        c_zw = [2.0 * a * c for a, c in zip(c_z, c_w)]
-        c_ww = [c * c for c in c_w]
         writes = []
         for l in range(loads):
-
-            def mix(i, carry, l=l):
-                at = pl.ds(pl.multiple_of(i * 8, 8), 8)
+            for i in range(tiles):
+                at = pl.ds(i * 8, 8)
                 x_ref[l, at, :] = c_z[l] * z_ref[l, at, :] + c_w[l] * w_ref[l, at, :]
-                return carry
-
-            lax.fori_loop(0, tiles, mix, 0, unroll=8)
             writes.append(
                 pltpu.make_async_copy(x_ref.at[l], x_hbm.at[l], written.at[l])
             )
@@ -811,11 +775,20 @@
         def body(x):
             for t in range(T):
                 at = row(x, t)
+                inside = valid(x, t)
+                ks_tile, ks_near = plain_neighbours(lambda x, t: ks_ref[row(x, t), :], x, t)
+                gaps_of = [jnp.zeros((8, lanes), F32) for _ in range(6)]
+                for l in range(loads):
+                    tile, near_tiles = plain_neighbours(
+                        lambda x, t: x_ref[l, row(x, t), :], x, t
+                    )
+                    for d in range(6):
+                        gap = tile - near_tiles[d]
+                        gaps_of[d] = gaps_of[d] + gap * gap
                 energy = jnp.zeros((8, lanes), F32)
-                for l in range(loads):
-                    energy = energy + c_zz[l] * energy_ref[0, l, at, :]
-                    energy = energy + c_zw[l] * energy_ref[1, l, at, :]
-                    energy = energy + c_ww[l] * energy_ref[2, l, at, :]
+                for d in range(6):
+                    solid = jnp.logical_and(inside[d], joined(ks_tile, ks_near[d]) > 0.0)
+                    energy = energy + jnp.where(solid, gaps_of[d], 0.0)
                 plain_ref[at, :] = energy
 
         over_rows(body)
@@ -846,8 +819,6 @@
         p = phase_ref[...]
         negative = 1.5 * (1.0 - void_stiffness) * (p * p) * energy
         sens_ref[...] = -negative
-        writes.append(pltpu.make_async_copy(sens_ref, sens_hbm, written.at[loads]))
-        writes[-1].start()
         peak = jnp.max(jnp.max(negative, axis=0, keepdims=True), axis=1, keepdims=True)
         peak = jnp.broadcast_to(peak, (1, lanes))
         high, rest = halves(peak)
@@ -880,10 +851,10 @@
         for write in writes:
             write.wait()
 
-    sens_field, outgoing, displacement, sensitivity = call(
+    sens_field, outgoing, displacement = call(
         solve_kernel,
         [
-            (coords, SM), (sums, VM), (energies, VM), (phase_f, VM), (z_field, VM),
+            (coords, SM), (sums, VM), (ks, VM), (phase_f, VM), (z_field, VM),
             (w_field, VM),
         ]
         + [(a, VM) for a in gaps],
@@ -891,21 +862,21 @@
             (plain_shape, F32, VM),
             ((devices, message, lanes), BF16, VM),
             (field_shape, F32, HB),
-            (plain_shape, F32, HB),
         ],
         scratch=[
             pltpu.VMEM(field_shape, F32),
             pltpu.VMEM(plain_shape, F32),
             pltpu.VMEM((8, X * Y), F32),
-            pltpu.SemaphoreType.DMA((loads + 1,)),
+            pltpu.SemaphoreType.DMA((loads,)),
         ],
-        name="solve",
     )
     incoming = everyone(outgoing)
 
     def sweep_kernel(coords_ref, in_ref, sens_ref, start_ref, phase_ref, *refs):
         starts = refs[:face_count]
-        out_hbm, out_ref, once_ref, held_ref, written = refs[face_count:]
+        out_hbm, sens_hbm, out_ref, once_ref, held_ref, written = refs[face_count:]
+        writes = [pltpu.make_async_copy(sens_ref, sens_hbm, written.at[2])]
+        writes[0].start()
         sub, lane = iotas()
         tails = in_ref[:, pl.ds(face_rows, 1), :].astype(F32)
         tails = tails.reshape(devices, lanes)
@@ -916,6 +887,31 @@
         for i in range(tiles):
             at = pl.ds(i * 8, 8)
             once_ref[at, :] = start_ref[at, :] - inverse * (sens_ref[at, :] * scale)
+
+        held_ref[...] = jnp.zeros(held_ref.shape, F32)
+        factor = interface_weight * inverse
+        edges = []
+        for (d, b), start_b in zip(faces, starts):
+            is_open = face_open(coords_ref, d, b)
+            source = device_beyond(coords_ref, d, b)
+            sent = in_ref[source].astype(F32)
+            if d < 2:
+                value = start_b[...] - (inverse * scale1) * sent[: (Y if d == 0 else X)]
+                value = jnp.where(is_open, factor * value, 0.0)
+                if d == 0:
+                    x = face_position(coords_ref, d, b, X)
+                    at = pl.ds(pl.multiple_of(x * Y, 8), Y)
+                else:
+                    at = pl.ds(face_position(coords_ref, d, b, Y), X, stride=Y)
+                edges.append((at, value))
+            else:
+                for i in range(X * Y // lanes):
+                    at = pl.ds(i * lanes, lanes)
+                    value = start_b[pl.ds(0, 1), at] - (inverse * scale1) * sent[i : i + 1]
+                    held_ref[pl.ds(b, 1), at] = jnp.where(is_open, factor * value, 0.0)
+        out_ref[...] = spread_depth(turned_depth(held_ref[...]), coords_ref, (0, 1))
+        for at, value in edges:
+            out_ref[at, :] = out_ref[at, :] + value
 
         def body(x):
             for t in range(T):
@@ -931,48 +927,31 @@
                     - 0.5 * p * (1.0 - p) * (1.0 - 2.0 * p)
                     - sens_ref[at, :] * scale
                 )
-                out_ref[at, :] = (drive + interface_weight * around) * inverse
-
-        over_rows(body)
-        held_ref[...] = jnp.zeros(held_ref.shape, F32)
-        factor = interface_weight * inverse
-        for (d, b), start_b in zip(faces, starts):
-            is_open = face_open(coords_ref, d, b)
-            source = device_beyond(coords_ref, d, b)
-            sent = in_ref[source].astype(F32)
-            if d < 2:
-                value = start_b[...] - (inverse * scale1) * sent[: (Y if d == 0 else X)]
-                value = jnp.where(is_open, factor * value, 0.0)
-                if d == 0:
-                    x = face_position(coords_ref, d, b, X)
-                    at = pl.ds(pl.multiple_of(x * Y, 8), Y)
-                else:
-                    at = pl.ds(face_position(coords_ref, d, b, Y), X, stride=Y)
-                out_ref[at, :] = out_ref[at, :] + value
-            else:
-                for i in range(X * Y // lanes):
-                    at = pl.ds(i * lanes, lanes)
-                    value = start_b[pl.ds(0, 1), at] - (inverse * scale1) * sent[i : i + 1]
-                    held_ref[pl.ds(b, 1), at] = jnp.where(is_open, factor * value, 0.0)
-        out_ref[...] = out_ref[...] + spread_depth(
-            turned_depth(held_ref[...]), coords_ref, (0, 1)
-        )
-        write = pltpu.make_async_copy(out_ref, out_hbm, written)
-        write.start()
-        write.wait()
-
-    (phase_next,) = call(
+                out_ref[at, :] += (drive + interface_weight * around) * inverse
+
+        half = X // 2
+        for part in range(2):
+            for x in range(part * half, (part + 1) * half):
+                body(x)
+            at = pl.ds(part * half * Y, half * Y)
+            writes.append(
+                pltpu.make_async_copy(out_ref.at[at], out_hbm.at[at], written.at[part])
+            )
+            writes[-1].start()
+        for write in writes:
+            write.wait()
+
+    phase_next, sensitivity = call(
         sweep_kernel,
         [(coords, SM), (incoming, VM), (sens_field, VM), (start, VM), (phase_f, VM)]
         + [(a, VM) for a in start_halo],
-        [(plain_shape, F32, HB)],
+        [(plain_shape, F32, HB), (plain_shape, F32, HB)],
         scratch=[
             pltpu.VMEM(plain_shape, F32),
             pltpu.VMEM(plain_shape, F32),
             pltpu.VMEM((8, X * Y), F32),
-            pltpu.SemaphoreType.DMA,
+            pltpu.SemaphoreType.DMA((3,)),
         ],
-        name="sweeps",
     )
     return (
         displacement.reshape(load.shape),
@@ -982,6 +961,10 @@
 
 
 def solution(mesh):
+    return program(mesh)
+
+
+def program(mesh):
     return jax.shard_map(
         local,
         mesh=mesh,

time: 79.8 us -> 72.6 us (0.910)
  waiting for transfers between devices: 14 us -> 11.2 us
  Pallas kernels: 23.2 us -> 20.7 us
  starting transfers between devices: 19.2 us -> 16.8 us
    ppermute x4, waiting for transfers between devices: 13.1 us -> 8.67 us  [to_owners(): lax.ppermute(part, 'span', [(i, (i + sign * shift) % spans) for i in rang...]
    ppermute x10, starting transfers between devices: 13.1 us -> 10.9 us  [exchange(): received[faces.index((d, b))] = lax.ppermute(part, AXES[d], swap)]
    pallas_call x14 -> x13, Pallas kernels: 19.4 us -> 17.8 us  [call(): pl.pallas_call(kernel, in_specs=[spec for _, spec in ins], out_specs=[spe...]
    ppermute x10, waiting for transfers between devices: 1 us -> 2.49 us  [exchange(): received[faces.index((d, b))] = lax.ppermute(part, AXES[d], swap)]
    pallas_call x1, Pallas kernels: 3.81 us -> 2.88 us  [local(): pl.pallas_call(first_kernel, in_specs=[HB] * 5, out_specs=[SM, VM, VM, VM...]
  transfers between devices with their start and end apart: 14 -> 14, of which waited for: 5 -> 6; matrix products, arithmetic and copies ran while one was open for 0% -> 0% of each run, Pallas kernels for 10% -> 11%
where the time goes in v3:
time: 72.6 us; the launch traced here: 72.4 us
  blocking collectives  23 us (32%)
  Pallas kernels  20.7 us (29%)
  starting transfers between devices  16.8 us (23%)
  waiting for transfers between devices  11.2 us (15%)
  between operations  0.73 us (1%)
    all_to_all x2, blocking collectives, everyone(): lax.all_to_all(partial, AXES, split_axis=0, concat_axis=0, tiled=True)  23 us
    pallas_call x13, Pallas kernels, call(): pl.pallas_call(kernel, in_specs=[spec for _, spec in ins], out_specs=[spe...  17.8 us
    ppermute x10, starting transfers between devices, exchange(): received[faces.index((d, b))] = lax.ppermute(part, AXES[d], swap)  10.9 us
    ppermute x4, waiting for transfers between devices, to_owners(): lax.ppermute(part, 'span', [(i, (i + sign * shift) % spans) for i in rang...  8.67 us
    ppermute x4, starting transfers between devices, to_owners(): lax.ppermute(part, 'span', [(i, (i + sign * shift) % spans) for i in rang...  5.91 us
    pallas_call x1, Pallas kernels, local(): pl.pallas_call(first_kernel, in_specs=[HB] * 5, out_specs=[SM, VM, VM, VM...  2.88 us
    ppermute x10, waiting for transfers between devices, exchange(): received[faces.index((d, b))] = lax.ppermute(part, AXES[d], swap)  2.49 us
  transfers between devices with their start and end apart: 14, of which 6 were waited for; matrix products, arithmetic and copies ran while one was open for 0% of the time, Pallas kernels for 11%

profile of v3, /device:TPU:0, one launch (start us, length us, event | category | flops | bytes accessed | tf_op | source)
XLA Modules:
  0.0 72.4 jit_solution(10101378161161727254)
XLA Ops:
  0.6 2.9 %first.1 = (s32[17]{0:T(128)S(4)}, bf16[8,8,512]{2,1,0:T(8,128)(2,1)S(1)}, f32[8,256,128]{2,1,0:T(8,128)S(1)}, f32[256,128]{1,0:T(8,128)S(1)}, bf16[8,512,512]{2...) custom-call(s32[2,2,16]{2,1,0:T(2,128)} %void_hbm.1, s32[2,2,16]{2,1,0:T(2,128)} %owner_hbm.1, ...), custom_call_target="tpu_custom_call" | custom-call | tf_op jit(solution)/shard_map/first/pallas_call | solution.py:365
  3.5 3.1 %collective-permute-start = (bf16[8,8,512]{2,1,0:T(8,128)(2,1)S(1)}, bf16[8,8,512]{2,1,0:T(8,128)(2,1)S(1)}, u32[]{:S(2)}, u32[]{:S(2)}) collective-permute-start(bf16[8,8,512]{2,1,0:T(8,128)(2,1)S(1)} %get-tuple-element.50), channel_id=1, source_target_pairs={{0,16},{16,0},{1,17},{17,1},{2,18},{18,2},{3,19},{19,3},{4,20},{20... | collective-permute-start | bytes 196616 | tf_op jit(solution)/shard_map/ppermute | solution.py:311
  6.6 3.0 %shard_map.76 = (f32[8,256,128]{2,1,0:T(8,128)S(1)}, bf16[8,512,512]{2,1,0:T(8,128)(2,1)S(1)}) custom-call(s32[17]{0:T(128)S(4)} %get-tuple-element.49.table_ref, s32[3]{0:T(128)S(4)} %get-tuple-element.48.coords_ref, f32[8,256,128]{2,1,0:T(8,128)S(1)} %get-tuple-element.51.source_ref.load_ref, bf16[8,512,512]{2,1,0:T(8,128)(2,1)S(1)} %get-tuple-element.52.blocks_ref, ...), custom_call_target="tpu_custom_call" | custom-call | flops 8000000000 | bytes 1048576 | tf_op jit(solution)/shard_map/pallas_call | solution.py:35
  9.6 0.0 collective-permute-done.rows_ref
  9.6 0.6 shard_map.77
  10.2 1.3 %collective-permute-start.1 = (f32[8,8,512]{2,1,0:T(8,128)S(1)}, f32[8,8,512]{2,1,0:T(8,128)S(1)}, u32[]{:S(2)}, u32[]{:S(2)}) collective-permute-start(f32[8,8,512]{2,1,0:T(8,128)S(1)} %shard_map.77), channel_id=1, source_target_pairs={{0,16},{16,0},{1,17},{17,1},{2,18},{18,2},{3,19},{19,3},{4,20},{20... | collective-permute-start | bytes 393224 | tf_op jit(solution)/shard_map/ppermute | solution.py:311
  11.5 0.1 shard_map.78.refs_0_.ks_ref
  11.6 3.6 %collective-permute-done.1.image_ref = f32[8,8,512]{2,1,0:T(8,128)S(1)} collective-permute-done((f32[8,8,512]{2,1,0:T(8,128)S(1)}, f32[8,8,512]{2,1,0:T(8,128)S(1)}, u32[]{:S(2)}, u32[]{:S(2)}) %collective-permute-start.1) | collective-permute-done | bytes 131104 | tf_op jit(solution)/shard_map/ppermute | solution.py:311
  15.2 1.3 %shard_map.79 = (f32[8,256,128]{2,1,0:T(8,128)S(1)}, f32[10,16,128]{2,1,0:T(8,128)S(1)}, f32[10,16,128]{2,1,0:T(8,128)S(1)}, f32[10,16,128]{2,1,0:T(8,128)S(1)},...) custom-call(s32[17]{0:T(128)S(4)} %get-tuple-element.49.table_ref, ...), custom_call_target="tpu_custom_call", output_to_operand_aliasing={{0}: (3, {})} | custom-call | bytes 1048576 | tf_op jit(solution)/shard_map/pallas_call | solution.py:35
  16.6 1.6 %collective-permute-start.5 = (f32[16,256]{1,0:T(8,128)S(1)}, f32[16,256]{1,0:T(8,128)S(1)}, u32[]{:S(2)}, u32[]{:S(2)}) collective-permute-start(f32[16,256]{1,0:T(8,128)S(1)} %get-tuple-element.64.refs_3_), channel_id=1, source_target_pairs={{0,1},{1,0},{2,3},{3,2},{4,5},{5,4},{6,7},{7,6},{8,9},{9,8},{10,11... | collective-permute-start | bytes 49160 | tf_op jit(solution)/shard_map/ppermute | solution.py:303
  18.2 2.5 %collective-permute-start.6 = (f32[16,256]{1,0:T(8,128)S(1)}, f32[16,256]{1,0:T(8,128)S(1)}, u32[]{:S(2)}, u32[]{:S(2)}) collective-permute-start(f32[16,256]{1,0:T(8,128)S(1)} %get-tuple-element.65.refs_4_), channel_id=1, source_target_pairs={{0,3},{1,2},{2,1},{3,0},{4,7},{5,6},{6,5},{7,4},{8,11},{9,10},{10,... | collective-permute-start | bytes 49160 | tf_op jit(solution)/shard_map/ppermute | solution.py:303
  20.6 1.3 %collective-permute-start.2 = (f32[10,16,128]{2,1,0:T(8,128)S(1)}, f32[10,16,128]{2,1,0:T(8,128)S(1)}, u32[]{:S(2)}, u32[]{:S(2)}) collective-permute-start(f32[10,16,128]{2,1,0:T(8,128)S(1)} %get-tuple-element.61.refs_0_), channel_id=1, source_target_pairs={{0,16},{16,0},{1,17},{17,1},{2,18},{18,2},{3,19},{19,3},{4,20},{20... | collective-permute-start | bytes 245768 | tf_op jit(solution)/shard_map/ppermute | solution.py:303
  21.9 0.0 collective-permute-start.3
  21.9 1.6 %collective-permute-start.4 = (f32[10,16,128]{2,1,0:T(8,128)S(1)}, f32[10,16,128]{2,1,0:T(8,128)S(1)}, u32[]{:S(2)}, u32[]{:S(2)}) collective-permute-start(f32[10,16,128]{2,1,0:T(8,128)S(1)} %get-tuple-element.63.refs_2_), channel_id=1, source_target_pairs={{0,12},{4,8},{8,4},{12,0},{1,13},{5,9},{9,5},{13,1},{2,14},{6,10},... | collective-permute-start | bytes 245768 | tf_op jit(solution)/shard_map/ppermute | solution.py:303
  23.5 1.3 %shard_map.80 = (f32[8,256,128]{2,1,0:T(8,128)S(1)}, f32[6,256,128]{2,1,0:T(8,128)S(1)}, f32[256,128]{1,0:T(8,128)S(1)}, f32[2,8,8,128]{3,2,1,0:T(8,128)S(1)}) custom-call(f32[8,256,128]{2,1,0:T(8,128)S(1)} %get-tuple-element.57.z_ref, f32[8,256,128]{2,1,0:T(8,128)S(1)} %get-tuple-element.51.source_ref.load_ref, f32[256,128]{1,0:T(8,128)S(1)} %shard_map.78.refs_0_.ks_ref, ...), custom_call_target="tpu_custom_call" | custom-call | flops 8000000000 | bytes 1048576 | tf_op jit(solution)/shard_map/pallas_call | solution.py:35
  24.8 0.0 collective-permute-done.5.refs_8_
  24.8 0.0 collective-permute-done.6.refs_9_
  24.8 0.2 collective-permute-done.2.refs_5_
  25.1 0.0 collective-permute-done.3.refs_6_
  25.1 0.9 %collective-permute-done.4.refs_7_ = f32[10,16,128]{2,1,0:T(8,128)S(1)} collective-permute-done((f32[10,16,128]{2,1,0:T(8,128)S(1)}, f32[10,16,128]{2,1,0:T(8,128)S(1)}, u32[]{:S(2)}, u32[]{:S(2)}) %collective-permute-start.4) | collective-permute-done | bytes 81952 | tf_op jit(solution)/shard_map/ppermute | solution.py:303
  26.0 2.1 %shard_map.81 = (f32[8,256,128]{2,1,0:T(8,128)S(1)}, f32[256,128]{1,0:T(8,128)S(1)}, f32[2,8,8,128]{3,2,1,0:T(8,128)S(1)}, bf16[8,8,512]{2,1,0:T(8,128)(2,1)S(1)}) custom-call(s32[3]{0:T(128)S(4)} %get-tuple-element.48.coords_ref, s32[17]{0:T(128)S(4)} %get-tuple-element.49.table_ref, ...), custom_call_target="tpu_custom_call", output_to_operand_aliasing={{0}: (2, {}), {1}: (3, {}), {2}: (4, {})} | custom-call | bytes 1048576 | tf_op jit(solution)/shard_map/pallas_call | solution.py:35
  28.0 0.8 %collective-permute-start.7 = (bf16[8,8,512]{2,1,0:T(8,128)(2,1)S(1)}, bf16[8,8,512]{2,1,0:T(8,128)(2,1)S(1)}, u32[]{:S(2)}, u32[]{:S(2)}) collective-permute-start(bf16[8,8,512]{2,1,0:T(8,128)(2,1)S(1)} %get-tuple-element.67), channel_id=1, source_target_pairs={{0,16},{16,0},{1,17},{17,1},{2,18},{18,2},{3,19},{19,3},{4,20},{20... | collective-permute-start | bytes 196616 | tf_op jit(solution)/shard_map/ppermute | solution.py:311
  28.8 3.7 %collective-permute-done.7.rows_ref = bf16[8,8,512]{2,1,0:T(8,128)(2,1)S(1)} collective-permute-done((bf16[8,8,512]{2,1,0:T(8,128)(2,1)S(1)}, bf16[8,8,512]{2,1,0:T(8,128)(2,1)S(1)}, u32[]{:S(2)}, u32[]{:S(2)}) %collective-permute-start.7) | collective-permute-done | bytes 65568 | tf_op jit(solution)/shard_map/ppermute | solution.py:311
  32.6 0.6 shard_map.82
  33.2 0.8 %collective-permute-start.8 = (f32[8,8,512]{2,1,0:T(8,128)S(1)}, f32[8,8,512]{2,1,0:T(8,128)S(1)}, u32[]{:S(2)}, u32[]{:S(2)}) collective-permute-start(f32[8,8,512]{2,1,0:T(8,128)S(1)} %shard_map.82), channel_id=1, source_target_pairs={{0,16},{16,0},{1,17},{17,1},{2,18},{18,2},{3,19},{19,3},{4,20},{20... | collective-permute-start | bytes 393224 | tf_op jit(solution)/shard_map/ppermute | solution.py:311
  34.0 3.0 %shard_map.83.begun_ref = f32[8,256,128]{2,1,0:T(8,128)S(1)} custom-call(s32[17]{0:T(128)S(4)} %get-tuple-element.49.table_ref, s32[3]{0:T(128)S(4)} %get-tuple-element.48.coords_ref, f32[8,256,128]{2,1,0:T(8,128)S(1)} %get-tuple-element.68.source_ref.q_ref, bf16[8,512,512]{2,1,0:T(8,128)(2,1)S(1)} %get-tuple-element.52.blocks_ref), custom_call_target="tpu_custom_call" | custom-call | flops 8000000000 | bytes 1048576 | tf_op jit(solution)/shard_map/pallas_call | solution.py:35
  37.0 1.3 %collective-permute-done.8.image_ref = f32[8,8,512]{2,1,0:T(8,128)S(1)} collective-permute-done((f32[8,8,512]{2,1,0:T(8,128)S(1)}, f32[8,8,512]{2,1,0:T(8,128)S(1)}, u32[]{:S(2)}, u32[]{:S(2)}) %collective-permute-start.8) | collective-permute-done | bytes 131104 | tf_op jit(solution)/shard_map/ppermute | solution.py:311
  38.3 1.3 %shard_map.84 = (f32[8,256,128]{2,1,0:T(8,128)S(1)}, f32[9,16,128]{2,1,0:T(8,128)S(1)}, f32[9,16,128]{2,1,0:T(8,128)S(1)}, f32[9,16,128]{2,1,0:T(8,128)S(1)}, f3...) custom-call(s32[17]{0:T(128)S(4)} %get-tuple-element.49.table_ref, ...), custom_call_target="tpu_custom_call", output_to_operand_aliasing={{0}: (3, {})} | custom-call | bytes 1048576 | tf_op jit(solution)/shard_map/pallas_call | solution.py:35
  39.5 0.7 %collective-permute-start.12 = (f32[16,256]{1,0:T(8,128)S(1)}, f32[16,256]{1,0:T(8,128)S(1)}, u32[]{:S(2)}, u32[]{:S(2)}) collective-permute-start(f32[16,256]{1,0:T(8,128)S(1)} %get-tuple-element.75.refs_13_), channel_id=1, source_target_pairs={{0,1},{1,0},{2,3},{3,2},{4,5},{5,4},{6,7},{7,6},{8,9},{9,8},{10,11... | collective-permute-start | bytes 49160 | tf_op jit(solution)/shard_map/ppermute | solution.py:303
  40.3 0.9 %collective-permute-start.13 = (f32[16,256]{1,0:T(8,128)S(1)}, f32[16,256]{1,0:T(8,128)S(1)}, u32[]{:S(2)}, u32[]{:S(2)}) collective-permute-start(f32[16,256]{1,0:T(8,128)S(1)} %get-tuple-element.76.refs_14_), channel_id=1, source_target_pairs={{0,3},{1,2},{2,1},{3,0},{4,7},{5,6},{6,5},{7,4},{8,11},{9,10},{10,... | collective-permute-start | bytes 49160 | tf_op jit(solution)/shard_map/ppermute | solution.py:303
  41.2 0.8 %collective-permute-start.9 = (f32[9,16,128]{2,1,0:T(8,128)S(1)}, f32[9,16,128]{2,1,0:T(8,128)S(1)}, u32[]{:S(2)}, u32[]{:S(2)}) collective-permute-start(f32[9,16,128]{2,1,0:T(8,128)S(1)} %get-tuple-element.72.refs_10_), channel_id=1, source_target_pairs={{0,16},{16,0},{1,17},{17,1},{2,18},{18,2},{3,19},{19,3},{4,20},{20... | collective-permute-start | bytes 221192 | tf_op jit(solution)/shard_map/ppermute | solution.py:303
  41.9 0.0 collective-permute-start.10
  42.0 1.6 %collective-permute-start.11 = (f32[9,16,128]{2,1,0:T(8,128)S(1)}, f32[9,16,128]{2,1,0:T(8,128)S(1)}, u32[]{:S(2)}, u32[]{:S(2)}) collective-permute-start(f32[9,16,128]{2,1,0:T(8,128)S(1)} %get-tuple-element.74.refs_12_), channel_id=1, source_target_pairs={{0,12},{4,8},{8,4},{12,0},{1,13},{5,9},{9,5},{13,1},{2,14},{6,10},... | collective-permute-start | bytes 221192 | tf_op jit(solution)/shard_map/ppermute | solution.py:303
  43.5 0.9 %shard_map.85.more_in = f32[3,8,8,128]{3,2,1,0:T(8,128)S(1)} custom-call(f32[8,256,128]{2,1,0:T(8,128)S(1)} %get-tuple-element.70.w_ref, f32[8,256,128]{2,1,0:T(8,128)S(1)} %get-tuple-element.68.source_ref.q_ref, f32[8,256,128]{2,1,0:T(8,128)S(1)} %get-tuple-element.51.source_ref.load_ref, f32[6,256,128]{2,1,0:T(8,128)S(1)} %get-tuple-element.71.weight_ref, ...), custom_call_target="tpu_custom_call" | custom-call | flops 8000000000 | bytes 1048576 | tf_op jit(solution)/shard_map/pallas_call | solution.py:35
  44.5 0.0 collective-permute-done.12.refs_18_
  44.5 1.4 %collective-permute-done.13.refs_19_ = f32[16,256]{1,0:T(8,128)S(1)} collective-permute-done((f32[16,256]{1,0:T(8,128)S(1)}, f32[16,256]{1,0:T(8,128)S(1)}, u32[]{:S(2)}, u32[]{:S(2)}) %collective-permute-start.13) | collective-permute-done | bytes 16416 | tf_op jit(solution)/shard_map/ppermute | solution.py:303
  45.8 0.0 collective-permute-done.9.refs_15_
  45.8 0.0 collective-permute-done.10.refs_16_
  45.8 0.0 collective-permute-done.11.refs_17_
  45.8 0.2 shard_map.86
  46.0 12.0 %all_to_all.16 = f32[32,1,128]{2,1,0:T(1,128)S(1)} all-to-all(f32[32,1,128]{2,1,0:T(1,128)S(1)} %bitcast.10), channel_id=1, replica_groups=mesh['span'=2,'height'=4,'depth'=4] {'span','height','depth'}, dimensions={0} | all-to-all | bytes 32768 | tf_op jit(solution)/shard_map/all_to_all | solution.py:318
  58.0 2.2 %shard_map.87 = (f32[256,128]{1,0:T(8,128)S(1)}, bf16[32,17,128]{2,1,0:T(8,128)(2,1)S(1)}, f32[8,256,128]{2,1,0:T(8,128)}) custom-call(s32[3]{0:T(128)S(4)} %get-tuple-element.48.coords_ref, f32[32,128]{1,0:T(8,128)S(1)} %bitcast.9, f32[256,128]{1,0:T(8,128)S(1)} %shard_map.78.refs_0_.ks_ref, f32[256,128]{1,0:T(8,128)S(1)} %get-tuple-element.56.phase_ref.refs_1_, ...), custom_call_target="tpu_custom_call" | custom-call | bytes 1048576 | tf_op jit(solution)/shard_map/pallas_call | solution.py:35
  60.3 11.0 %all_to_all.17.in_ref = bf16[32,17,128]{2,1,0:T(8,128)(2,1)S(1)} all-to-all(bf16[32,17,128]{2,1,0:T(8,128)(2,1)S(1)} %get-tuple-element.84), channel_id=1, replica_groups=mesh['span'=2,'height'=4,'depth'=4] {'span','height','depth'}, dimensions={0} | all-to-all | bytes 278528 | tf_op jit(solution)/shard_map/all_to_all | solution.py:318
  71.3 1.1 %shard_map.88 = (f32[256,128]{1,0:T(8,128)}, f32[256,128]{1,0:T(8,128)}) custom-call(s32[3]{0:T(128)S(4)} %get-tuple-element.48.coords_ref, bf16[32,17,128]{2,1,0:T(8,128)(2,1)S(1)} %all_to_all.17.in_ref, f32[256,128]{1,0:T(8,128)S(1)} %get-tuple-element.85.sens_ref, f32[256,128]{1,0:T(8,128)S(1)} %get-tuple-element.69.refs_0_.start_ref, ...), custom_call_target="tpu_custom_call" | custom-call | bytes 1048576 | tf_op jit(solution)/shard_map/pallas_call | solution.py:35
Async XLA Ops:
  3.5 6.1 %collective-permute-start = (bf16[8,8,512]{2,1,0:T(8,128)(2,1)S(1)}, bf16[8,8,512]{2,1,0:T(8,128)(2,1)S(1)}, u32[]{:S(2)}, u32[]{:S(2)}) collective-permute-start(bf16[8,8,512]{2,1,0:T(8,128)(2,1)S(1)} %get-tuple-element.50), channel_id=1, source_target_pairs={{0,16},{16,0},{1,17},{17,1},{2,18},{18,2},{3,19},{19,3},{4,20},{20... | collective-permute-start | bytes 196616 | tf_op jit(solution)/shard_map/ppermute | solution.py:311
  10.2 5.0 %collective-permute-start.1 = (f32[8,8,512]{2,1,0:T(8,128)S(1)}, f32[8,8,512]{2,1,0:T(8,128)S(1)}, u32[]{:S(2)}, u32[]{:S(2)}) collective-permute-start(f32[8,8,512]{2,1,0:T(8,128)S(1)} %shard_map.77), channel_id=1, source_target_pairs={{0,16},{16,0},{1,17},{17,1},{2,18},{18,2},{3,19},{19,3},{4,20},{20... | collective-permute-start | bytes 393224 | tf_op jit(solution)/shard_map/ppermute | solution.py:311
  16.6 8.3 %collective-permute-start.5 = (f32[16,256]{1,0:T(8,128)S(1)}, f32[16,256]{1,0:T(8,128)S(1)}, u32[]{:S(2)}, u32[]{:S(2)}) collective-permute-start(f32[16,256]{1,0:T(8,128)S(1)} %get-tuple-element.64.refs_3_), channel_id=1, source_target_pairs={{0,1},{1,0},{2,3},{3,2},{4,5},{5,4},{6,7},{7,6},{8,9},{9,8},{10,11... | collective-permute-start | bytes 49160 | tf_op jit(solution)/shard_map/ppermute | solution.py:303
  18.2 6.7 %collective-permute-start.6 = (f32[16,256]{1,0:T(8,128)S(1)}, f32[16,256]{1,0:T(8,128)S(1)}, u32[]{:S(2)}, u32[]{:S(2)}) collective-permute-start(f32[16,256]{1,0:T(8,128)S(1)} %get-tuple-element.65.refs_4_), channel_id=1, source_target_pairs={{0,3},{1,2},{2,1},{3,0},{4,7},{5,6},{6,5},{7,4},{8,11},{9,10},{10,... | collective-permute-start | bytes 49160 | tf_op jit(solution)/shard_map/ppermute | solution.py:303
  20.6 4.4 %collective-permute-start.2 = (f32[10,16,128]{2,1,0:T(8,128)S(1)}, f32[10,16,128]{2,1,0:T(8,128)S(1)}, u32[]{:S(2)}, u32[]{:S(2)}) collective-permute-start(f32[10,16,128]{2,1,0:T(8,128)S(1)} %get-tuple-element.61.refs_0_), channel_id=1, source_target_pairs={{0,16},{16,0},{1,17},{17,1},{2,18},{18,2},{3,19},{19,3},{4,20},{20... | collective-permute-start | bytes 245768 | tf_op jit(solution)/shard_map/ppermute | solution.py:303
  21.9 3.2 %collective-permute-start.3 = (f32[10,16,128]{2,1,0:T(8,128)S(1)}, f32[10,16,128]{2,1,0:T(8,128)S(1)}, u32[]{:S(2)}, u32[]{:S(2)}) collective-permute-start(f32[10,16,128]{2,1,0:T(8,128)S(1)} %get-tuple-element.62.refs_1_), channel_id=1, source_target_pairs={{0,4},{4,0},{8,12},{12,8},{1,5},{5,1},{9,13},{13,9},{2,6},{6,2},{1... | collective-permute-start | bytes 245768 | tf_op jit(solution)/shard_map/ppermute | solution.py:303
  21.9 4.1 %collective-permute-start.4 = (f32[10,16,128]{2,1,0:T(8,128)S(1)}, f32[10,16,128]{2,1,0:T(8,128)S(1)}, u32[]{:S(2)}, u32[]{:S(2)}) collective-permute-start(f32[10,16,128]{2,1,0:T(8,128)S(1)} %get-tuple-element.63.refs_2_), channel_id=1, source_target_pairs={{0,12},{4,8},{8,4},{12,0},{1,13},{5,9},{9,5},{13,1},{2,14},{6,10},... | collective-permute-start | bytes 245768 | tf_op jit(solution)/shard_map/ppermute | solution.py:303
  28.0 4.5 %collective-permute-start.7 = (bf16[8,8,512]{2,1,0:T(8,128)(2,1)S(1)}, bf16[8,8,512]{2,1,0:T(8,128)(2,1)S(1)}, u32[]{:S(2)}, u32[]{:S(2)}) collective-permute-start(bf16[8,8,512]{2,1,0:T(8,128)(2,1)S(1)} %get-tuple-element.67), channel_id=1, source_target_pairs={{0,16},{16,0},{1,17},{17,1},{2,18},{18,2},{3,19},{19,3},{4,20},{20... | collective-permute-start | bytes 196616 | tf_op jit(solution)/shard_map/ppermute | solution.py:311
  33.2 5.1 %collective-permute-start.8 = (f32[8,8,512]{2,1,0:T(8,128)S(1)}, f32[8,8,512]{2,1,0:T(8,128)S(1)}, u32[]{:S(2)}, u32[]{:S(2)}) collective-permute-start(f32[8,8,512]{2,1,0:T(8,128)S(1)} %shard_map.82), channel_id=1, source_target_pairs={{0,16},{16,0},{1,17},{17,1},{2,18},{18,2},{3,19},{19,3},{4,20},{20... | collective-permute-start | bytes 393224 | tf_op jit(solution)/shard_map/ppermute | solution.py:311
  39.5 4.9 %collective-permute-start.12 = (f32[16,256]{1,0:T(8,128)S(1)}, f32[16,256]{1,0:T(8,128)S(1)}, u32[]{:S(2)}, u32[]{:S(2)}) collective-permute-start(f32[16,256]{1,0:T(8,128)S(1)} %get-tuple-element.75.refs_13_), channel_id=1, source_target_pairs={{0,1},{1,0},{2,3},{3,2},{4,5},{5,4},{6,7},{7,6},{8,9},{9,8},{10,11... | collective-permute-start | bytes 49160 | tf_op jit(solution)/shard_map/ppermute | solution.py:303
  40.3 5.5 %collective-permute-start.13 = (f32[16,256]{1,0:T(8,128)S(1)}, f32[16,256]{1,0:T(8,128)S(1)}, u32[]{:S(2)}, u32[]{:S(2)}) collective-permute-start(f32[16,256]{1,0:T(8,128)S(1)} %get-tuple-element.76.refs_14_), channel_id=1, source_target_pairs={{0,3},{1,2},{2,1},{3,0},{4,7},{5,6},{6,5},{7,4},{8,11},{9,10},{10,... | collective-permute-start | bytes 49160 | tf_op jit(solution)/shard_map/ppermute | solution.py:303
  41.2 4.6 %collective-permute-start.9 = (f32[9,16,128]{2,1,0:T(8,128)S(1)}, f32[9,16,128]{2,1,0:T(8,128)S(1)}, u32[]{:S(2)}, u32[]{:S(2)}) collective-permute-start(f32[9,16,128]{2,1,0:T(8,128)S(1)} %get-tuple-element.72.refs_10_), channel_id=1, source_target_pairs={{0,16},{16,0},{1,17},{17,1},{2,18},{18,2},{3,19},{19,3},{4,20},{20... | collective-permute-start | bytes 221192 | tf_op jit(solution)/shard_map/ppermute | solution.py:303
  41.9 3.9 %collective-permute-start.10 = (f32[9,16,128]{2,1,0:T(8,128)S(1)}, f32[9,16,128]{2,1,0:T(8,128)S(1)}, u32[]{:S(2)}, u32[]{:S(2)}) collective-permute-start(f32[9,16,128]{2,1,0:T(8,128)S(1)} %get-tuple-element.73.refs_11_), channel_id=1, source_target_pairs={{0,4},{4,0},{8,12},{12,8},{1,5},{5,1},{9,13},{13,9},{2,6},{6,2},{1... | collective-permute-start | bytes 221192 | tf_op jit(solution)/shard_map/ppermute | solution.py:303
  42.0 3.9 %collective-permute-start.11 = (f32[9,16,128]{2,1,0:T(8,128)S(1)}, f32[9,16,128]{2,1,0:T(8,128)S(1)}, u32[]{:S(2)}, u32[]{:S(2)}) collective-permute-start(f32[9,16,128]{2,1,0:T(8,128)S(1)} %get-tuple-element.74.refs_12_), channel_id=1, source_target_pairs={{0,12},{4,8},{8,4},{12,0},{1,13},{5,9},{9,5},{13,1},{2,14},{6,10},... | collective-permute-start | bytes 221192 | tf_op jit(solution)/shard_map/ppermute | solution.py:303
